TPU v7x, 8 devices: a whole 2x2x1 slice. The times are simulated.
8 devices in a mesh: dp: 1 (over z), ep: 8 (over y, x, core).
Axes of the slice: x: 2, y: 2, z: 1, core: 2. Of those that a mesh axis runs over, the one named last changes fastest.
Arguments:
- tokens: bfloat16 [512, 4096], P(('dp', 'ep'))
- slot_ids: int32 [512, 4, 32], P(('dp', 'ep'))
- request_rows: int32 [8, 8, 128], P(('dp', 'ep'))
- gate_vals: float32 [512, 4, 32], P(('dp', 'ep'))
- grad_out: bfloat16 [512, 4096], P(('dp', 'ep'))
- table_up: bfloat16 [16384, 4096], P('ep')
- table_down: bfloat16 [16384, 4096], P('ep')
Outputs:
- output 1: bfloat16 [512, 4096], P(('dp', 'ep'))
- output 2: bfloat16 [512, 4096], P(('dp', 'ep'))
- output 3: bfloat16 [16384, 4096], P(('dp', 'ep'))
- output 4: bfloat16 [16384, 4096], P(('dp', 'ep'))
All inputs are finite; a program needn't handle non-finite values.
Results may differ from a plain program's by a relative error of at most 0.0087426.
Values are sent between devices in bfloat16 or wider.
A program may use at most 1 GiB of HBM per device.

v0:
```python
import math
import jax
import jax.numpy as jnp
from jax import lax
from jax.sharding import PartitionSpec as P


def gelu_pair(pre_act):
    normal_cdf = 0.5 * (1.0 + lax.erf(pre_act * (2.0 ** -0.5)))
    normal_pdf = jnp.exp(-0.5 * pre_act * pre_act) * ((2.0 * math.pi) ** -0.5)
    return pre_act * normal_cdf, normal_cdf + pre_act * normal_pdf


def local_layer(tokens, slot_flat, gate_flat, grad_out, up_table, down_table):
    tok_dev, width = tokens.shape
    sel_tok = slot_flat.shape[1]
    n_slots = up_table.shape[0]
    cap_tokens = max(1, 2 ** 23 // (sel_tok * width))
    block_tok = math.gcd(tok_dev, 2 ** int(math.log2(cap_tokens)))
    n_blocks = tok_dev // block_tok

    def scan_step(acc_pair, block_in):
        acc_up, acc_down = acc_pair
        x_blk, slot_blk, gate_blk, dy_blk = block_in
        up_rows = up_table[slot_blk]
        down_rows = down_table[slot_blk]
        pre_act = jnp.einsum('bsd,bd->bs', up_rows, x_blk, preferred_element_type=jnp.float32)
        act_val, slope_val = gelu_pair(pre_act)
        w_out = (gate_blk * act_val).astype(jnp.bfloat16)
        y_blk = jnp.einsum('bs,bsd->bd', w_out, down_rows, preferred_element_type=jnp.float32).astype(jnp.bfloat16)
        back_dot = jnp.einsum('bsd,bd->bs', down_rows, dy_blk, preferred_element_type=jnp.float32)
        coef_bf = (gate_blk * slope_val * back_dot).astype(jnp.bfloat16)
        dx_blk = jnp.einsum('bs,bsd->bd', coef_bf, up_rows, preferred_element_type=jnp.float32).astype(jnp.bfloat16)
        flat_slots = slot_blk.reshape(-1)
        up_part = coef_bf.astype(jnp.float32)[:, :, None] * x_blk[:, None, :]
        down_part = w_out.astype(jnp.float32)[:, :, None] * dy_blk[:, None, :]
        acc_up = acc_up.at[flat_slots].add(up_part.reshape(-1, width))
        acc_down = acc_down.at[flat_slots].add(down_part.reshape(-1, width))
        return (acc_up, acc_down), (y_blk, dx_blk)

    zero_acc = jnp.zeros((n_slots, width), jnp.float32)
    blocks_in = (tokens.reshape(n_blocks, block_tok, width), slot_flat.reshape(n_blocks, block_tok, sel_tok), gate_flat.reshape(n_blocks, block_tok, sel_tok), grad_out.reshape(n_blocks, block_tok, width))
    (acc_up, acc_down), (y_all, dx_all) = lax.scan(scan_step, (zero_acc, zero_acc), blocks_in)
    return acc_up, acc_down, y_all.reshape(tok_dev, width), dx_all.reshape(tok_dev, width)


def solution(mesh):
    n_group = mesh.shape['ep']
    tok_spec = P(('dp', 'ep'))
    table_spec = P('ep')

    def per_device(tokens, slot_ids, request_rows, gate_vals, grad_out, up_local, down_local):
        tok_dev, width = tokens.shape
        rows_owner = up_local.shape[0]
        n_req = request_rows.shape[2]
        sel_tok = slot_ids.shape[1] * slot_ids.shape[2]
        asked_rows = lax.all_to_all(request_rows[0], 'ep', 0, 0, tiled=True)
        up_pulled = lax.all_to_all(up_local[asked_rows], 'ep', 0, 0, tiled=True).reshape(n_group * n_req, width)
        down_pulled = lax.all_to_all(down_local[asked_rows], 'ep', 0, 0, tiled=True).reshape(n_group * n_req, width)
        acc_up, acc_down, y_local, dx_local = local_layer(tokens, slot_ids.reshape(tok_dev, sel_tok), gate_vals.reshape(tok_dev, sel_tok), grad_out, up_pulled, down_pulled)
        back_up = lax.all_to_all(acc_up.astype(jnp.bfloat16).reshape(n_group, n_req, width), 'ep', 0, 0, tiled=True)
        back_down = lax.all_to_all(acc_down.astype(jnp.bfloat16).reshape(n_group, n_req, width), 'ep', 0, 0, tiled=True)
        flat_asked = asked_rows.reshape(-1)
        grad_up = jax.ops.segment_sum(back_up.reshape(-1, width).astype(jnp.float32), flat_asked, num_segments=rows_owner)
        grad_down = jax.ops.segment_sum(back_down.reshape(-1, width).astype(jnp.float32), flat_asked, num_segments=rows_owner)
        return y_local, dx_local, grad_up.astype(jnp.bfloat16), grad_down.astype(jnp.bfloat16)

    return jax.shard_map(per_device, mesh=mesh, in_specs=(tok_spec, tok_spec, tok_spec, tok_spec, tok_spec, table_spec, table_spec), out_specs=(tok_spec, tok_spec, tok_spec, tok_spec), check_vma=False)
```

profile of v0, /device:TPU:0, one launch (start us, length us, event | category | flops | bytes accessed | tf_op | source)
XLA Modules:
  0.0 1489.5 jit_solution(2685759455095425351)
XLA Ops:
  0.6 8.8 all_to_all.32
  10.1 23.0 %gather_fusion.3 = bf16[1024,4096]{1,0:T(8,128)(2,1)} fusion(bf16[2048,4096]{1,0:T(8,128)(2,1)} %param.15, s32[1024]{0:T(1024)S(1)} %fusion.29), kind=kCustom, calls=%fused_computation.3 | custom fusion | bytes 16781312 | tf_op jit(solution)/shard_map/gather | solution.py:59
  36.8 23.0 %gather_fusion.2 = bf16[1024,4096]{1,0:T(8,128)(2,1)} fusion(bf16[2048,4096]{1,0:T(8,128)(2,1)} %param.14, s32[1024]{0:T(1024)S(1)} %fusion.29), kind=kCustom, calls=%fused_computation.2 | custom fusion | bytes 16781312 | tf_op jit(solution)/shard_map/gather | solution.py:58
  59.8 71.0 %all-to-all-done.2 = bf16[8,128,4096]{2,1,0:T(8,128)(2,1)} async-done(((bf16[8,128,4096]{2,1,0:T(8,128)(2,1)}), bf16[8,128,4096]{2,1,0:T(8,128)(2,1)}, u32[]{:S(2)}, u32[]{:S(2)}) %all-to-all-start.2) | async-done | bytes 8388640 | tf_op jit(solution)/shard_map/all_to_all | solution.py:59
  135.0 93.5 %all-to-all-done.1 = bf16[8,128,4096]{2,1,0:T(8,128)(2,1)} async-done(((bf16[8,128,4096]{2,1,0:T(8,128)(2,1)}), bf16[8,128,4096]{2,1,0:T(8,128)(2,1)}, u32[]{:S(2)}, u32[]{:S(2)}) %all-to-all-start.1) | async-done | bytes 8388640 | tf_op jit(solution)/shard_map/all_to_all | solution.py:58
  228.4 8.3 broadcast_in_dim.8.clone
  236.7 8.3 broadcast_in_dim.8
  245.0 984.7 %while.16 = (s32[]{:T(128)}, f32[1024,4096]{1,0:T(8,128)}, f32[1024,4096]{1,0:T(8,128)}, bf16[4,16,4096]{2,1,0:T(8,128)(2,1)}, bf16[4,16,4096]{2,1,0:T(8,128)(2,...) while((s32[]{:T(128)}, f32[1024,4096]{1,0:T(8,128)}, ...), condition=%wide.region_3.4_spmd, body=%wide.region_0.3_spmd.sunk | while | flops 100841472 | bytes 456294784 | solution.py:43
  247.2 33.1 %gather_fusion.1 = bf16[2048,4096]{1,0:T(8,128)(2,1)} fusion(bf16[1024,4096]{1,0:T(8,128)(2,1)} %get-tuple-element.234, s32[2048]{0:T(1024)S(1)} %get-tuple-element.189), kind=kCustom, calls=%fused_computation.1.clone.1 | custom fusion | bytes 33562624 | tf_op jit(solution)/shard_map/while/body/eval_jaxpr/gather | solution.py:26
  280.3 8.0 fusion.60
  288.3 33.1 %gather_fusion = bf16[2048,4096]{1,0:T(8,128)(2,1)} fusion(bf16[1024,4096]{1,0:T(8,128)(2,1)} %get-tuple-element.232, s32[2048]{0:T(1024)S(1)} %get-tuple-element.189), kind=kCustom, calls=%fused_computation.clone.1 | custom fusion | bytes 33562624 | tf_op jit(solution)/shard_map/while/body/eval_jaxpr/gather | solution.py:25
  321.5 20.6 %fusion.59 = f32[16,1,128]{2,1,0:T(1,128)S(1)} fusion(bf16[16,128,4096]{2,1,0:T(8,128)(2,1)} %bitcast.130, bf16[16,4096,1]{1,0,2:T(8,128)(2,1)S(1)} %get-tuple-element.190), kind=kOutput, calls=%fused_computation.14.clone.1 | convolution fusion | flops 16777216 | bytes 16916480 | tf_op jit(solution)/shard_map/while/body/eval_jaxpr/bsd,bd->bs/dot_general | solution.py:27
  342.1 8.2 fusion.62
  353.6 22.0 %bitcast_multiply_fusion.4 = (f32[2048,4096]{1,0:T(8,128)}, f32[2048,4096]{1,0:T(8,128)}) fusion(f32[16,4096]{1,0:T(8,128)S(1)} %get-tuple-element.188, f32[2048]{0:T(1024)S(1)} %get-tuple-element.192, f32[16,4096]{1,0:T(8,128)S(1)} %get-tuple-element.193, f32[2048]{0:T(1024)S(1)} %get-tuple-element.194), kind=kLoop, calls=%fused_computation.8.clone.1 | loop fusion | flops 16777216 | bytes 67649536 | tf_op jit(solution)/shard_map/while/body/eval_jaxpr/mul | solution.py:36
  375.6 61.8 %scatter_fusion = f32[1024,4096]{1,0:T(8,128)} fusion(f32[1024,4096]{1,0:T(8,128)} %get-tuple-element.214, s32[2048]{0:T(1024)S(1)} %bitcast.136, f32[2048,4096]{1,0:T(8,128)} %get-tuple-element.195), kind=kCustom, calls=%fused_computation.4.clone.1 | custom fusion | flops 8388608 | bytes 100671488 | tf_op jit(solution)/shard_map/while/body/eval_jaxpr/scatter-add | solution.py:37
  437.4 62.2 %scatter_fusion.1 = f32[1024,4096]{1,0:T(8,128)} fusion(f32[1024,4096]{1,0:T(8,128)} %get-tuple-element.215, s32[2048]{0:T(1024)S(1)} %bitcast.137, f32[2048,4096]{1,0:T(8,128)} %get-tuple-element.196), kind=kCustom, calls=%fused_computation.5.clone.1 | custom fusion | flops 8388608 | bytes 100671488 | tf_op jit(solution)/shard_map/while/body/eval_jaxpr/scatter-add | solution.py:38
  501.7 33.1 %gather_fusion.1 = bf16[2048,4096]{1,0:T(8,128)(2,1)} fusion(bf16[1024,4096]{1,0:T(8,128)(2,1)} %get-tuple-element.234, s32[2048]{0:T(1024)S(1)} %get-tuple-element.189), kind=kCustom, calls=%fused_computation.1.clone.1 | custom fusion | bytes 33562624 | tf_op jit(solution)/shard_map/while/body/eval_jaxpr/gather | solution.py:26
  534.8 8.0 fusion.60
  542.8 33.1 %gather_fusion = bf16[2048,4096]{1,0:T(8,128)(2,1)} fusion(bf16[1024,4096]{1,0:T(8,128)(2,1)} %get-tuple-element.232, s32[2048]{0:T(1024)S(1)} %get-tuple-element.189), kind=kCustom, calls=%fused_computation.clone.1 | custom fusion | bytes 33562624 | tf_op jit(solution)/shard_map/while/body/eval_jaxpr/gather | solution.py:25
  576.0 8.6 fusion.59
  584.6 8.2 fusion.62
  596.1 22.0 %bitcast_multiply_fusion.4 = (f32[2048,4096]{1,0:T(8,128)}, f32[2048,4096]{1,0:T(8,128)}) fusion(f32[16,4096]{1,0:T(8,128)S(1)} %get-tuple-element.188, f32[2048]{0:T(1024)S(1)} %get-tuple-element.192, f32[16,4096]{1,0:T(8,128)S(1)} %get-tuple-element.193, f32[2048]{0:T(1024)S(1)} %get-tuple-element.194), kind=kLoop, calls=%fused_computation.8.clone.1 | loop fusion | flops 16777216 | bytes 67649536 | tf_op jit(solution)/shard_map/while/body/eval_jaxpr/mul | solution.py:36
  618.1 61.8 %scatter_fusion = f32[1024,4096]{1,0:T(8,128)} fusion(f32[1024,4096]{1,0:T(8,128)} %get-tuple-element.214, s32[2048]{0:T(1024)S(1)} %bitcast.136, f32[2048,4096]{1,0:T(8,128)} %get-tuple-element.195), kind=kCustom, calls=%fused_computation.4.clone.1 | custom fusion | flops 8388608 | bytes 100671488 | tf_op jit(solution)/shard_map/while/body/eval_jaxpr/scatter-add | solution.py:37
  679.9 61.9 %scatter_fusion.1 = f32[1024,4096]{1,0:T(8,128)} fusion(f32[1024,4096]{1,0:T(8,128)} %get-tuple-element.215, s32[2048]{0:T(1024)S(1)} %bitcast.137, f32[2048,4096]{1,0:T(8,128)} %get-tuple-element.196), kind=kCustom, calls=%fused_computation.5.clone.1 | custom fusion | flops 8388608 | bytes 100671488 | tf_op jit(solution)/shard_map/while/body/eval_jaxpr/scatter-add | solution.py:38
  744.2 33.1 %gather_fusion.1 = bf16[2048,4096]{1,0:T(8,128)(2,1)} fusion(bf16[1024,4096]{1,0:T(8,128)(2,1)} %get-tuple-element.234, s32[2048]{0:T(1024)S(1)} %get-tuple-element.189), kind=kCustom, calls=%fused_computation.1.clone.1 | custom fusion | bytes 33562624 | tf_op jit(solution)/shard_map/while/body/eval_jaxpr/gather | solution.py:26
  777.3 8.0 fusion.60
  785.3 33.1 %gather_fusion = bf16[2048,4096]{1,0:T(8,128)(2,1)} fusion(bf16[1024,4096]{1,0:T(8,128)(2,1)} %get-tuple-element.232, s32[2048]{0:T(1024)S(1)} %get-tuple-element.189), kind=kCustom, calls=%fused_computation.clone.1 | custom fusion | bytes 33562624 | tf_op jit(solution)/shard_map/while/body/eval_jaxpr/gather | solution.py:25
  818.5 8.4 fusion.59
  826.9 8.2 fusion.62
  838.4 22.0 %bitcast_multiply_fusion.4 = (f32[2048,4096]{1,0:T(8,128)}, f32[2048,4096]{1,0:T(8,128)}) fusion(f32[16,4096]{1,0:T(8,128)S(1)} %get-tuple-element.188, f32[2048]{0:T(1024)S(1)} %get-tuple-element.192, f32[16,4096]{1,0:T(8,128)S(1)} %get-tuple-element.193, f32[2048]{0:T(1024)S(1)} %get-tuple-element.194), kind=kLoop, calls=%fused_computation.8.clone.1 | loop fusion | flops 16777216 | bytes 67649536 | tf_op jit(solution)/shard_map/while/body/eval_jaxpr/mul | solution.py:36
  860.4 61.8 %scatter_fusion = f32[1024,4096]{1,0:T(8,128)} fusion(f32[1024,4096]{1,0:T(8,128)} %get-tuple-element.214, s32[2048]{0:T(1024)S(1)} %bitcast.136, f32[2048,4096]{1,0:T(8,128)} %get-tuple-element.195), kind=kCustom, calls=%fused_computation.4.clone.1 | custom fusion | flops 8388608 | bytes 100671488 | tf_op jit(solution)/shard_map/while/body/eval_jaxpr/scatter-add | solution.py:37
  922.2 62.2 %scatter_fusion.1 = f32[1024,4096]{1,0:T(8,128)} fusion(f32[1024,4096]{1,0:T(8,128)} %get-tuple-element.215, s32[2048]{0:T(1024)S(1)} %bitcast.137, f32[2048,4096]{1,0:T(8,128)} %get-tuple-element.196), kind=kCustom, calls=%fused_computation.5.clone.1 | custom fusion | flops 8388608 | bytes 100671488 | tf_op jit(solution)/shard_map/while/body/eval_jaxpr/scatter-add | solution.py:38
  986.4 33.1 %gather_fusion.1 = bf16[2048,4096]{1,0:T(8,128)(2,1)} fusion(bf16[1024,4096]{1,0:T(8,128)(2,1)} %get-tuple-element.234, s32[2048]{0:T(1024)S(1)} %get-tuple-element.189), kind=kCustom, calls=%fused_computation.1.clone.1 | custom fusion | bytes 33562624 | tf_op jit(solution)/shard_map/while/body/eval_jaxpr/gather | solution.py:26
  1019.5 8.0 fusion.60
  1027.6 33.1 %gather_fusion = bf16[2048,4096]{1,0:T(8,128)(2,1)} fusion(bf16[1024,4096]{1,0:T(8,128)(2,1)} %get-tuple-element.232, s32[2048]{0:T(1024)S(1)} %get-tuple-element.189), kind=kCustom, calls=%fused_computation.clone.1 | custom fusion | bytes 33562624 | tf_op jit(solution)/shard_map/while/body/eval_jaxpr/gather | solution.py:25
  1060.7 8.6 fusion.59
  1069.4 8.2 fusion.62
  1080.9 22.0 %bitcast_multiply_fusion.4 = (f32[2048,4096]{1,0:T(8,128)}, f32[2048,4096]{1,0:T(8,128)}) fusion(f32[16,4096]{1,0:T(8,128)S(1)} %get-tuple-element.188, f32[2048]{0:T(1024)S(1)} %get-tuple-element.192, f32[16,4096]{1,0:T(8,128)S(1)} %get-tuple-element.193, f32[2048]{0:T(1024)S(1)} %get-tuple-element.194), kind=kLoop, calls=%fused_computation.8.clone.1 | loop fusion | flops 16777216 | bytes 67649536 | tf_op jit(solution)/shard_map/while/body/eval_jaxpr/mul | solution.py:36
  1102.9 61.8 %scatter_fusion = f32[1024,4096]{1,0:T(8,128)} fusion(f32[1024,4096]{1,0:T(8,128)} %get-tuple-element.214, s32[2048]{0:T(1024)S(1)} %bitcast.136, f32[2048,4096]{1,0:T(8,128)} %get-tuple-element.195), kind=kCustom, calls=%fused_computation.4.clone.1 | custom fusion | flops 8388608 | bytes 100671488 | tf_op jit(solution)/shard_map/while/body/eval_jaxpr/scatter-add | solution.py:37
  1164.7 61.9 %scatter_fusion.1 = f32[1024,4096]{1,0:T(8,128)} fusion(f32[1024,4096]{1,0:T(8,128)} %get-tuple-element.215, s32[2048]{0:T(1024)S(1)} %bitcast.137, f32[2048,4096]{1,0:T(8,128)} %get-tuple-element.196), kind=kCustom, calls=%fused_computation.5.clone.1 | custom fusion | flops 8388608 | bytes 100671488 | tf_op jit(solution)/shard_map/while/body/eval_jaxpr/scatter-add | solution.py:38
  1229.7 9.0 convert_element_type.58
  1242.4 9.0 convert_element_type.54
  1251.4 85.0 %all-to-all-done.4 = bf16[8,128,4096]{2,1,0:T(8,128)(2,1)} async-done(((bf16[8,128,4096]{2,1,0:T(8,128)(2,1)}), bf16[8,128,4096]{2,1,0:T(8,128)(2,1)}, u32[]{:S(2)}, u32[]{:S(2)}) %all-to-all-start.4) | async-done | bytes 8388640 | tf_op jit(solution)/shard_map/all_to_all | solution.py:62
  1340.1 38.0 %scatter_custom_fusion.3 = f32[2048,4096]{1,0:T(8,128)} fusion(s32[1024]{0:T(1024)} %bitcast.146, bf16[1024,4096]{1,0:T(8,128)(2,1)} %bitcast.44, f32[]{:T(128)} %constant.9.clone.1), kind=kCustom, calls=%fused_computation.46 | custom fusion | flops 8388608 | bytes 41943552 | tf_op jit(solution)/shard_map/scatter-add | solution.py:65
  1378.1 17.4 %convert_element_type.61 = bf16[2048,4096]{1,0:T(8,128)(2,1)} convert(f32[2048,4096]{1,0:T(8,128)} %scatter_custom_fusion.3) | non-fusion elementwise | flops 8388608 | bytes 50331648 | tf_op jit(solution)/shard_map/convert_element_type | solution.py:66
  1395.5 38.6 %all-to-all-done.3 = bf16[8,128,4096]{2,1,0:T(8,128)(2,1)} async-done(((bf16[8,128,4096]{2,1,0:T(8,128)(2,1)}), bf16[8,128,4096]{2,1,0:T(8,128)(2,1)}, u32[]{:S(2)}, u32[]{:S(2)}) %all-to-all-start.3) | async-done | bytes 8388640 | tf_op jit(solution)/shard_map/all_to_all | solution.py:61
  1434.1 37.5 %scatter_custom_fusion.2 = f32[2048,4096]{1,0:T(8,128)} fusion(s32[1024]{0:T(1024)} %bitcast.147, bf16[1024,4096]{1,0:T(8,128)(2,1)} %bitcast.43, f32[]{:T(128)} %constant.9.clone.1), kind=kCustom, calls=%fused_computation.48 | custom fusion | flops 8388608 | bytes 41943552 | tf_op jit(solution)/shard_map/scatter-add | solution.py:64
  1471.7 17.4 %convert_element_type.57 = bf16[2048,4096]{1,0:T(8,128)(2,1)} convert(f32[2048,4096]{1,0:T(8,128)} %scatter_custom_fusion.2) | non-fusion elementwise | flops 8388608 | bytes 50331648 | tf_op jit(solution)/shard_map/convert_element_type | solution.py:66
  (113 shorter events, 36.8 us)
Async XLA Ops:
  9.5 0.6 copy-start.6
  33.0 97.7 %all-to-all-start.2 = ((bf16[8,128,4096]{2,1,0:T(8,128)(2,1)}), bf16[8,128,4096]{2,1,0:T(8,128)(2,1)}, u32[]{:S(2)}, u32[]{:S(2)}) async-start(bf16[8,128,4096]{2,1,0:T(8,128)(2,1)} %bitcast.135), calls=%async_computation.2 | async-start | bytes 16777216 | tf_op jit(solution)/shard_map/all_to_all | solution.py:59
  59.8 74.7 %copy-start.4 = (s32[64,4,32]{0,2,1:T(8,128)S(1)}, s32[64,4,32]{0,2,1:T(8,128)}, u32[]{:S(2)}) copy-start(s32[64,4,32]{0,2,1:T(8,128)} %param.10) | copy-start | bytes 98308
  59.8 74.9 %copy-start.5 = (f32[64,4,32]{0,2,1:T(8,128)S(1)}, f32[64,4,32]{0,2,1:T(8,128)}, u32[]{:S(2)}) copy-start(f32[64,4,32]{0,2,1:T(8,128)} %param.12) | copy-start | bytes 98308
  130.8 97.7 %all-to-all-start.1 = ((bf16[8,128,4096]{2,1,0:T(8,128)(2,1)}), bf16[8,128,4096]{2,1,0:T(8,128)(2,1)}, u32[]{:S(2)}, u32[]{:S(2)}) async-start(bf16[8,128,4096]{2,1,0:T(8,128)(2,1)} %bitcast.132), calls=%async_computation.1 | async-start | bytes 16777216 | tf_op jit(solution)/shard_map/all_to_all | solution.py:58
  245.2 1.0 copy-start
  245.2 96.8 %copy-start.2 = (f32[4,16,128]{2,1,0:T(8,128)}, f32[4,16,128]{2,1,0:T(8,128)S(1)}, u32[]{:S(2)}) copy-start(f32[4,16,128]{2,1,0:T(8,128)S(1)} %get-tuple-element.231) | copy-start | bytes 98308 | tf_op jit(solution)/shard_map/while
  321.5 28.8 %slice-start = ((s8[16777216]{0:T(1024)(128)(4,1)}), s8[4194304]{0:T(1024)(128)(4,1)S(1)}, s32[]{:S(2)}) async-start(s8[16777216]{0:T(1024)(128)(4,1)} %bitcast.127), calls=%async_computation.5 | async-start | bytes 8388608 | tf_op jit(solution)/shard_map/while
  321.5 28.8 %slice-start.1 = ((s8[16777216]{0:T(1024)(128)(4,1)}), s8[4194304]{0:T(1024)(128)(4,1)S(1)}, s32[]{:S(2)}) async-start(s8[16777216]{0:T(1024)(128)(4,1)} %bitcast.127), calls=%async_computation.6 | async-start | bytes 8388608 | tf_op jit(solution)/shard_map/while
  321.5 28.8 %slice-start.2 = ((s8[16777216]{0:T(1024)(128)(4,1)}), s8[4194304]{0:T(1024)(128)(4,1)S(1)}, s32[]{:S(2)}) async-start(s8[16777216]{0:T(1024)(128)(4,1)} %bitcast.127), calls=%async_computation.7 | async-start | bytes 8388608 | tf_op jit(solution)/shard_map/while
  342.1 8.2 slice-start.3
  437.4 62.2 %copy-start.1 = (s32[4,16,128]{2,1,0:T(8,128)S(1)}, s32[4,16,128]{2,1,0:T(8,128)}, u32[]{:S(2)}) copy-start(s32[4,16,128]{2,1,0:T(8,128)} %copy-done) | copy-start | bytes 98308 | tf_op jit(solution)/shard_map/while
  437.4 62.2 %copy-start.3 = (f32[4,16,128]{2,1,0:T(8,128)S(1)}, f32[4,16,128]{2,1,0:T(8,128)}, u32[]{:S(2)}) copy-start(f32[4,16,128]{2,1,0:T(8,128)} %copy-done.2) | copy-start | bytes 98308 | tf_op jit(solution)/shard_map/while
  499.7 1.0 copy-start
  499.7 84.8 %copy-start.2 = (f32[4,16,128]{2,1,0:T(8,128)}, f32[4,16,128]{2,1,0:T(8,128)S(1)}, u32[]{:S(2)}) copy-start(f32[4,16,128]{2,1,0:T(8,128)S(1)} %get-tuple-element.231) | copy-start | bytes 98308 | tf_op jit(solution)/shard_map/while
  575.9 16.9 %slice-start = ((s8[16777216]{0:T(1024)(128)(4,1)}), s8[4194304]{0:T(1024)(128)(4,1)S(1)}, s32[]{:S(2)}) async-start(s8[16777216]{0:T(1024)(128)(4,1)} %bitcast.127), calls=%async_computation.5 | async-start | bytes 8388608 | tf_op jit(solution)/shard_map/while
  575.9 16.9 %slice-start.1 = ((s8[16777216]{0:T(1024)(128)(4,1)}), s8[4194304]{0:T(1024)(128)(4,1)S(1)}, s32[]{:S(2)}) async-start(s8[16777216]{0:T(1024)(128)(4,1)} %bitcast.127), calls=%async_computation.6 | async-start | bytes 8388608 | tf_op jit(solution)/shard_map/while
  576.0 16.9 %slice-start.2 = ((s8[16777216]{0:T(1024)(128)(4,1)}), s8[4194304]{0:T(1024)(128)(4,1)S(1)}, s32[]{:S(2)}) async-start(s8[16777216]{0:T(1024)(128)(4,1)} %bitcast.127), calls=%async_computation.7 | async-start | bytes 8388608 | tf_op jit(solution)/shard_map/while
  584.6 8.2 slice-start.3
  679.9 61.9 %copy-start.1 = (s32[4,16,128]{2,1,0:T(8,128)S(1)}, s32[4,16,128]{2,1,0:T(8,128)}, u32[]{:S(2)}) copy-start(s32[4,16,128]{2,1,0:T(8,128)} %copy-done) | copy-start | bytes 98308 | tf_op jit(solution)/shard_map/while
  679.9 61.9 %copy-start.3 = (f32[4,16,128]{2,1,0:T(8,128)S(1)}, f32[4,16,128]{2,1,0:T(8,128)}, u32[]{:S(2)}) copy-start(f32[4,16,128]{2,1,0:T(8,128)} %copy-done.2) | copy-start | bytes 98308 | tf_op jit(solution)/shard_map/while
  742.2 1.0 copy-start
  742.2 84.6 %copy-start.2 = (f32[4,16,128]{2,1,0:T(8,128)}, f32[4,16,128]{2,1,0:T(8,128)S(1)}, u32[]{:S(2)}) copy-start(f32[4,16,128]{2,1,0:T(8,128)S(1)} %get-tuple-element.231) | copy-start | bytes 98308 | tf_op jit(solution)/shard_map/while
  818.4 16.6 %slice-start = ((s8[16777216]{0:T(1024)(128)(4,1)}), s8[4194304]{0:T(1024)(128)(4,1)S(1)}, s32[]{:S(2)}) async-start(s8[16777216]{0:T(1024)(128)(4,1)} %bitcast.127), calls=%async_computation.5 | async-start | bytes 8388608 | tf_op jit(solution)/shard_map/while
  818.5 16.6 %slice-start.1 = ((s8[16777216]{0:T(1024)(128)(4,1)}), s8[4194304]{0:T(1024)(128)(4,1)S(1)}, s32[]{:S(2)}) async-start(s8[16777216]{0:T(1024)(128)(4,1)} %bitcast.127), calls=%async_computation.6 | async-start | bytes 8388608 | tf_op jit(solution)/shard_map/while
  818.5 16.6 %slice-start.2 = ((s8[16777216]{0:T(1024)(128)(4,1)}), s8[4194304]{0:T(1024)(128)(4,1)S(1)}, s32[]{:S(2)}) async-start(s8[16777216]{0:T(1024)(128)(4,1)} %bitcast.127), calls=%async_computation.7 | async-start | bytes 8388608 | tf_op jit(solution)/shard_map/while
  826.9 8.2 slice-start.3
  922.2 62.2 %copy-start.1 = (s32[4,16,128]{2,1,0:T(8,128)S(1)}, s32[4,16,128]{2,1,0:T(8,128)}, u32[]{:S(2)}) copy-start(s32[4,16,128]{2,1,0:T(8,128)} %copy-done) | copy-start | bytes 98308 | tf_op jit(solution)/shard_map/while
  922.2 62.2 %copy-start.3 = (f32[4,16,128]{2,1,0:T(8,128)S(1)}, f32[4,16,128]{2,1,0:T(8,128)}, u32[]{:S(2)}) copy-start(f32[4,16,128]{2,1,0:T(8,128)} %copy-done.2) | copy-start | bytes 98308 | tf_op jit(solution)/shard_map/while
  984.5 1.0 copy-start
  984.5 84.8 %copy-start.2 = (f32[4,16,128]{2,1,0:T(8,128)}, f32[4,16,128]{2,1,0:T(8,128)S(1)}, u32[]{:S(2)}) copy-start(f32[4,16,128]{2,1,0:T(8,128)S(1)} %get-tuple-element.231) | copy-start | bytes 98308 | tf_op jit(solution)/shard_map/while
  1060.7 16.9 %slice-start = ((s8[16777216]{0:T(1024)(128)(4,1)}), s8[4194304]{0:T(1024)(128)(4,1)S(1)}, s32[]{:S(2)}) async-start(s8[16777216]{0:T(1024)(128)(4,1)} %bitcast.127), calls=%async_computation.5 | async-start | bytes 8388608 | tf_op jit(solution)/shard_map/while
  1060.7 16.9 %slice-start.1 = ((s8[16777216]{0:T(1024)(128)(4,1)}), s8[4194304]{0:T(1024)(128)(4,1)S(1)}, s32[]{:S(2)}) async-start(s8[16777216]{0:T(1024)(128)(4,1)} %bitcast.127), calls=%async_computation.6 | async-start | bytes 8388608 | tf_op jit(solution)/shard_map/while
  1060.7 16.9 %slice-start.2 = ((s8[16777216]{0:T(1024)(128)(4,1)}), s8[4194304]{0:T(1024)(128)(4,1)S(1)}, s32[]{:S(2)}) async-start(s8[16777216]{0:T(1024)(128)(4,1)} %bitcast.127), calls=%async_computation.7 | async-start | bytes 8388608 | tf_op jit(solution)/shard_map/while
  1069.4 8.2 slice-start.3
  1164.7 61.9 %copy-start.1 = (s32[4,16,128]{2,1,0:T(8,128)S(1)}, s32[4,16,128]{2,1,0:T(8,128)}, u32[]{:S(2)}) copy-start(s32[4,16,128]{2,1,0:T(8,128)} %copy-done) | copy-start | bytes 98308 | tf_op jit(solution)/shard_map/while
  1164.7 61.9 %copy-start.3 = (f32[4,16,128]{2,1,0:T(8,128)S(1)}, f32[4,16,128]{2,1,0:T(8,128)}, u32[]{:S(2)}) copy-start(f32[4,16,128]{2,1,0:T(8,128)} %copy-done.2) | copy-start | bytes 98308 | tf_op jit(solution)/shard_map/while
  1238.8 97.7 %all-to-all-start.4 = ((bf16[8,128,4096]{2,1,0:T(8,128)(2,1)}), bf16[8,128,4096]{2,1,0:T(8,128)(2,1)}, u32[]{:S(2)}, u32[]{:S(2)}) async-start(bf16[8,128,4096]{2,1,0:T(8,128)(2,1)} %bitcast.134), calls=%async_computation.4 | async-start | bytes 16777216 | tf_op jit(solution)/shard_map/all_to_all | solution.py:62
  1336.4 97.7 %all-to-all-start.3 = ((bf16[8,128,4096]{2,1,0:T(8,128)(2,1)}), bf16[8,128,4096]{2,1,0:T(8,128)(2,1)}, u32[]{:S(2)}, u32[]{:S(2)}) async-start(bf16[8,128,4096]{2,1,0:T(8,128)(2,1)} %bitcast.133), calls=%async_computation.3 | async-start | bytes 16777216 | tf_op jit(solution)/shard_map/all_to_all | solution.py:61
where the time goes:
time: 1500 us; the launch traced here: 1490 us
  other arithmetic  719 us (48%)
  local copies, waits for them, and re-layouts  333 us (22%)
  waiting for transfers between devices  288 us (19%)
  matrix products  120 us (8%)
    scatter-add x4, other arithmetic, scan_step(): acc_down = acc_down.at[flat_slots].add(down_part.reshape(-1, width))  248 us
    scatter-add x4, other arithmetic, scan_step(): acc_up = acc_up.at[flat_slots].add(up_part.reshape(-1, width))  247 us
    gather x4, local copies, waits for them, and re-layouts, scan_step(): up_rows = up_table[slot_blk]  133 us
    gather x4, local copies, waits for them, and re-layouts, scan_step(): down_rows = down_table[slot_blk]  132 us
    all_to_all x1, waiting for transfers between devices, per_device(): lax.all_to_all(up_local[asked_rows], 'ep', 0, 0, tiled=True)  93.5 us
    mul x8, other arithmetic, scan_step(): down_part = w_out.astype(jnp.float32)[:, :, None] * dy_blk[:, None, :]  88.1 us
    all_to_all x1, waiting for transfers between devices, per_device(): lax.all_to_all(acc_down.astype(jnp.bfloat16).reshape(n_group, n_req, widt...  85 us
    all_to_all x1, waiting for transfers between devices, per_device(): lax.all_to_all(down_local[asked_rows], 'ep', 0, 0, tiled=True)  71 us
  transfers between devices with their start and end apart: 4, of which 4 were waited for; matrix products, arithmetic and copies ran while one was open for 6% of the time, Pallas kernels for 0%

commit v1 on v0

v1 whole, which is shorter than its diff:
```python
import functools
import math
import jax
import jax.numpy as jnp
from jax import lax
from jax.experimental import pallas as pl
from jax.experimental.pallas import tpu as pltpu
from jax.sharding import PartitionSpec as P

F32, BF16 = jnp.float32, jnp.bfloat16
N_DEV, TOK, SLOTS, SEL = 8, 64, 128, 128
VMEM_BYTES = 60 * 1024 * 1024


def gelu_pair(pre_act):
    normal_cdf = 0.5 * (1.0 + lax.erf(pre_act * (2.0 ** -0.5)))
    normal_pdf = jnp.exp(-0.5 * pre_act * pre_act) * ((2.0 * math.pi) ** -0.5)
    return pre_act * normal_cdf, normal_cdf + pre_act * normal_pdf


def split3(wide):
    high = wide.astype(BF16)
    rest = wide - high.astype(F32)
    mid = rest.astype(BF16)
    low = (rest - mid.astype(F32)).astype(BF16)
    return high, mid, low


def select_kernel(act_ref, slope_ref, slot_ref, gate_ref, w_ref, c_ref, wt_ref, ct_ref, slot_t, w_t, c_t):
    owner = lax.axis_index("ep")
    local = slot_ref[...] - owner * SLOTS
    valid = (local >= 0) & (local < SLOTS)
    index = jnp.where(valid, local, 0)
    act = jnp.take_along_axis(act_ref[...], index, axis=1)
    slope = jnp.take_along_axis(slope_ref[...], index, axis=1)
    gate = gate_ref[...]
    w_sel = jnp.where(valid, (gate * act).astype(BF16).astype(F32), 0.0)
    c_sel = jnp.where(valid, (gate * slope).astype(BF16).astype(F32), 0.0)
    slot_t[...] = jnp.where(valid, local, -1).T
    w_t[...] = w_sel.T
    c_t[...] = c_sel.T
    rows = lax.broadcasted_iota(jnp.int32, (SLOTS, 2 * TOK), 0)

    def step(s, acc):
        acc_w, acc_c = acc
        hit = rows == slot_t[pl.ds(s, 1), :]
        acc_w += jnp.where(hit, w_t[pl.ds(s, 1), :], 0.0)
        acc_c += jnp.where(hit, c_t[pl.ds(s, 1), :], 0.0)
        return acc_w, acc_c

    zero = jnp.zeros((SLOTS, 2 * TOK), F32)
    acc_w, acc_c = lax.fori_loop(0, SEL, step, (zero, zero), unroll=4)
    for k, term in enumerate(split3(acc_w.T)):
        w_ref[k] = term
    for k, term in enumerate(split3(acc_c.T)):
        c_ref[k] = term
    for k, term in enumerate(split3(acc_w)):
        wt_ref[k] = term
    for k, term in enumerate(split3(acc_c)):
        ct_ref[k] = term


def token_kernel(w_ref, c_ref, v_ref, u_ref, out_ref):
    width = v_ref.shape[1]
    for col in range(0, width, 512):
        out_ref[:, col:col + 512] = sum(jnp.dot(w_ref[k], v_ref[:, col:col + 512], preferred_element_type=F32) for k in range(3))
        out_ref[:, width + col:width + col + 512] = sum(jnp.dot(c_ref[k], u_ref[:, col:col + 512], preferred_element_type=F32) for k in range(3))


def row_kernel(block, req_ref, wt_ref, ct_ref, x_ref, dy_ref, du_ref, dv_ref, lhs):
    first = pl.program_id(0) * block
    rows = lax.broadcasted_iota(jnp.int32, (block, SLOTS), 0) + first
    for q in range(N_DEV):
        pick = jnp.where(rows == req_ref[pl.ds(q, 1), :], 1.0, 0.0).astype(BF16)
        cols = slice(q * TOK, (q + 1) * TOK)
        half = slice((q % 2) * TOK, (q % 2 + 1) * TOK)
        for k in range(3):
            for m, ref in enumerate((ct_ref, wt_ref)):
                full = jnp.dot(pick, ref[k, (q // 2) * SLOTS:(q // 2 + 1) * SLOTS, :], preferred_element_type=F32)
                lhs[m, k, :, cols] = full[:, half].astype(BF16)
    width = x_ref.shape[1]
    for col in range(0, width, 512):
        du_ref[:, col:col + 512] = sum(jnp.dot(lhs[0, k], x_ref[:, col:col + 512], preferred_element_type=F32) for k in range(3)).astype(BF16)
        dv_ref[:, col:col + 512] = sum(jnp.dot(lhs[1, k], dy_ref[:, col:col + 512], preferred_element_type=F32) for k in range(3)).astype(BF16)


def solution(mesh):
    tok_spec = P(('dp', 'ep'))
    table_spec = P('ep')

    def per_device(tokens, slot_ids, request_rows, gate_vals, grad_out, up_local, down_local):
        width = tokens.shape[1]
        rows_owner = up_local.shape[0]
        owner = lax.axis_index('ep')
        n_tok = N_DEV * TOK
        small = jnp.concatenate([request_rows[0].astype(F32), slot_ids.reshape(TOK, SEL).astype(F32), gate_vals.reshape(TOK, SEL)], axis=0)
        small_all = lax.all_gather(small, 'ep', axis=0)
        x_all = lax.all_gather(tokens, 'ep', axis=0)
        dy_all = lax.all_gather(grad_out, 'ep', axis=0)
        asked = lax.dynamic_index_in_dim(small_all[:, :N_DEV], owner, 1, keepdims=False).astype(jnp.int32)
        slot_all = small_all[:, N_DEV:N_DEV + TOK].astype(jnp.int32).reshape(n_tok, SEL)
        gate_all = small_all[:, N_DEV + TOK:].reshape(n_tok, SEL)
        up_rows = up_local[asked]
        down_rows = down_local[asked]
        pre_act = jnp.einsum('qtd,qrd->qtr', x_all, up_rows, preferred_element_type=F32)
        back_dot = jnp.einsum('qtd,qrd->qtr', dy_all, down_rows, preferred_element_type=F32)
        act, slope = gelu_pair(pre_act)
        slope = slope * back_dot
        pair = 2 * TOK
        blk = pl.BlockSpec((pair, SLOTS), lambda i: (i, 0))
        tok_blk = pl.BlockSpec((3, pair, SLOTS), lambda i: (0, i, 0))
        tr_blk = pl.BlockSpec((3, SLOTS, pair), lambda i: (0, i, 0))
        w_tok, c_tok, w_tr, c_tr = pl.pallas_call(
            select_kernel,
            grid=(n_tok // pair,),
            in_specs=[blk] * 4,
            out_specs=[tok_blk, tok_blk, tr_blk, tr_blk],
            out_shape=[jax.ShapeDtypeStruct((3, n_tok, SLOTS), BF16)] * 2 + [jax.ShapeDtypeStruct((3, n_tok // pair * SLOTS, pair), BF16)] * 2,
            scratch_shapes=[pltpu.VMEM((SEL, pair), jnp.int32), pltpu.VMEM((SEL, pair), F32), pltpu.VMEM((SEL, pair), F32)],
        )(act.reshape(n_tok, SLOTS), slope.reshape(n_tok, SLOTS), slot_all, gate_all)
        coef = pl.BlockSpec((3, TOK, SLOTS), lambda q: (0, q, 0))
        table = pl.BlockSpec((None, SLOTS, width), lambda q: (q, 0, 0))
        partial = pl.pallas_call(
            token_kernel,
            grid=(N_DEV,),
            in_specs=[coef, coef, table, table],
            out_specs=pl.BlockSpec((TOK, 2 * width), lambda q: (q, 0)),
            out_shape=jax.ShapeDtypeStruct((n_tok, 2 * width), F32),
            compiler_params=pltpu.CompilerParams(vmem_limit_bytes=VMEM_BYTES),
        )(w_tok, c_tok, down_rows, up_rows)
        token_out = lax.psum_scatter(partial, 'ep', scatter_dimension=0, tiled=True)
        block = 256
        whole = lambda *shape: pl.BlockSpec(shape, lambda i: (0,) * len(shape))
        rows_blk = pl.BlockSpec((block, width), lambda i: (i, 0))
        grad_up, grad_down = pl.pallas_call(
            functools.partial(row_kernel, block),
            grid=(rows_owner // block,),
            in_specs=[whole(N_DEV, SLOTS), whole(*w_tr.shape), whole(*c_tr.shape), whole(n_tok, width), whole(n_tok, width)],
            out_specs=[rows_blk, rows_blk],
            out_shape=[jax.ShapeDtypeStruct((rows_owner, width), BF16)] * 2,
            scratch_shapes=[pltpu.VMEM((2, 3, block, n_tok), BF16)],
            compiler_params=pltpu.CompilerParams(vmem_limit_bytes=VMEM_BYTES),
            cost_estimate=pl.CostEstimate(flops=12 * rows_owner * width * n_tok, bytes_accessed=4 * rows_owner * width, transcendentals=0),
        )(asked, w_tr, c_tr, x_all.reshape(n_tok, width), dy_all.reshape(n_tok, width))
        return token_out[:, :width].astype(BF16), token_out[:, width:].astype(BF16), grad_up, grad_down

    return jax.shard_map(per_device, mesh=mesh, in_specs=(tok_spec, tok_spec, tok_spec, tok_spec, tok_spec, table_spec, table_spec), out_specs=(tok_spec, tok_spec, tok_spec, tok_spec), check_vma=False)
```

time: 1500 us -> 238 us (0.16)
  other arithmetic: 719 us -> 5 us
  local copies, waits for them, and re-layouts: 333 us -> 48.1 us
  waiting for transfers between devices: 288 us -> 42.5 us
  matrix products: 120 us -> 16.6 us
  Pallas kernels: 0 us -> 94.4 us
    scatter-add x10 -> x0, other arithmetic: 571 us -> none  [the longest x4 248 us: scan_step(): acc_down = acc_down.at[flat_slots].add(down_part.reshape(-1, width))]
    all_to_all x4 -> x0, waiting for transfers between devices: 288 us -> none  [the longest x1 93.5 us: per_device(): lax.all_to_all(up_local[asked_rows], 'ep', 0, 0, tiled=True)]
    gather x10 -> x2, local copies, waits for them, and re-layouts: 311 us -> 46.2 us  [the longest x1 23.2 us: per_device(): down_rows = down_local[asked]]
    dot_general x16 -> x2, matrix products: 120 us -> 16.6 us  [the longest x1 8.31 us: per_device(): jnp.einsum('qtd,qrd->qtr', x_all, up_rows, preferred_element_type=F32)]
    pallas_call x0 -> x3, Pallas kernels: none -> 94.4 us  [the longest x1 65.4 us: per_device(): pl.pallas_call(functools.partial(row_kernel, block), grid=(rows_owner //...]
    mul x8 -> x0, other arithmetic: 88.1 us -> none  [scan_step(): down_part = w_out.astype(jnp.float32)[:, :, None] * dy_blk[:, None, :]]
    convert_element_type x8 -> x3, other arithmetic: 56.5 us -> 1.45 us  [the longest x1 0.85 us: per_device(): slot_ids.reshape(TOK, SEL).astype(F32)]
    reduce_scatter x0 -> x1, waiting for transfers between devices: none -> 41.1 us  [per_device(): token_out = lax.psum_scatter(partial, 'ep', scatter_dimension=0, tiled=True)]
  transfers between devices with their start and end apart: 4 -> 3, of which waited for: 4 -> 1; matrix products, arithmetic and copies ran while one was open for 6% -> 25% of each run, Pallas kernels for 0% -> 27%
where the time goes in v1:
time: 238 us
  Pallas kernels  94.4 us (40%)
  local copies, waits for them, and re-layouts  48.1 us (20%)
  waiting for transfers between devices  42.5 us (18%)
  blocking collectives  17.5 us (7%)
  matrix products  16.6 us (7%)
  between operations  13.8 us (6%)
  other arithmetic  5 us (2%)
    pallas_call x1, Pallas kernels, per_device(): pl.pallas_call(functools.partial(row_kernel, block), grid=(rows_owner //...  65.4 us
    reduce_scatter x1, waiting for transfers between devices, per_device(): token_out = lax.psum_scatter(partial, 'ep', scatter_dimension=0, tiled=True)  41.1 us
    gather x1, local copies, waits for them, and re-layouts, per_device(): down_rows = down_local[asked]  23.2 us
    gather x1, local copies, waits for them, and re-layouts, per_device(): up_rows = up_local[asked]  23 us
    all_gather x1, blocking collectives, per_device(): small_all = lax.all_gather(small, 'ep', axis=0)  17.5 us
    pallas_call x1, Pallas kernels, per_device(): pl.pallas_call(token_kernel, grid=(N_DEV,), in_specs=[coef, coef, table,...  17.2 us
    pallas_call x1, Pallas kernels, per_device(): pl.pallas_call(select_kernel, grid=(n_tok // pair,), in_specs=[blk] * 4,...  11.9 us
    dot_general x1, matrix products, per_device(): jnp.einsum('qtd,qrd->qtr', x_all, up_rows, preferred_element_type=F32)  8.31 us
  transfers between devices with their start and end apart: 3, of which 1 were waited for; matrix products, arithmetic and copies ran while one was open for 25% of the time, Pallas kernels for 27%

profile of v1, /device:TPU:0, one launch (start us, length us, event | category | flops | bytes accessed | tf_op | source)
XLA Modules:
  0.0 238.0 jit_solution(3409138008421800974)
XLA Ops:
  7.2 0.0 all-gather.6.cloned.1.call-start
  7.2 0.7 all-gather.6.cloned.1.call-update
  7.9 0.0 all-gather.8.cloned.1.call-start
  7.9 0.7 all-gather.8.cloned.1.call-update
  8.6 0.0 reduce-scatter.2.cloned.1.call-start
  8.7 0.8 convert_element_type.26
  9.5 0.8 copy.18
  10.3 1.0 pad_maximum_fusion
  11.3 0.1 copy.19
  11.4 17.5 %all-gather = f32[1088,128]{1,0:T(8,128)S(1)} all-gather(f32[136,128]{1,0:T(8,128)S(1)} %copy.19), channel_id=2, replica_groups=mesh['dp'=1,'ep'=8] {'ep'}, dimensions={0}, use_global_device_ids=true | all-gather | bytes 626688 | tf_op jit(solution)/shard_map/all_gather | solution.py:97
  28.9 23.2 %gather_fusion.1 = bf16[1024,4096]{1,0:T(8,128)(2,1)} fusion(bf16[2048,4096]{1,0:T(8,128)(2,1)} %param.13, s32[1024]{0:T(1024)S(1)} %fusion.6), kind=kCustom, calls=%fused_computation.1 | custom fusion | bytes 16781312 | tf_op jit(solution)/shard_map/gather | solution.py:104
  52.1 23.0 %gather_fusion = bf16[1024,4096]{1,0:T(8,128)(2,1)} fusion(bf16[2048,4096]{1,0:T(8,128)(2,1)} %param.12, s32[1024]{0:T(1024)S(1)} %fusion.6), kind=kCustom, calls=%fused_computation | custom fusion | bytes 16781312 | tf_op jit(solution)/shard_map/gather | solution.py:103
  75.1 0.9 fusion.9
  76.0 0.0 all-gather.6.cloned.1.call-done.x_ref
  76.0 8.3 %fusion.7 = (f32[8,64,128]{2,1,0:T(8,128)}, f32[8,64,128]{2,1,0:T(8,128)S(1)}) fusion(bf16[8,128,4096]{2,1,0:T(8,128)(2,1)} %bitcast.34, bf16[8,64,4096]{2,1,0:T(8,128)(2,1)} %bitcast.36), kind=kOutput, calls=%fused_computation.19 | convolution fusion | flops 537133056 | bytes 13107200 | tf_op jit(solution)/shard_map/qtd,qrd->qtr/dot_general | solution.py:105
  84.3 0.0 all-gather.8.cloned.1.call-done.dy_ref
  84.3 8.3 %fusion = f32[8,64,128]{2,1,0:T(8,128)} fusion(bf16[8,128,4096]{2,1,0:T(8,128)(2,1)} %bitcast.32, bf16[8,64,4096]{2,1,0:T(8,128)(2,1)} %bitcast.37, f32[8,64,128]{2,1,0:T(8,128)S(1)} %get-tuple-element.21), kind=kOutput, calls=%fused_computation.4 | convolution fusion | flops 537460736 | bytes 13107200 | tf_op jit(solution)/shard_map/qtd,qrd->qtr/dot_general | solution.py:106
  92.6 11.9 %shard_map.102 = (bf16[3,512,128]{2,1,0:T(8,128)(2,1)}, bf16[3,512,128]{2,1,0:T(8,128)(2,1)}, bf16[3,512,128]{2,1,0:T(8,128)(2,1)}, bf16[3,512,128]{2,1,0:T(8,128)(2,1)}) custom-call(f32[512,128]{1,0:T(8,128)} %bitcast.40, f32[512,128]{1,0:T(8,128)} %bitcast.41, s32[512,128]{1,0:T(8,128)} %bitcast.43, f32[512,128]{1,0:T(8,128)} %bitcast.42), custom_call_target="tpu_custom_call" | custom-call | tf_op jit(solution)/shard_map/pallas_call | solution.py:113
  104.4 17.2 %shard_map.103 = f32[512,8192]{1,0:T(8,128)} custom-call(bf16[3,512,128]{2,1,0:T(8,128)(2,1)} %get-tuple-element.10.w_ref, bf16[3,512,128]{2,1,0:T(8,128)(2,1)} %get-tuple-element.11.c_ref, bf16[8,128,4096]{2,1,0:T(8,128)(2,1)} %bitcast.33, bf16[8,128,4096]{2,1,0:T(8,128)(2,1)} %bitcast.35), custom_call_target="tpu_custom_call" | custom-call | tf_op jit(solution)/shard_map/pallas_call | solution.py:123
  121.6 0.0 reduce-scatter.2.cloned.1.call-update
  121.6 0.6 convert_bitcast_fusion.1.req_ref
  122.2 65.4 %shard_map.104 = (bf16[2048,4096]{1,0:T(8,128)(2,1)}, bf16[2048,4096]{1,0:T(8,128)(2,1)}) custom-call(s32[8,128]{1,0:T(8,128)} %convert_bitcast_fusion.1.req_ref, bf16[3,512,128]{2,1,0:T(8,128)(2,1)} %get-tuple-element.12.wt_ref, bf16[3,512,128]{2,1,0:T(8,128)(2,1)} %get-tuple-element.13.ct_ref, bf16[512,4096]{1,0:T(8,128)(2,1)} %all-gather.6.cloned.1.call-done.x_ref, ...), custom_call_target="tpu_custom_call" | custom-call | flops 51539607552 | bytes 33554432 | tf_op jit(solution)/shard_map/pallas_call | solution.py:135
  187.6 41.1 %reduce-scatter.2.cloned.1.call-done = f32[64,8192]{1,0:T(8,128)} async-done(((f32[512,8192]{1,0:T(8,128)}), f32[64,8192]{1,0:T(8,128)}) %reduce-scatter.2.cloned.1.call-update) | async-done | bytes 2097168 | tf_op jit(solution)/shard_map/reduce_scatter | solution.py:131
  228.7 1.7 convert.4
  230.4 1.0 fusion.8
  (4 shorter events, 0.0 us)
Async XLA Ops:
  7.2 68.8 %all-gather.6.cloned.1.call-start = ((), (), s32[]{:S(2)}) async-start(), calls=%async_computation.2 | async-start | bytes 4718592 | tf_op jit(solution)/shard_map/all_gather | solution.py:98
  7.9 76.4 %all-gather.8.cloned.1.call-start = ((), (), s32[]{:S(2)}) async-start(), calls=%async_computation.3 | async-start | bytes 4718592 | tf_op jit(solution)/shard_map/all_gather | solution.py:99
  8.6 220.1 %reduce-scatter.2.cloned.1.call-start = ((), (), s32[]{:S(2)}) async-start(), calls=%async_computation.1 | async-start | bytes 18874368 | tf_op jit(solution)/shard_map/reduce_scatter | solution.py:131
Sparse Core Ops, SparseCore 0:
  9.8 36.2 all-gather.5
  47.9 30.7 all-gather.7
  121.7 106.9 reduce-scatter.1

commit v2 on v1

--- a/solution.py
+++ b/solution.py
@@ -60,14 +60,15 @@
         ct_ref[k] = term
 
 
-def token_kernel(w_ref, c_ref, v_ref, u_ref, out_ref):
-    width = v_ref.shape[1]
-    for col in range(0, width, 512):
-        out_ref[:, col:col + 512] = sum(jnp.dot(w_ref[k], v_ref[:, col:col + 512], preferred_element_type=F32) for k in range(3))
-        out_ref[:, width + col:width + col + 512] = sum(jnp.dot(c_ref[k], u_ref[:, col:col + 512], preferred_element_type=F32) for k in range(3))
+def token_kernel(order_ref, w_m, c_m, v_m, u_m, w_o, c_o, v_o, u_o, mine_ref, other_ref):
+    half = v_m.shape[1]
+    for out, w, c, v, u in ((mine_ref, w_m, c_m, v_m, u_m), (other_ref, w_o, c_o, v_o, u_o)):
+        for col in range(0, half, 512):
+            out[:, col:col + 512] = sum(jnp.dot(w[k], v[:, col:col + 512], preferred_element_type=F32) for k in range(3))
+            out[:, half + col:half + col + 512] = sum(jnp.dot(c[k], u[:, col:col + 512], preferred_element_type=F32) for k in range(3))
 
 
-def row_kernel(block, req_ref, wt_ref, ct_ref, x_ref, dy_ref, du_ref, dv_ref, lhs):
+def row_kernel(block, req_ref, coef_ref, x_ref, out_ref, lhs):
     first = pl.program_id(0) * block
     rows = lax.broadcasted_iota(jnp.int32, (block, SLOTS), 0) + first
     for q in range(N_DEV):
@@ -75,13 +76,11 @@
         cols = slice(q * TOK, (q + 1) * TOK)
         half = slice((q % 2) * TOK, (q % 2 + 1) * TOK)
         for k in range(3):
-            for m, ref in enumerate((ct_ref, wt_ref)):
-                full = jnp.dot(pick, ref[k, (q // 2) * SLOTS:(q // 2 + 1) * SLOTS, :], preferred_element_type=F32)
-                lhs[m, k, :, cols] = full[:, half].astype(BF16)
+            full = jnp.dot(pick, coef_ref[k, (q // 2) * SLOTS:(q // 2 + 1) * SLOTS, :], preferred_element_type=F32)
+            lhs[k, :, cols] = full[:, half].astype(BF16)
     width = x_ref.shape[1]
     for col in range(0, width, 512):
-        du_ref[:, col:col + 512] = sum(jnp.dot(lhs[0, k], x_ref[:, col:col + 512], preferred_element_type=F32) for k in range(3)).astype(BF16)
-        dv_ref[:, col:col + 512] = sum(jnp.dot(lhs[1, k], dy_ref[:, col:col + 512], preferred_element_type=F32) for k in range(3)).astype(BF16)
+        out_ref[:, col:col + 512] = sum(jnp.dot(lhs[k], x_ref[:, col:col + 512], preferred_element_type=F32) for k in range(3)).astype(BF16)
 
 
 def solution(mesh):
@@ -118,30 +117,64 @@
             out_shape=[jax.ShapeDtypeStruct((3, n_tok, SLOTS), BF16)] * 2 + [jax.ShapeDtypeStruct((3, n_tok // pair * SLOTS, pair), BF16)] * 2,
             scratch_shapes=[pltpu.VMEM((SEL, pair), jnp.int32), pltpu.VMEM((SEL, pair), F32), pltpu.VMEM((SEL, pair), F32)],
         )(act.reshape(n_tok, SLOTS), slope.reshape(n_tok, SLOTS), slot_all, gate_all)
-        coef = pl.BlockSpec((3, TOK, SLOTS), lambda q: (0, q, 0))
-        table = pl.BlockSpec((None, SLOTS, width), lambda q: (q, 0, 0))
-        partial = pl.pallas_call(
+        core = owner % 2
+        chip = owner // 2
+        half = width // 2
+        masks = jnp.where(core == 0, jnp.array([0, 1, 2, 3]), jnp.array([0, 2, 1, 3]))
+        masks_other = jnp.where(core == 0, jnp.array([0, 2, 1, 3]), jnp.array([0, 1, 2, 3]))
+        order = jnp.stack([chip ^ masks, chip ^ masks_other, jnp.full((4,), core), jnp.full((4,), 1 - core)]).astype(jnp.int32)
+        coef_of = lambda m: pl.BlockSpec((3, TOK, SLOTS), lambda r, h, o: (0, o[m, r] * 2 + h, 0))
+        table_of = lambda m: pl.BlockSpec((None, SLOTS, half), lambda r, h, o: (o[m, r] * 2 + h, 0, o[2 + m, 0]))
+        out_blk = pl.BlockSpec((None, TOK, width), lambda r, h, o: (r, h, 0))
+        mine, other = pl.pallas_call(
             token_kernel,
-            grid=(N_DEV,),
-            in_specs=[coef, coef, table, table],
-            out_specs=pl.BlockSpec((TOK, 2 * width), lambda q: (q, 0)),
-            out_shape=jax.ShapeDtypeStruct((n_tok, 2 * width), F32),
+            grid_spec=pltpu.PrefetchScalarGridSpec(
+                num_scalar_prefetch=1,
+                grid=(4, 2),
+                in_specs=[coef_of(0), coef_of(0), table_of(0), table_of(0), coef_of(1), coef_of(1), table_of(1), table_of(1)],
+                out_specs=[out_blk, out_blk],
+            ),
+            out_shape=[jax.ShapeDtypeStruct((4, 2 * TOK, width), F32)] * 2,
             compiler_params=pltpu.CompilerParams(vmem_limit_bytes=VMEM_BYTES),
-        )(w_tok, c_tok, down_rows, up_rows)
-        token_out = lax.psum_scatter(partial, 'ep', scatter_dimension=0, tiled=True)
+        )(order, w_tok, c_tok, down_rows, up_rows, w_tok, c_tok, down_rows, up_rows)
+        partner = [(i, i ^ 1) for i in range(N_DEV)]
+        first_hop = [(i, i ^ (2 if i % 2 == 0 else 4)) for i in range(N_DEV)]
+        second_hop = [(i, i ^ (4 if i % 2 == 0 else 2)) for i in range(N_DEV)]
+        hop = lambda value, pairs: lax.ppermute(value, 'ep', pairs)
         block = 256
         whole = lambda *shape: pl.BlockSpec(shape, lambda i: (0,) * len(shape))
         rows_blk = pl.BlockSpec((block, width), lambda i: (i, 0))
-        grad_up, grad_down = pl.pallas_call(
-            functools.partial(row_kernel, block),
-            grid=(rows_owner // block,),
-            in_specs=[whole(N_DEV, SLOTS), whole(*w_tr.shape), whole(*c_tr.shape), whole(n_tok, width), whole(n_tok, width)],
-            out_specs=[rows_blk, rows_blk],
-            out_shape=[jax.ShapeDtypeStruct((rows_owner, width), BF16)] * 2,
-            scratch_shapes=[pltpu.VMEM((2, 3, block, n_tok), BF16)],
-            compiler_params=pltpu.CompilerParams(vmem_limit_bytes=VMEM_BYTES),
-            cost_estimate=pl.CostEstimate(flops=12 * rows_owner * width * n_tok, bytes_accessed=4 * rows_owner * width, transcendentals=0),
-        )(asked, w_tr, c_tr, x_all.reshape(n_tok, width), dy_all.reshape(n_tok, width))
-        return token_out[:, :width].astype(BF16), token_out[:, width:].astype(BF16), grad_up, grad_down
+
+        def grad_rows(coef, tok):
+            return pl.pallas_call(
+                functools.partial(row_kernel, block),
+                grid=(rows_owner // block,),
+                in_specs=[whole(N_DEV, SLOTS), whole(*coef.shape), whole(n_tok, width)],
+                out_specs=rows_blk,
+                out_shape=jax.ShapeDtypeStruct((rows_owner, width), BF16),
+                scratch_shapes=[pltpu.VMEM((3, block, n_tok), BF16)],
+                compiler_params=pltpu.CompilerParams(vmem_limit_bytes=VMEM_BYTES),
+                cost_estimate=pl.CostEstimate(flops=6 * rows_owner * width * n_tok, bytes_accessed=2 * rows_owner * width, transcendentals=0),
+            )(asked, coef, tok.reshape(n_tok, width))
+
+        pair_far = mine[3] + hop(other[3], partner)
+        pair_first = mine[1] + hop(other[1], partner)
+        got_second = hop(pair_far, first_hop)
+        got_own = hop(pair_first, first_hop)
+        pair_second = mine[2] + hop(other[2], partner)
+        pair_own = mine[0] + hop(other[0], partner)
+        grad_up = grad_rows(c_tr, x_all)
+        got_second, grad_up = lax.optimization_barrier((got_second, grad_up))
+        got_last = hop(pair_second + got_second, second_hop)
+        grad_down = grad_rows(w_tr, dy_all)
+        got_last, got_own, grad_down = lax.optimization_barrier((got_last, got_own, grad_down))
+        final = (pair_own + got_own + got_last).astype(BF16).reshape(2, TOK, 2, half)
+        keep = lax.dynamic_index_in_dim(final, core, 0, keepdims=False)
+        give = lax.dynamic_index_in_dim(final, 1 - core, 0, keepdims=False)
+        got = hop(give, partner)
+        low = jnp.where(core == 0, keep, got)
+        high = jnp.where(core == 0, got, keep)
+        token_out = jnp.concatenate([low, high], axis=2)
+        return token_out[:, 0], token_out[:, 1], grad_up, grad_down
 
     return jax.shard_map(per_device, mesh=mesh, in_specs=(tok_spec, tok_spec, tok_spec, tok_spec, tok_spec, table_spec, table_spec), out_specs=(tok_spec, tok_spec, tok_spec, tok_spec), check_vma=False)

time: 238 us -> 242 us (1.017)
  waiting for transfers between devices: 42.5 us -> 14.7 us
  other arithmetic: 5 us -> 19.3 us
  local copies, waits for them, and re-layouts: 48.1 us -> 56 us
  starting transfers between devices: 0.11 us -> 5.47 us
  Pallas kernels: 94.4 us -> 98.2 us
    reduce_scatter x1 -> x0, waiting for transfers between devices: 41.1 us -> none  [per_device(): token_out = lax.psum_scatter(partial, 'ep', scatter_dimension=0, tiled=True)]
    ppermute x0 -> x8, waiting for transfers between devices: none -> 13.3 us  [per_device(): hop = lambda value, pairs: lax.ppermute(value, 'ep', pairs)]
    add x0 -> x2, other arithmetic: none -> 10.7 us  [the longest x1 6.13 us: per_device(): pair_first = mine[1] + hop(other[1], partner)]
    squeeze x0 -> x1, local copies, waits for them, and re-layouts: none -> 7.07 us  [per_device(): pair_own = mine[0] + hop(other[0], partner)]
    ppermute x0 -> x8, starting transfers between devices: none -> 5.39 us  [per_device(): hop = lambda value, pairs: lax.ppermute(value, 'ep', pairs)]
    pallas_call x2 -> x3, Pallas kernels: 82.6 us -> 86.3 us  [the longest x2 69.1 us: grad_rows(): pl.pallas_call(functools.partial(row_kernel, block), grid=(rows_owner //...]
    convert_element_type x0 -> x1, other arithmetic: none -> 3.34 us  [per_device(): (pair_own + got_own + got_last).astype(BF16).reshape(2, TOK, 2, half)]
  transfers between devices with their start and end apart: 3 -> 10, of which waited for: 1 -> 5; matrix products, arithmetic and copies ran while one was open for 25% -> 29% of each run, Pallas kernels for 27% -> 29%
where the time goes in v2:
time: 242 us
  Pallas kernels  98.2 us (41%)
  local copies, waits for them, and re-layouts  56 us (23%)
  other arithmetic  19.3 us (8%)
  blocking collectives  17.3 us (7%)
  matrix products  16.6 us (7%)
  waiting for transfers between devices  14.7 us (6%)
  between operations  14.1 us (6%)
  starting transfers between devices  5.47 us (2%)
    pallas_call x2, Pallas kernels, grad_rows(): pl.pallas_call(functools.partial(row_kernel, block), grid=(rows_owner //...  69.1 us
    gather x1, local copies, waits for them, and re-layouts, per_device(): down_rows = down_local[asked]  23.2 us
    gather x1, local copies, waits for them, and re-layouts, per_device(): up_rows = up_local[asked]  23 us
    all_gather x1, blocking collectives, per_device(): small_all = lax.all_gather(small, 'ep', axis=0)  17.3 us
    pallas_call x1, Pallas kernels, per_device(): pl.pallas_call(token_kernel, grid_spec=pltpu.PrefetchScalarGridSpec(num_s...  17.2 us
    ppermute x8, waiting for transfers between devices, per_device(): hop = lambda value, pairs: lax.ppermute(value, 'ep', pairs)  13.3 us
    pallas_call x1, Pallas kernels, per_device(): pl.pallas_call(select_kernel, grid=(n_tok // pair,), in_specs=[blk] * 4,...  11.9 us
    dot_general x1, matrix products, per_device(): jnp.einsum('qtd,qrd->qtr', dy_all, down_rows, preferred_element_type=F32)  8.33 us
  transfers between devices with their start and end apart: 10, of which 5 were waited for; matrix products, arithmetic and copies ran while one was open for 29% of the time, Pallas kernels for 29%

profile of v2, /device:TPU:0, one launch (start us, length us, event | category | flops | bytes accessed | tf_op | source)
XLA Modules:
  0.0 241.8 jit_solution(16632099495781086051)
XLA Ops:
  7.2 0.0 all-gather.6.cloned.1.call-start
  7.2 0.7 all-gather.6.cloned.1.call-update
  7.9 0.0 all-gather.8.cloned.1.call-start
  7.9 0.7 all-gather.8.cloned.1.call-update
  8.7 0.1 pad.7.clone
  8.7 0.1 pad.8.clone
  8.8 0.8 convert_element_type.27
  9.7 0.8 copy.28
  10.5 1.0 pad_maximum_fusion.1
  11.4 0.1 copy.29
  11.5 17.3 %all-gather = f32[1088,128]{1,0:T(8,128)S(1)} all-gather(f32[136,128]{1,0:T(8,128)S(1)} %copy.29), channel_id=2, replica_groups=mesh['dp'=1,'ep'=8] {'ep'}, dimensions={0}, use_global_device_ids=true | all-gather | bytes 626688 | tf_op jit(solution)/shard_map/all_gather | solution.py:96
  28.9 23.2 %gather_fusion.1 = bf16[1024,4096]{1,0:T(8,128)(2,1)} fusion(bf16[2048,4096]{1,0:T(8,128)(2,1)} %param.17, s32[1024]{0:T(1024)S(1)} %fusion.13), kind=kCustom, calls=%fused_computation.1 | custom fusion | bytes 16781312 | tf_op jit(solution)/shard_map/gather | solution.py:103
  52.1 23.0 %gather_fusion = bf16[1024,4096]{1,0:T(8,128)(2,1)} fusion(bf16[2048,4096]{1,0:T(8,128)(2,1)} %param.16, s32[1024]{0:T(1024)S(1)} %fusion.13), kind=kCustom, calls=%fused_computation | custom fusion | bytes 16781312 | tf_op jit(solution)/shard_map/gather | solution.py:102
  75.1 0.0 copy-done
  75.1 0.6 add_add_fusion.order_ref
  75.8 0.8 fusion.19
  76.6 8.3 %fusion.18 = (f32[8,64,128]{2,1,0:T(8,128)}, f32[8,64,128]{2,1,0:T(8,128)S(1)}) fusion(bf16[8,128,4096]{2,1,0:T(8,128)(2,1)} %bitcast.75, bf16[8,64,4096]{2,1,0:T(8,128)(2,1)} %bitcast.79), kind=kOutput, calls=%fused_computation.49 | convolution fusion | flops 537133056 | bytes 13107200 | tf_op jit(solution)/shard_map/qtd,qrd->qtr/dot_general | solution.py:104
  84.9 8.3 %fusion.4 = f32[8,64,128]{2,1,0:T(8,128)} fusion(bf16[8,128,4096]{2,1,0:T(8,128)(2,1)} %bitcast.72, bf16[8,64,4096]{2,1,0:T(8,128)(2,1)} %bitcast.78, f32[8,64,128]{2,1,0:T(8,128)S(1)} %get-tuple-element.43), kind=kOutput, calls=%fused_computation.16 | convolution fusion | flops 537460736 | bytes 13107200 | tf_op jit(solution)/shard_map/qtd,qrd->qtr/dot_general | solution.py:105
  93.2 11.9 %shard_map.138 = (bf16[3,512,128]{2,1,0:T(8,128)(2,1)}, bf16[3,512,128]{2,1,0:T(8,128)(2,1)}, bf16[3,512,128]{2,1,0:T(8,128)(2,1)}, bf16[3,512,128]{2,1,0:T(8,128)(2,1)}) custom-call(f32[512,128]{1,0:T(8,128)} %bitcast.82, f32[512,128]{1,0:T(8,128)} %bitcast.83, s32[512,128]{1,0:T(8,128)} %bitcast.85, f32[512,128]{1,0:T(8,128)} %bitcast.84), custom_call_target="tpu_custom_call" | custom-call | tf_op jit(solution)/shard_map/pallas_call | solution.py:112
  105.1 17.2 %shard_map.139 = (f32[4,128,4096]{2,1,0:T(8,128)}, f32[4,128,4096]{2,1,0:T(8,128)}) custom-call(s32[4,4]{1,0:T(4,128)} %add_add_fusion.order_ref, bf16[3,512,128]{2,1,0:T(8,128)(2,1)} %get-tuple-element.15.w_m.w_o, bf16[3,512,128]{2,1,0:T(8,128)(2,1)} %get-tuple-element.16.c_m.c_o, bf16[8,128,4096]{2,1,0:T(8,128)(2,1)} %bitcast.73, ...), custom_call_target="tpu_custom_call" | custom-call | tf_op jit(solution)/shard_map/pallas_call | solution.py:129
  122.3 7.1 %slice_bitcast_fusion.3 = (f32[128,4096]{1,0:T(8,128)}, f32[128,4096]{1,0:T(8,128)}, f32[128,4096]{1,0:T(8,128)}, f32[128,4096]{1,0:T(8,128)}) fusion(f32[4,128,4096]{2,1,0:T(8,128)} %get-tuple-element.18), kind=kLoop, calls=%fused_computation.13 | loop fusion | bytes 16777216 | tf_op jit(solution)/shard_map/squeeze | solution.py:165
  129.4 0.0 collective-permute-start.5
  129.4 0.5 collective-permute-start.2
  129.9 0.6 convert_bitcast_fusion.1.req_ref
  130.5 0.0 collective-permute-start
  130.5 0.5 collective-permute-start.1
  131.0 2.5 %collective-permute-done.5 = f32[128,4096]{1,0:T(8,128)} collective-permute-done((f32[128,4096]{1,0:T(8,128)}, f32[128,4096]{1,0:T(8,128)}, u32[]{:S(2)}, u32[]{:S(2)}) %collective-permute-start.5) | collective-permute-done | bytes 2097184 | tf_op jit(solution)/shard_map/ppermute | solution.py:143
  133.5 3.0 %collective-permute-done.2 = f32[128,4096]{1,0:T(8,128)} collective-permute-done((f32[128,4096]{1,0:T(8,128)}, f32[128,4096]{1,0:T(8,128)}, u32[]{:S(2)}, u32[]{:S(2)}) %collective-permute-start.2) | collective-permute-done | bytes 2097184 | tf_op jit(solution)/shard_map/ppermute | solution.py:143
  136.5 6.1 %bitcast_add_fusion = (f32[128,4096]{1,0:T(8,128)}, f32[128,4096]{1,0:T(8,128)}) fusion(f32[128,4096]{1,0:T(8,128)} %collective-permute-done.5, f32[4,128,4096]{2,1,0:T(8,128)} %get-tuple-element.17, f32[128,4096]{1,0:T(8,128)} %collective-permute-done.2), kind=kLoop, calls=%fused_computation.2 | loop fusion | flops 1048576 | bytes 12582912 | tf_op jit(solution)/shard_map/add | solution.py:161
  142.6 1.4 collective-permute-start.3
  144.1 34.6 %shard_map.140 = bf16[2048,4096]{1,0:T(8,128)(2,1)} custom-call(s32[8,128]{1,0:T(8,128)} %convert_bitcast_fusion.1.req_ref, bf16[3,512,128]{2,1,0:T(8,128)(2,1)} %get-tuple-element.19.coef_ref, bf16[512,4096]{1,0:T(8,128)(2,1)} %all-gather.6.cloned.1.call-done.x_ref), custom_call_target="tpu_custom_call" | custom-call | flops 25769803776 | bytes 16777216 | tf_op jit(solution)/shard_map/pallas_call | solution.py:149
  178.6 0.6 collective-permute-start.6
  179.2 0.0 collective-permute-done.3
  179.2 0.0 collective-permute-done.1
  179.2 4.5 %fusion = f32[128,4096]{1,0:T(8,128)} fusion(f32[128,4096]{1,0:T(8,128)} %collective-permute-done.3, f32[128,4096]{1,0:T(8,128)} %collective-permute-done.1, f32[4,128,4096]{2,1,0:T(8,128)} %get-tuple-element.17), kind=kLoop, calls=%fused_computation.5 | loop fusion | flops 1048576 | bytes 8388608 | tf_op jit(solution)/shard_map/add | solution.py:168
  183.7 1.1 collective-permute-start.4
  184.8 34.6 %shard_map.141 = bf16[2048,4096]{1,0:T(8,128)(2,1)} custom-call(s32[8,128]{1,0:T(8,128)} %convert_bitcast_fusion.1.req_ref, bf16[3,512,128]{2,1,0:T(8,128)(2,1)} %get-tuple-element.21.coef_ref, bf16[512,4096]{1,0:T(8,128)(2,1)} %all-gather.8.cloned.1.call-done.x_ref), custom_call_target="tpu_custom_call" | custom-call | flops 25769803776 | bytes 16777216 | tf_op jit(solution)/shard_map/pallas_call | solution.py:149
  219.4 4.0 %collective-permute-done.6 = f32[128,4096]{1,0:T(8,128)} collective-permute-done((f32[128,4096]{1,0:T(8,128)}, f32[128,4096]{1,0:T(8,128)}, u32[]{:S(2)}, u32[]{:S(2)}) %collective-permute-start.6) | collective-permute-done | bytes 2097184 | tf_op jit(solution)/shard_map/ppermute | solution.py:143
  223.4 2.4 collective-permute-done.4
  225.7 0.0 collective-permute-done
  225.7 3.3 %fusion.3 = bf16[128,4096]{1,0:T(8,128)(2,1)S(1)} fusion(f32[128,4096]{1,0:T(8,128)} %collective-permute-done.4, f32[128,4096]{1,0:T(8,128)} %collective-permute-done.6, f32[128,4096]{1,0:T(8,128)S(1)} %collective-permute-done, f32[4,128,4096]{2,1,0:T(8,128)} %get-tuple-element.17), kind=kLoop, calls=%fused_computation.9 | loop fusion | flops 2097152 | bytes 9437184 | tf_op jit(solution)/shard_map/convert_element_type | solution.py:171
  229.1 0.8 reshape.63
  229.9 0.7 constant_dynamic-slice_fusion.1
  230.6 0.2 copy.38
  230.8 1.3 collective-permute-start.7
  232.0 1.5 collective-permute-done.7
  233.6 0.4 bitcast_select_fusion
  233.9 1.0 fusion.7
  (8 shorter events, 0.0 us)
Async XLA Ops:
  7.2 69.4 %all-gather.6.cloned.1.call-start = ((), (), s32[]{:S(2)}) async-start(), calls=%async_computation | async-start | bytes 4718592 | tf_op jit(solution)/shard_map/all_gather | solution.py:97
  7.9 77.0 %all-gather.8.cloned.1.call-start = ((), (), s32[]{:S(2)}) async-start(), calls=%async_computation.1 | async-start | bytes 4718592 | tf_op jit(solution)/shard_map/all_gather | solution.py:98
  52.1 23.0 %copy-start = (s32[4]{0:T(128)S(1)}, s32[4]{0:T(128)}, u32[]{:S(2)}) copy-start(s32[4]{0:T(128)} %constant.60.clone) | copy-start | bytes 52
  129.4 4.1 %collective-permute-start.5 = (f32[128,4096]{1,0:T(8,128)}, f32[128,4096]{1,0:T(8,128)}, u32[]{:S(2)}, u32[]{:S(2)}) collective-permute-start(f32[128,4096]{1,0:T(8,128)} %get-tuple-element.27), channel_id=1, source_target_pairs={{0,1},{1,0},{2,3},{3,2},{4,5},{5,4},{6,7},{7,6}} | collective-permute-start | bytes 6291464 | tf_op jit(solution)/shard_map/ppermute | solution.py:143
  129.4 7.1 %collective-permute-start.2 = (f32[128,4096]{1,0:T(8,128)}, f32[128,4096]{1,0:T(8,128)}, u32[]{:S(2)}, u32[]{:S(2)}) collective-permute-start(f32[128,4096]{1,0:T(8,128)} %get-tuple-element.28), channel_id=1, source_target_pairs={{0,1},{1,0},{2,3},{3,2},{4,5},{5,4},{6,7},{7,6}} | collective-permute-start | bytes 6291464 | tf_op jit(solution)/shard_map/ppermute | solution.py:143
  130.5 95.2 %collective-permute-start = (f32[128,4096]{1,0:T(8,128)}, f32[128,4096]{1,0:T(8,128)S(1)}, u32[]{:S(2)}, u32[]{:S(2)}) collective-permute-start(f32[128,4096]{1,0:T(8,128)} %get-tuple-element.26), channel_id=1, source_target_pairs={{0,1},{1,0},{2,3},{3,2},{4,5},{5,4},{6,7},{7,6}} | collective-permute-start | bytes 6291464 | tf_op jit(solution)/shard_map/ppermute | solution.py:143
  130.5 48.7 %collective-permute-start.1 = (f32[128,4096]{1,0:T(8,128)}, f32[128,4096]{1,0:T(8,128)}, u32[]{:S(2)}, u32[]{:S(2)}) collective-permute-start(f32[128,4096]{1,0:T(8,128)} %get-tuple-element.29), channel_id=1, source_target_pairs={{0,1},{1,0},{2,3},{3,2},{4,5},{5,4},{6,7},{7,6}} | collective-permute-start | bytes 6291464 | tf_op jit(solution)/shard_map/ppermute | solution.py:143
  142.6 36.6 %collective-permute-start.3 = (f32[128,4096]{1,0:T(8,128)}, f32[128,4096]{1,0:T(8,128)}, u32[]{:S(2)}, u32[]{:S(2)}) collective-permute-start(f32[128,4096]{1,0:T(8,128)} %get-tuple-element.31), channel_id=1, source_target_pairs={{0,2},{1,5},{2,0},{3,7},{4,6},{5,1},{6,4},{7,3}} | collective-permute-start | bytes 6291464 | tf_op jit(solution)/shard_map/ppermute | solution.py:143
  178.6 44.7 %collective-permute-start.6 = (f32[128,4096]{1,0:T(8,128)}, f32[128,4096]{1,0:T(8,128)}, u32[]{:S(2)}, u32[]{:S(2)}) collective-permute-start(f32[128,4096]{1,0:T(8,128)} %get-tuple-element.30), channel_id=1, source_target_pairs={{0,2},{1,5},{2,0},{3,7},{4,6},{5,1},{6,4},{7,3}} | collective-permute-start | bytes 6291464 | tf_op jit(solution)/shard_map/ppermute | solution.py:143
  183.7 42.0 %collective-permute-start.4 = (f32[128,4096]{1,0:T(8,128)}, f32[128,4096]{1,0:T(8,128)}, u32[]{:S(2)}, u32[]{:S(2)}) collective-permute-start(f32[128,4096]{1,0:T(8,128)} %fusion), channel_id=1, source_target_pairs={{0,4},{1,3},{2,6},{3,1},{4,0},{5,7},{6,2},{7,5}} | collective-permute-start | bytes 6291464 | tf_op jit(solution)/shard_map/ppermute | solution.py:143
  230.8 2.8 %collective-permute-start.7 = (bf16[64,2,2048]{2,0,1:T(8,128)(2,1)S(1)}, bf16[64,2,2048]{2,0,1:T(8,128)(2,1)S(1)}, u32[]{:S(2)}, u32[]{:S(2)}) collective-permute-start(bf16[64,2,2048]{2,0,1:T(8,128)(2,1)S(1)} %bitcast.86), channel_id=1, source_target_pairs={{0,1},{1,0},{2,3},{3,2},{4,5},{5,4},{6,7},{7,6}} | collective-permute-start | bytes 1572872 | tf_op jit(solution)/shard_map/ppermute | solution.py:143
Sparse Core Ops, SparseCore 0:
  9.8 36.3 all-gather.5
  48.0 30.7 all-gather.7

commit v3 on v0

v3 whole, which is shorter than its diff:
```python
import functools
import math
import jax
import jax.numpy as jnp
from jax import lax
from jax.experimental import pallas as pl
from jax.experimental.pallas import tpu as pltpu
from jax.sharding import PartitionSpec as P

F32, BF16, I32 = jnp.float32, jnp.bfloat16, jnp.int32
N_DEV, TOK, SLOTS, SEL = 8, 64, 128, 128
PAIR = 2 * TOK
TERMS = 3
CHUNK = 1024
LANES = 128
PAD = 8
VMEM_BYTES = 62 * 1024 * 1024
MESH = pl.DeviceIdType.MESH


def gelu_pair(pre_act):
    normal_cdf = 0.5 * (1.0 + lax.erf(pre_act * (2.0 ** -0.5)))
    normal_pdf = jnp.exp(-0.5 * pre_act * pre_act) * ((2.0 * math.pi) ** -0.5)
    return pre_act * normal_cdf, normal_cdf + pre_act * normal_pdf


def split3(wide):
    high = wide.astype(BF16)
    rest = wide - high.astype(F32)
    mid = rest.astype(BF16)
    low = (rest - mid.astype(F32)).astype(BF16)
    return high, mid, low


def share_kernel(x_ref, dy_ref, slot_ref, gate_ref, req_ref, up_ref, down_ref,
                 x_all, dy_all, slot_all, gate_all, up_rows, down_rows, asked_out,
                 asked, asked_s, table, wide, picked, staged,
                 send_sem, recv_sem, own_sem, smem_sem, in_sem, out_sem):
    me = lax.axis_index("ep")
    n_rows, width = up_ref.shape
    n_ask = N_DEV * SLOTS
    steps = [(ref, out, col) for ref, out in ((up_ref, up_rows), (down_ref, down_rows)) for col in range(0, width, CHUNK)]

    def fetch(k):
        ref, _, col = steps[k]
        return pltpu.make_async_copy(ref.at[:, pl.ds(col, CHUNK)], table.at[k % 2], in_sem.at[k % 2])

    fetch(0).start()
    fetch(1).start()
    barrier = pltpu.get_barrier_semaphore()
    for b in range(1, N_DEV):
        pl.semaphore_signal(barrier, inc=1, device_id={"ep": me ^ b}, device_id_type=MESH)
    pl.semaphore_wait(barrier, N_DEV - 1)

    count = [0]
    sent = []

    def push(src, dst, mask):
        k = count[0]
        count[0] += 1
        copy = pltpu.make_async_remote_copy(src_ref=src, dst_ref=dst, send_sem=send_sem.at[k], recv_sem=recv_sem.at[k],
                                            device_id={"ep": me ^ mask}, device_id_type=MESH)
        copy.start()
        sent.append(copy)
        return copy

    asks = [push(req_ref.at[0, pl.ds(me ^ b, 1)], asked.at[pl.ds(b, 1)], b) for b in range(1, N_DEV)]
    first = [
        push(gate_ref, gate_all.at[4], 4), push(slot_ref, slot_all.at[2], 2),
        push(x_ref, x_all.at[4], 4), push(dy_ref, dy_all.at[2], 2),
    ]
    near = [push(gate_ref, gate_all.at[1], 1), push(slot_ref, slot_all.at[1], 1), push(x_ref, x_all.at[1], 1), push(dy_ref, dy_all.at[1], 1)]
    low, top = pl.ds(0, TOK // 2), pl.ds(TOK // 2, TOK // 2)
    second = [
        push(gate_ref, gate_all.at[2], 2), push(slot_ref, slot_all.at[4], 4),
        push(x_ref.at[low], x_all.at[2, low], 2), push(dy_ref.at[low], dy_all.at[4, low], 4),
    ]
    own = [pltpu.make_async_copy(src, dst.at[0], own_sem.at[k]) for k, (src, dst) in enumerate(((x_ref, x_all), (dy_ref, dy_all), (slot_ref, slot_all), (gate_ref, gate_all)))]
    for copy in own:
        copy.start()

    asked[pl.ds(0, 1), :] = req_ref[0, pl.ds(me, 1), :]
    for copy in asks:
        copy.wait_recv()
    asked_out[...] = asked[...]
    to_smem = pltpu.make_async_copy(asked, asked_s, smem_sem)
    to_smem.start()
    to_smem.wait()

    tiles = CHUNK // LANES
    wide_step, pick_step = n_rows + PAD, n_ask + PAD

    def gather(k):
        fetch(k).wait()

        def fill(t, _):
            r = pl.multiple_of(t * 32, 32)
            for j in range(tiles):
                wide[pl.ds(j * wide_step + r, 32), :] = table[k % 2, pl.ds(r, 32), j * LANES:(j + 1) * LANES].astype(F32)
            return 0

        lax.fori_loop(0, n_rows // 32, fill, 0)
        if k + 2 < len(steps):
            fetch(k + 2).start()

        def pick(t, _):
            for u in range(16):
                r = t * 16 + u
                row = asked_s[r // SLOTS, r % SLOTS]
                picked[pl.ds(r, tiles, stride=pick_step), :] = wide[pl.ds(row, tiles, stride=wide_step), :]
            return 0

        lax.fori_loop(0, n_ask // 16, pick, 0)
        if k >= 2:
            drain_copy(k - 2).wait()

        def drain(t, _):
            r = pl.multiple_of(t * 32, 32)
            for j in range(tiles):
                staged[k % 2, pl.ds(r, 32), j * LANES:(j + 1) * LANES] = picked[pl.ds(j * pick_step + r, 32), :].astype(BF16)
            return 0

        lax.fori_loop(0, n_ask // 32, drain, 0)
        drain_copy(k).start()

    def drain_copy(k):
        _, out, col = steps[k]
        return pltpu.make_async_copy(staged.at[k % 2], out.at[:, pl.ds(col, CHUNK)], out_sem.at[k % 2])

    for k in range(4):
        gather(k)
    for copy in first:
        copy.wait_recv()
    far = [
        push(gate_all.at[4], gate_all.at[6], 2), push(slot_all.at[2], slot_all.at[6], 4),
        push(x_all.at[4], x_all.at[6], 2), push(dy_all.at[2], dy_all.at[6], 4),
    ]
    second += [push(x_ref.at[top], x_all.at[2, top], 2), push(dy_ref.at[top], dy_all.at[4, top], 4)]
    near += [push(gate_all.at[4], gate_all.at[5], 1), push(slot_all.at[2], slot_all.at[3], 1), push(x_all.at[4], x_all.at[5], 1), push(dy_all.at[2], dy_all.at[3], 1)]
    for k in range(4, len(steps)):
        gather(k)
    for copy in far:
        copy.wait_recv()
    near += [push(ref.at[6], ref.at[7], 1) for ref in (gate_all, slot_all, x_all, dy_all)]
    for copy in second:
        copy.wait_recv()
    near += [push(gate_all.at[2], gate_all.at[3], 1), push(slot_all.at[4], slot_all.at[5], 1), push(x_all.at[2], x_all.at[3], 1), push(dy_all.at[4], dy_all.at[5], 1)]
    for copy in near:
        copy.wait_recv()
    for copy in sent:
        copy.wait_send()
    for copy in own:
        copy.wait()
    drain_copy(len(steps) - 2).wait()
    drain_copy(len(steps) - 1).wait()


N_COPIES = 7 + 4 + 4 + 4 + 4 + 2 + 4 + 4 + 4


def block_kernel(core_ref, x_ref, dy_ref, slot_ref, gate_ref, up_ref, down_ref, mine_ref, other_ref, wt_ref, ct_ref, slot_t, w_t, c_t):
    owner = lax.axis_index("ep")
    width = x_ref.shape[2]
    half = width // 2
    dims = (((1,), (1,)), ((), ()))
    up, down = up_ref, down_ref

    def dots(tok, rows):
        full = lax.dot_general(tok.reshape(PAIR, width), rows, dims, preferred_element_type=F32)
        return jnp.concatenate([full[:TOK, :SLOTS], full[TOK:, SLOTS:]], axis=0)

    act, slope = gelu_pair(dots(x_ref[...], up[...]))
    slope = slope * dots(dy_ref[...], down[...])
    local = slot_ref[...].reshape(PAIR, SEL) - owner * SLOTS
    valid = (local >= 0) & (local < SLOTS)
    index = jnp.where(valid, local, 0)
    act = jnp.take_along_axis(act, index, axis=1)
    slope = jnp.take_along_axis(slope, index, axis=1)
    gate = gate_ref[...].reshape(PAIR, SEL)
    w_t[...] = jnp.where(valid, (gate * act).astype(BF16).astype(F32), 0.0).T
    c_t[...] = jnp.where(valid, (gate * slope).astype(BF16).astype(F32), 0.0).T
    slot_t[...] = jnp.where(valid, local, -1).T
    rows = lax.broadcasted_iota(I32, (SLOTS, PAIR), 0)

    def step(s, acc):
        acc_w, acc_c = acc
        hit = rows == slot_t[pl.ds(s, 1), :]
        acc_w += jnp.where(hit, w_t[pl.ds(s, 1), :], 0.0)
        acc_c += jnp.where(hit, c_t[pl.ds(s, 1), :], 0.0)
        return acc_w, acc_c

    zero = jnp.zeros((SLOTS, PAIR), F32)
    acc_w, acc_c = lax.fori_loop(0, SEL, step, (zero, zero), unroll=4)
    for ref, acc in ((wt_ref, acc_w), (ct_ref, acc_c)):
        for k, term in enumerate(split3(acc)[:TERMS]):
            ref[k] = term
    first_half = lax.broadcasted_iota(I32, (PAIR, 2 * SLOTS), 0) < TOK
    first_cols = lax.broadcasted_iota(I32, (PAIR, 2 * SLOTS), 1) < SLOTS

    def spread(acc):
        both = jnp.concatenate([acc.T, acc.T], axis=1)
        return split3(jnp.where(first_half == first_cols, both, 0.0))

    w_terms, c_terms = spread(acc_w), spread(acc_c)
    core = core_ref[0]
    for col in range(0, half, 512):
        for shift, terms, table in ((0, w_terms, down), (half, c_terms, up)):
            here = pl.ds(pl.multiple_of(core * half + col, 512), 512)
            there = pl.ds(pl.multiple_of((1 - core) * half + col, 512), 512)
            dst = slice(shift + col, shift + col + 512)
            mine_ref[:, dst] = sum(jnp.dot(term, table[:, here], preferred_element_type=F32) for term in terms)
            part = sum(jnp.dot(term, table[:, there], preferred_element_type=F32) for term in terms)
            other_ref[:TOK, dst] = part[TOK:]
            other_ref[TOK:, dst] = part[:TOK]


def row_kernel(block, req_ref, near_ref, far_ref, x_ref, out_ref, lhs):
    first = pl.program_id(0) * block
    rows = lax.broadcasted_iota(I32, (block, SLOTS), 0) + first
    chips = [near_ref.at[2], near_ref.at[0], near_ref.at[1], far_ref.at[0]]
    for q in range(N_DEV):
        pick = jnp.where(rows == req_ref[pl.ds(q, 1), :], 1.0, 0.0).astype(BF16)
        cols = slice(q * TOK, (q + 1) * TOK)
        half = slice((q % 2) * TOK, (q % 2 + 1) * TOK)
        for k in range(TERMS):
            full = jnp.dot(pick, chips[q // 2][k], preferred_element_type=F32)
            lhs[k, :, cols] = full[:, half].astype(BF16)
    width = x_ref.shape[1]
    for col in range(0, width, 512):
        out_ref[:, col:col + 512] = sum(jnp.dot(lhs[k], x_ref[:, col:col + 512], preferred_element_type=F32) for k in range(TERMS)).astype(BF16)


def solution(mesh):
    tok_spec = P(('dp', 'ep'))
    table_spec = P('ep')

    def per_device(tokens, slot_ids, request_rows, gate_vals, grad_out, up_local, down_local):
        width = tokens.shape[1]
        rows_owner = up_local.shape[0]
        n_tok = N_DEV * TOK
        half = width // 2
        core = lax.axis_index('ep') % 2
        vmem, anyw = pl.BlockSpec(memory_space=pltpu.VMEM), pl.BlockSpec(memory_space=pl.ANY)
        shape = jax.ShapeDtypeStruct
        x_all, dy_all, slot_all, gate_all, up_rows, down_rows, asked = pl.pallas_call(
            share_kernel,
            in_specs=[vmem] * 5 + [anyw] * 2,
            out_specs=[anyw] * 6 + [vmem],
            out_shape=[shape((N_DEV, TOK, width), BF16)] * 2 + [shape((N_DEV, TOK, SEL), I32), shape((N_DEV, TOK, SEL), F32)]
            + [shape((N_DEV * SLOTS, width), BF16)] * 2 + [shape((N_DEV, SLOTS), I32)],
            scratch_shapes=[
                pltpu.VMEM((N_DEV, SLOTS), I32), pltpu.SMEM((N_DEV, SLOTS), I32),
                pltpu.VMEM((2, rows_owner, CHUNK), BF16),
                pltpu.VMEM((CHUNK // LANES * (rows_owner + PAD), LANES), F32),
                pltpu.VMEM((CHUNK // LANES * (N_DEV * SLOTS + PAD), LANES), F32),
                pltpu.VMEM((2, N_DEV * SLOTS, CHUNK), BF16),
                pltpu.SemaphoreType.DMA((N_COPIES,)), pltpu.SemaphoreType.DMA((N_COPIES,)),
                pltpu.SemaphoreType.DMA((4,)), pltpu.SemaphoreType.DMA,
                pltpu.SemaphoreType.DMA((2,)), pltpu.SemaphoreType.DMA((2,)),
            ],
            compiler_params=pltpu.CompilerParams(collective_id=0, has_side_effects=True, vmem_limit_bytes=VMEM_BYTES),
        )(tokens, grad_out, slot_ids.reshape(TOK, SEL), gate_vals.reshape(TOK, SEL), request_rows, up_local, down_local)

        core_arr = core.reshape(1).astype(I32)

        def blocks(n, chip, mine_at, other_at):
            tok = pl.BlockSpec((2, TOK, width), lambda i, c: (chip(i), 0, 0))
            side = pl.BlockSpec((2, TOK, SEL), lambda i, c: (chip(i), 0, 0))
            table = pl.BlockSpec((2 * SLOTS, width), lambda i, c: (chip(i), 0))
            coef = pl.BlockSpec((None, TERMS, SLOTS, PAIR), lambda i, c: (i, 0, 0, 0))
            return pl.pallas_call(
                block_kernel,
                grid_spec=pltpu.PrefetchScalarGridSpec(
                    num_scalar_prefetch=1,
                    grid=(n,),
                    in_specs=[tok, tok, side, side, table, table],
                    out_specs=[pl.BlockSpec((None, PAIR, width), lambda i, c: (mine_at(i, c[0]), 0, 0)),
                               pl.BlockSpec((None, PAIR, width), lambda i, c: (other_at(i, c[0]), 0, 0)), coef, coef],
                    scratch_shapes=[pltpu.VMEM((SEL, PAIR), I32), pltpu.VMEM((SEL, PAIR), F32), pltpu.VMEM((SEL, PAIR), F32)],
                ),
                out_shape=[shape((n, PAIR, width), F32)] * 2 + [shape((n, TERMS, SLOTS, PAIR), BF16)] * 2,
                compiler_params=pltpu.CompilerParams(vmem_limit_bytes=VMEM_BYTES),
                cost_estimate=pl.CostEstimate(flops=n * 10 ** 10, bytes_accessed=10 ** 6, transcendentals=0),
            )(core_arr, x_all, dy_all, slot_all, gate_all, up_rows, down_rows)

        def near_slot(i, c):
            return jnp.where(i == 2, 2, i ^ c)

        mine_far, other_far, w_far, c_far = blocks(1, lambda i: i + 3, lambda i, c: i, lambda i, c: i)
        mine, other, w_near, c_near = blocks(3, lambda i: lax.rem(i + 1, 3), near_slot, lambda i, c: near_slot(i, 1 - c))
        partner = [(i, i ^ 1) for i in range(N_DEV)]
        first_hop = [(i, i ^ (2 if i % 2 == 0 else 4)) for i in range(N_DEV)]
        second_hop = [(i, i ^ (4 if i % 2 == 0 else 2)) for i in range(N_DEV)]
        hop = lambda value, pairs: lax.ppermute(value, 'ep', pairs)
        block = 256
        whole = lambda *dims: pl.BlockSpec(dims, lambda i: (0,) * len(dims))

        def grad_rows(coef_near, coef_far, tok):
            return pl.pallas_call(
                functools.partial(row_kernel, block),
                grid=(rows_owner // block,),
                in_specs=[whole(N_DEV, SLOTS), whole(*coef_near.shape), whole(*coef_far.shape), whole(n_tok, width)],
                out_specs=pl.BlockSpec((block, width), lambda i: (i, 0)),
                out_shape=shape((rows_owner, width), BF16),
                scratch_shapes=[pltpu.VMEM((TERMS, block, n_tok), BF16)],
                compiler_params=pltpu.CompilerParams(vmem_limit_bytes=VMEM_BYTES),
                cost_estimate=pl.CostEstimate(flops=6 * rows_owner * width * n_tok, bytes_accessed=2 * rows_owner * width, transcendentals=0),
            )(asked, coef_near, coef_far, tok.reshape(n_tok, width))

        got_far = hop(other_far, partner)
        got_far, mine = lax.optimization_barrier((got_far, mine))
        got_second = hop(mine_far[0] + got_far[0], first_hop)
        got = hop(other, partner)
        got_own = hop(mine[0] + got[0], first_hop)
        grad_up = grad_rows(c_near, c_far, x_all)
        got_second, grad_up = lax.optimization_barrier((got_second, grad_up))
        got_last = hop(mine[1] + got[1] + got_second, second_hop)
        grad_down = grad_rows(w_near, w_far, dy_all)
        got_last, got_own, grad_down = lax.optimization_barrier((got_last, got_own, grad_down))
        final = (mine[2] + got[2] + got_own + got_last).astype(BF16).reshape(2, TOK, 2, half)
        keep, give = final[0], final[1]
        back = hop(give, partner)
        low = jnp.where(core == 0, keep, back)
        high = jnp.where(core == 0, back, keep)
        token_out = jnp.concatenate([low, high], axis=2)
        return token_out[:, 0], token_out[:, 1], grad_up, grad_down

    return jax.shard_map(per_device, mesh=mesh, in_specs=(tok_spec, tok_spec, tok_spec, tok_spec, tok_spec, table_spec, table_spec), out_specs=(tok_spec, tok_spec, tok_spec, tok_spec), check_vma=False)
```

time: 1500 us -> 227 us (0.15)
  other arithmetic: 719 us -> 16.6 us
  local copies, waits for them, and re-layouts: 333 us -> 3.18 us
  waiting for transfers between devices: 288 us -> 11.9 us
  Pallas kernels: 0 us -> 189 us
  matrix products: 120 us -> 0 us
    scatter-add x10 -> x0, other arithmetic: 571 us -> none  [the longest x4 248 us: scan_step(): acc_down = acc_down.at[flat_slots].add(down_part.reshape(-1, width))]
    gather x10 -> x0, local copies, waits for them, and re-layouts: 311 us -> none  [the longest x4 133 us: scan_step(): up_rows = up_table[slot_blk]]
    all_to_all x4 -> x0, waiting for transfers between devices: 288 us -> none  [the longest x1 93.5 us: per_device(): lax.all_to_all(up_local[asked_rows], 'ep', 0, 0, tiled=True)]
    pallas_call x0 -> x5, Pallas kernels: none -> 189 us  [the longest x1 87.3 us: per_device(): pl.pallas_call(share_kernel, in_specs=[vmem] * 5 + [anyw] * 2, out_specs=...]
    dot_general x16 -> x0, matrix products: 120 us -> none  [the longest x4 46.1 us: scan_step(): jnp.einsum('bsd,bd->bs', up_rows, x_blk, preferred_element_type=jnp.float32)]
    mul x8 -> x0, other arithmetic: 88.1 us -> none  [scan_step(): down_part = w_out.astype(jnp.float32)[:, :, None] * dy_blk[:, None, :]]
    convert_element_type x8 -> x1, other arithmetic: 56.5 us -> 3.96 us  [per_device(): (mine[2] + got[2] + got_own + got_last).astype(BF16)]
    broadcast_in_dim x2 -> x0, local copies, waits for them, and re-layouts: 16.5 us -> none  [local_layer(): zero_acc = jnp.zeros((n_slots, width), jnp.float32)]
  transfers between devices with their start and end apart: 4 -> 6, of which waited for: 4 -> 4; matrix products, arithmetic and copies ran while one was open for 6% -> 3% of each run, Pallas kernels for 0% -> 35%
where the time goes in v3:
time: 227 us; the launch traced here: 226 us
  Pallas kernels  189 us (83%)
  other arithmetic  16.6 us (7%)
  waiting for transfers between devices  11.9 us (5%)
  starting transfers between devices  4.94 us (2%)
  local copies, waits for them, and re-layouts  3.18 us (1%)
    pallas_call x1, Pallas kernels, per_device(): pl.pallas_call(share_kernel, in_specs=[vmem] * 5 + [anyw] * 2, out_specs=...  87.3 us
    pallas_call x2, Pallas kernels, grad_rows(): pl.pallas_call(functools.partial(row_kernel, block), grid=(rows_owner //...  69.1 us
    pallas_call x2, Pallas kernels, blocks(): pl.pallas_call(block_kernel, grid_spec=pltpu.PrefetchScalarGridSpec(num_s...  32.8 us
    ppermute x6, waiting for transfers between devices, per_device(): hop = lambda value, pairs: lax.ppermute(value, 'ep', pairs)  11.9 us
    ppermute x6, starting transfers between devices, per_device(): hop = lambda value, pairs: lax.ppermute(value, 'ep', pairs)  4.94 us
    add x1, other arithmetic, per_device(): got_last = hop(mine[1] + got[1] + got_second, second_hop)  4.56 us
  transfers between devices with their start and end apart: 6, of which 4 were waited for; matrix products, arithmetic and copies ran while one was open for 3% of the time, Pallas kernels for 35%

profile of v3, /device:TPU:0, one launch (start us, length us, event | category | flops | bytes accessed | tf_op | source)
XLA Modules:
  0.0 226.5 jit_solution(6990100510790688622)
XLA Ops:
  0.6 1.5 copy.16.slot_ref
  2.2 1.5 copy.17.gate_ref
  3.7 87.3 %shard_map.102 = (bf16[8,64,4096]{2,1,0:T(8,128)(2,1)}, bf16[8,64,4096]{2,1,0:T(8,128)(2,1)}, s32[8,64,128]{2,1,0:T(8,128)}, f32[8,64,128]{2,1,0:T(8,128)}, bf16...) custom-call(bf16[64,4096]{1,0:T(8,128)(2,1)} %x_ref.1, bf16[64,4096]{1,0:T(8,128)(2,1)} %dy_ref.1, ...), custom_call_target="tpu_custom_call" | custom-call | tf_op jit(solution)/shard_map/pallas_call | solution.py:245
  91.0 22.2 %shard_map.104 = (f32[3,128,4096]{2,1,0:T(8,128)}, f32[3,128,4096]{2,1,0:T(8,128)}, bf16[3,3,128,128]{3,2,1,0:T(8,128)(2,1)}, bf16[3,3,128,128]{3,2,1,0:T(8,128)(2,1)}) custom-call(s32[1]{0:T(128)} %bitcast.core_ref, bf16[8,64,4096]{2,1,0:T(8,128)(2,1)} %get-tuple-element.26.x_ref, bf16[8,64,4096]{2,1,0:T(8,128)(2,1)} %get-tuple-element.27.dy_ref, ...), custom_call_target="tpu_custom_call" | custom-call | flops 30000001024 | bytes 1000000 | tf_op jit(solution)/shard_map/pallas_call | solution.py:271
  113.2 0.4 collective-permute-start.1
  113.6 10.6 %shard_map.103 = (f32[1,128,4096]{2,1,0:T(8,128)}, f32[1,128,4096]{2,1,0:T(8,128)}, bf16[1,3,128,128]{3,2,1,0:T(8,128)(2,1)}, bf16[1,3,128,128]{3,2,1,0:T(8,128)(2,1)}) custom-call(s32[1]{0:T(128)} %bitcast.core_ref, bf16[8,64,4096]{2,1,0:T(8,128)(2,1)} %get-tuple-element.26.x_ref, bf16[8,64,4096]{2,1,0:T(8,128)(2,1)} %get-tuple-element.27.dy_ref, ...), custom_call_target="tpu_custom_call" | custom-call | flops 10000000000 | bytes 1000000 | tf_op jit(solution)/shard_map/pallas_call | solution.py:271
  124.2 0.1 collective-permute-start
  124.3 4.0 %collective-permute-done = f32[1,128,4096]{2,1,0:T(8,128)S(1)} collective-permute-done((f32[1,128,4096]{2,1,0:T(8,128)}, f32[1,128,4096]{2,1,0:T(8,128)S(1)}, u32[]{:S(2)}, u32[]{:S(2)}) %collective-permute-start) | collective-permute-done | bytes 2097184 | tf_op jit(solution)/shard_map/ppermute | solution.py:294
  128.3 3.2 %add_bitcast_fusion = f32[128,4096]{1,0:T(8,128)} fusion(f32[1,128,4096]{2,1,0:T(8,128)} %get-tuple-element.36, f32[1,128,4096]{2,1,0:T(8,128)S(1)} %collective-permute-done), kind=kLoop, calls=%fused_computation.10 | loop fusion | flops 524288 | bytes 6291456 | tf_op jit(solution)/shard_map/add | solution.py:312
  131.5 1.5 collective-permute-start.2
  133.0 34.6 %shard_map.105 = bf16[2048,4096]{1,0:T(8,128)(2,1)} custom-call(s32[8,128]{1,0:T(8,128)} %get-tuple-element.38.req_ref, bf16[3,3,128,128]{3,2,1,0:T(8,128)(2,1)} %get-tuple-element.39.near_ref, bf16[1,3,128,128]{3,2,1,0:T(8,128)(2,1)} %get-tuple-element.40.far_ref, bf16[512,4096]{1,0:T(8,128)(2,1)} %bitcast.39), custom_call_target="tpu_custom_call" | custom-call | flops 25769803776 | bytes 16777216 | tf_op jit(solution)/shard_map/pallas_call | solution.py:299
  167.6 0.0 collective-permute-done.2
  167.6 0.0 collective-permute-done.1
  167.6 3.8 %fusion = f32[128,4096]{1,0:T(8,128)} fusion(f32[3,128,4096]{2,1,0:T(8,128)} %collective-permute-done.1, f32[3,128,4096]{2,1,0:T(8,128)} %get-tuple-element.34), kind=kLoop, calls=%fused_computation.1 | loop fusion | flops 524288 | bytes 6291456 | tf_op jit(solution)/shard_map/add | solution.py:314
  171.4 0.5 collective-permute-start.4
  171.9 4.6 %fusion.2 = f32[128,4096]{1,0:T(8,128)} fusion(f32[128,4096]{1,0:T(8,128)} %collective-permute-done.2, f32[3,128,4096]{2,1,0:T(8,128)} %collective-permute-done.1, f32[3,128,4096]{2,1,0:T(8,128)} %get-tuple-element.34), kind=kLoop, calls=%fused_computation.4 | loop fusion | flops 1048576 | bytes 8388608 | tf_op jit(solution)/shard_map/add | solution.py:317
  176.5 1.5 collective-permute-start.3
  178.0 34.6 %shard_map.106 = bf16[2048,4096]{1,0:T(8,128)(2,1)} custom-call(s32[8,128]{1,0:T(8,128)} %get-tuple-element.38.req_ref, bf16[3,3,128,128]{3,2,1,0:T(8,128)(2,1)} %get-tuple-element.42.near_ref, bf16[1,3,128,128]{3,2,1,0:T(8,128)(2,1)} %get-tuple-element.43.far_ref, bf16[512,4096]{1,0:T(8,128)(2,1)} %bitcast.38), custom_call_target="tpu_custom_call" | custom-call | flops 25769803776 | bytes 16777216 | tf_op jit(solution)/shard_map/pallas_call | solution.py:299
  212.5 3.7 %collective-permute-done.4 = f32[128,4096]{1,0:T(8,128)} collective-permute-done((f32[128,4096]{1,0:T(8,128)}, f32[128,4096]{1,0:T(8,128)}, u32[]{:S(2)}, u32[]{:S(2)}) %collective-permute-start.4) | collective-permute-done | bytes 2097184 | tf_op jit(solution)/shard_map/ppermute | solution.py:294
  216.2 2.6 %collective-permute-done.3 = f32[128,4096]{1,0:T(8,128)} collective-permute-done((f32[128,4096]{1,0:T(8,128)}, f32[128,4096]{1,0:T(8,128)}, u32[]{:S(2)}, u32[]{:S(2)}) %collective-permute-start.3) | collective-permute-done | bytes 2097184 | tf_op jit(solution)/shard_map/ppermute | solution.py:294
  218.8 4.0 %fusion.6 = bf16[128,4096]{1,0:T(8,128)(2,1)S(1)} fusion(f32[128,4096]{1,0:T(8,128)} %collective-permute-done.3, f32[128,4096]{1,0:T(8,128)} %collective-permute-done.4, f32[3,128,4096]{2,1,0:T(8,128)} %collective-permute-done.1, f32[3,128,4096]{2,1,0:T(8,128)} %get-tuple-element.34), kind=kLoop, calls=%fused_computation.9 | loop fusion | flops 2097152 | bytes 9437184 | tf_op jit(solution)/shard_map/convert_element_type | solution.py:320
  222.8 0.1 fusion.10
  222.9 0.9 collective-permute-start.5
  223.8 1.5 collective-permute-done.5
  225.4 0.1 bitcast_select_fusion
  225.4 1.0 fusion.9
  (1 shorter events, 0.0 us)
Async XLA Ops:
  113.2 54.4 %collective-permute-start.1 = (f32[3,128,4096]{2,1,0:T(8,128)}, f32[3,128,4096]{2,1,0:T(8,128)}, u32[]{:S(2)}, u32[]{:S(2)}) collective-permute-start(f32[3,128,4096]{2,1,0:T(8,128)} %get-tuple-element.35), channel_id=1, source_target_pairs={{0,1},{1,0},{2,3},{3,2},{4,5},{5,4},{6,7},{7,6}} | collective-permute-start | bytes 18874376 | tf_op jit(solution)/shard_map/ppermute | solution.py:294
  124.2 4.2 %collective-permute-start = (f32[1,128,4096]{2,1,0:T(8,128)}, f32[1,128,4096]{2,1,0:T(8,128)S(1)}, u32[]{:S(2)}, u32[]{:S(2)}) collective-permute-start(f32[1,128,4096]{2,1,0:T(8,128)} %get-tuple-element.32), channel_id=1, source_target_pairs={{0,1},{1,0},{2,3},{3,2},{4,5},{5,4},{6,7},{7,6}} | collective-permute-start | bytes 6291464 | tf_op jit(solution)/shard_map/ppermute | solution.py:294
  131.5 36.1 %collective-permute-start.2 = (f32[128,4096]{1,0:T(8,128)}, f32[128,4096]{1,0:T(8,128)}, u32[]{:S(2)}, u32[]{:S(2)}) collective-permute-start(f32[128,4096]{1,0:T(8,128)} %add_bitcast_fusion), channel_id=1, source_target_pairs={{0,2},{1,5},{2,0},{3,7},{4,6},{5,1},{6,4},{7,3}} | collective-permute-start | bytes 6291464 | tf_op jit(solution)/shard_map/ppermute | solution.py:294
  171.4 44.8 %collective-permute-start.4 = (f32[128,4096]{1,0:T(8,128)}, f32[128,4096]{1,0:T(8,128)}, u32[]{:S(2)}, u32[]{:S(2)}) collective-permute-start(f32[128,4096]{1,0:T(8,128)} %fusion), channel_id=1, source_target_pairs={{0,2},{1,5},{2,0},{3,7},{4,6},{5,1},{6,4},{7,3}} | collective-permute-start | bytes 6291464 | tf_op jit(solution)/shard_map/ppermute | solution.py:294
  176.5 42.4 %collective-permute-start.3 = (f32[128,4096]{1,0:T(8,128)}, f32[128,4096]{1,0:T(8,128)}, u32[]{:S(2)}, u32[]{:S(2)}) collective-permute-start(f32[128,4096]{1,0:T(8,128)} %fusion.2), channel_id=1, source_target_pairs={{0,4},{1,3},{2,6},{3,1},{4,0},{5,7},{6,2},{7,5}} | collective-permute-start | bytes 6291464 | tf_op jit(solution)/shard_map/ppermute | solution.py:294
  222.9 2.4 %collective-permute-start.5 = (bf16[64,2,2048]{2,0,1:T(8,128)(2,1)S(1)}, bf16[64,2,2048]{2,0,1:T(8,128)(2,1)S(1)}, u32[]{:S(2)}, u32[]{:S(2)}) collective-permute-start(bf16[64,2,2048]{2,0,1:T(8,128)(2,1)S(1)} %bitcast.35), channel_id=1, source_target_pairs={{0,1},{1,0},{2,3},{3,2},{4,5},{5,4},{6,7},{7,6}} | collective-permute-start | bytes 1572872 | tf_op jit(solution)/shard_map/ppermute | solution.py:294

commit v4 on v3

--- a/solution.py
+++ b/solution.py
@@ -103,14 +103,16 @@
         if k + 2 < len(steps):
             fetch(k + 2).start()
 
-        def pick(t, _):
-            for u in range(16):
-                r = t * 16 + u
-                row = asked_s[r // SLOTS, r % SLOTS]
-                picked[pl.ds(r, tiles, stride=pick_step), :] = wide[pl.ds(row, tiles, stride=wide_step), :]
-            return 0
-
-        lax.fori_loop(0, n_ask // 16, pick, 0)
+        def pick_device(b, _):
+            def pick(t, _):
+                for u in range(16):
+                    row = asked_s[b, t * 16 + u]
+                    picked[pl.ds(b * SLOTS + t * 16 + u, tiles, stride=pick_step), :] = wide[pl.ds(row, tiles, stride=wide_step), :]
+                return 0
+
+            return lax.fori_loop(0, SLOTS // 16, pick, 0)
+
+        lax.fori_loop(0, N_DEV, pick_device, 0)
         if k >= 2:
             drain_copy(k - 2).wait()
 
@@ -192,8 +194,9 @@
     zero = jnp.zeros((SLOTS, PAIR), F32)
     acc_w, acc_c = lax.fori_loop(0, SEL, step, (zero, zero), unroll=4)
     for ref, acc in ((wt_ref, acc_w), (ct_ref, acc_c)):
-        for k, term in enumerate(split3(acc)[:TERMS]):
-            ref[k] = term
+        terms = split3(acc)
+        for j in range(2):
+            ref[j] = jnp.concatenate([term[:, j * TOK:(j + 1) * TOK] for term in terms], axis=1)
     first_half = lax.broadcasted_iota(I32, (PAIR, 2 * SLOTS), 0) < TOK
     first_cols = lax.broadcasted_iota(I32, (PAIR, 2 * SLOTS), 1) < SLOTS
 
@@ -214,20 +217,41 @@
             other_ref[TOK:, dst] = part[:TOK]
 
 
-def row_kernel(block, req_ref, near_ref, far_ref, x_ref, out_ref, lhs):
-    first = pl.program_id(0) * block
-    rows = lax.broadcasted_iota(I32, (block, SLOTS), 0) + first
+def row_kernel(asked_ref, near_ref, far_ref, x_ref, out_ref, wide, part):
+    n_rows, cols = out_ref.shape
+    tiles = cols // LANES
+    wide_step, part_step = n_rows + PAD, SLOTS + PAD
+
+    def clear(t, _):
+        r = pl.multiple_of(t * 32, 32)
+        for j in range(tiles):
+            wide[pl.ds(j * wide_step + r, 32), :] = jnp.zeros((32, LANES), F32)
+        return 0
+
+    lax.fori_loop(0, n_rows // 32, clear, 0)
     chips = [near_ref.at[2], near_ref.at[0], near_ref.at[1], far_ref.at[0]]
     for q in range(N_DEV):
-        pick = jnp.where(rows == req_ref[pl.ds(q, 1), :], 1.0, 0.0).astype(BF16)
-        cols = slice(q * TOK, (q + 1) * TOK)
-        half = slice((q % 2) * TOK, (q % 2 + 1) * TOK)
-        for k in range(TERMS):
-            full = jnp.dot(pick, chips[q // 2][k], preferred_element_type=F32)
-            lhs[k, :, cols] = full[:, half].astype(BF16)
-    width = x_ref.shape[1]
-    for col in range(0, width, 512):
-        out_ref[:, col:col + 512] = sum(jnp.dot(lhs[k], x_ref[:, col:col + 512], preferred_element_type=F32) for k in range(TERMS)).astype(BF16)
+        tok = x_ref[q * TOK:(q + 1) * TOK, :]
+        full = jnp.dot(chips[q // 2][q % 2], jnp.concatenate([tok] * TERMS, axis=0), preferred_element_type=F32)
+        for j in range(tiles):
+            part[pl.ds(j * part_step, SLOTS), :] = full[:, j * LANES:(j + 1) * LANES]
+
+        def add(t, _):
+            rows = [asked_ref[q, t * 16 + u] for u in range(16)]
+            sums = [wide[pl.ds(rows[u], tiles, stride=wide_step), :] + part[pl.ds(t * 16 + u, tiles, stride=part_step), :] for u in range(16)]
+            for u in range(16):
+                wide[pl.ds(rows[u], tiles, stride=wide_step), :] = sums[u]
+            return 0
+
+        lax.fori_loop(0, SLOTS // 16, add, 0)
+
+    def drain(t, _):
+        r = pl.multiple_of(t * 32, 32)
+        for j in range(tiles):
+            out_ref[pl.ds(r, 32), j * LANES:(j + 1) * LANES] = wide[pl.ds(j * wide_step + r, 32), :].astype(BF16)
+        return 0
+
+    lax.fori_loop(0, n_rows // 32, drain, 0)
 
 
 def solution(mesh):
@@ -267,7 +291,7 @@
             tok = pl.BlockSpec((2, TOK, width), lambda i, c: (chip(i), 0, 0))
             side = pl.BlockSpec((2, TOK, SEL), lambda i, c: (chip(i), 0, 0))
             table = pl.BlockSpec((2 * SLOTS, width), lambda i, c: (chip(i), 0))
-            coef = pl.BlockSpec((None, TERMS, SLOTS, PAIR), lambda i, c: (i, 0, 0, 0))
+            coef = pl.BlockSpec((None, 2, SLOTS, TERMS * TOK), lambda i, c: (i, 0, 0, 0))
             return pl.pallas_call(
                 block_kernel,
                 grid_spec=pltpu.PrefetchScalarGridSpec(
@@ -278,7 +302,7 @@
                                pl.BlockSpec((None, PAIR, width), lambda i, c: (other_at(i, c[0]), 0, 0)), coef, coef],
                     scratch_shapes=[pltpu.VMEM((SEL, PAIR), I32), pltpu.VMEM((SEL, PAIR), F32), pltpu.VMEM((SEL, PAIR), F32)],
                 ),
-                out_shape=[shape((n, PAIR, width), F32)] * 2 + [shape((n, TERMS, SLOTS, PAIR), BF16)] * 2,
+                out_shape=[shape((n, PAIR, width), F32)] * 2 + [shape((n, 2, SLOTS, TERMS * TOK), BF16)] * 2,
                 compiler_params=pltpu.CompilerParams(vmem_limit_bytes=VMEM_BYTES),
                 cost_estimate=pl.CostEstimate(flops=n * 10 ** 10, bytes_accessed=10 ** 6, transcendentals=0),
             )(core_arr, x_all, dy_all, slot_all, gate_all, up_rows, down_rows)
@@ -292,17 +316,19 @@
         first_hop = [(i, i ^ (2 if i % 2 == 0 else 4)) for i in range(N_DEV)]
         second_hop = [(i, i ^ (4 if i % 2 == 0 else 2)) for i in range(N_DEV)]
         hop = lambda value, pairs: lax.ppermute(value, 'ep', pairs)
-        block = 256
-        whole = lambda *dims: pl.BlockSpec(dims, lambda i: (0,) * len(dims))
+        whole = lambda *dims: pl.BlockSpec(dims, lambda i, a: (0,) * len(dims))
 
         def grad_rows(coef_near, coef_far, tok):
             return pl.pallas_call(
-                functools.partial(row_kernel, block),
-                grid=(rows_owner // block,),
-                in_specs=[whole(N_DEV, SLOTS), whole(*coef_near.shape), whole(*coef_far.shape), whole(n_tok, width)],
-                out_specs=pl.BlockSpec((block, width), lambda i: (i, 0)),
+                row_kernel,
+                grid_spec=pltpu.PrefetchScalarGridSpec(
+                    num_scalar_prefetch=1,
+                    grid=(width // CHUNK,),
+                    in_specs=[whole(*coef_near.shape), whole(*coef_far.shape), pl.BlockSpec((n_tok, CHUNK), lambda i, a: (0, i))],
+                    out_specs=pl.BlockSpec((rows_owner, CHUNK), lambda i, a: (0, i)),
+                    scratch_shapes=[pltpu.VMEM((CHUNK // LANES * (rows_owner + PAD), LANES), F32), pltpu.VMEM((CHUNK // LANES * (SLOTS + PAD), LANES), F32)],
+                ),
                 out_shape=shape((rows_owner, width), BF16),
-                scratch_shapes=[pltpu.VMEM((TERMS, block, n_tok), BF16)],
                 compiler_params=pltpu.CompilerParams(vmem_limit_bytes=VMEM_BYTES),
                 cost_estimate=pl.CostEstimate(flops=6 * rows_owner * width * n_tok, bytes_accessed=2 * rows_owner * width, transcendentals=0),
             )(asked, coef_near, coef_far, tok.reshape(n_tok, width))

time: 227 us -> 185 us (0.81)
  Pallas kernels: 189 us -> 145 us
  waiting for transfers between devices: 11.9 us -> 14.6 us
    pallas_call x1, Pallas kernels: 87.3 us -> 48.7 us  [per_device(): pl.pallas_call(share_kernel, in_specs=[vmem] * 5 + [anyw] * 2, out_specs=...]
    pallas_call x2, Pallas kernels: 69.1 us -> 63.5 us  [grad_rows(): pl.pallas_call(row_kernel, grid_spec=pltpu.PrefetchScalarGridSpec(num_sca...]
    ppermute x6, waiting for transfers between devices: 11.9 us -> 14.6 us  [per_device(): hop = lambda value, pairs: lax.ppermute(value, 'ep', pairs)]
  transfers between devices with their start and end apart: 6 -> 6, of which waited for: 4 -> 4; matrix products, arithmetic and copies ran while one was open for 3% -> 4% of each run, Pallas kernels for 35% -> 40%
where the time goes in v4:
time: 185 us
  Pallas kernels  145 us (78%)
  other arithmetic  16.6 us (9%)
  waiting for transfers between devices  14.6 us (8%)
  starting transfers between devices  4.62 us (2%)
  local copies, waits for them, and re-layouts  3.18 us (2%)
    pallas_call x2, Pallas kernels, grad_rows(): pl.pallas_call(row_kernel, grid_spec=pltpu.PrefetchScalarGridSpec(num_sca...  63.5 us
    pallas_call x1, Pallas kernels, per_device(): pl.pallas_call(share_kernel, in_specs=[vmem] * 5 + [anyw] * 2, out_specs=...  48.7 us
    pallas_call x2, Pallas kernels, blocks(): pl.pallas_call(block_kernel, grid_spec=pltpu.PrefetchScalarGridSpec(num_s...  32.8 us
    ppermute x6, waiting for transfers between devices, per_device(): hop = lambda value, pairs: lax.ppermute(value, 'ep', pairs)  14.6 us
    ppermute x6, starting transfers between devices, per_device(): hop = lambda value, pairs: lax.ppermute(value, 'ep', pairs)  4.62 us
    add x1, other arithmetic, per_device(): got_last = hop(mine[1] + got[1] + got_second, second_hop)  4.56 us
    convert_element_type x1, other arithmetic, per_device(): (mine[2] + got[2] + got_own + got_last).astype(BF16)  3.96 us
    add x1, other arithmetic, per_device(): got_own = hop(mine[0] + got[0], first_hop)  3.81 us
  transfers between devices with their start and end apart: 6, of which 4 were waited for; matrix products, arithmetic and copies ran while one was open for 4% of the time, Pallas kernels for 40%

profile of v4, /device:TPU:0, one launch (start us, length us, event | category | flops | bytes accessed | tf_op | source)
XLA Modules:
  0.0 184.7 jit_solution(17710788591562355306)
XLA Ops:
  0.6 1.5 copy.16.slot_ref
  2.2 1.5 copy.17.gate_ref
  3.7 48.7 %shard_map.102 = (bf16[8,64,4096]{2,1,0:T(8,128)(2,1)}, bf16[8,64,4096]{2,1,0:T(8,128)(2,1)}, s32[8,64,128]{2,1,0:T(8,128)}, f32[8,64,128]{2,1,0:T(8,128)}, bf16...) custom-call(bf16[64,4096]{1,0:T(8,128)(2,1)} %x_ref.1, bf16[64,4096]{1,0:T(8,128)(2,1)} %dy_ref.1, ...), custom_call_target="tpu_custom_call" | custom-call | tf_op jit(solution)/shard_map/pallas_call | solution.py:269
  52.4 22.2 %shard_map.104 = (f32[3,128,4096]{2,1,0:T(8,128)}, f32[3,128,4096]{2,1,0:T(8,128)}, bf16[3,2,128,192]{3,2,1,0:T(8,128)(2,1)}, bf16[3,2,128,192]{3,2,1,0:T(8,128)(2,1)}) custom-call(s32[1]{0:T(128)} %bitcast.core_ref, bf16[8,64,4096]{2,1,0:T(8,128)(2,1)} %get-tuple-element.26.x_ref, bf16[8,64,4096]{2,1,0:T(8,128)(2,1)} %get-tuple-element.27.dy_ref, ...), custom_call_target="tpu_custom_call" | custom-call | flops 30000001024 | bytes 1000000 | tf_op jit(solution)/shard_map/pallas_call | solution.py:295
  74.6 0.4 collective-permute-start.1
  75.0 10.6 %shard_map.103 = (f32[1,128,4096]{2,1,0:T(8,128)}, f32[1,128,4096]{2,1,0:T(8,128)}, bf16[1,2,128,192]{3,2,1,0:T(8,128)(2,1)}, bf16[1,2,128,192]{3,2,1,0:T(8,128)(2,1)}) custom-call(s32[1]{0:T(128)} %bitcast.core_ref, bf16[8,64,4096]{2,1,0:T(8,128)(2,1)} %get-tuple-element.26.x_ref, bf16[8,64,4096]{2,1,0:T(8,128)(2,1)} %get-tuple-element.27.dy_ref, ...), custom_call_target="tpu_custom_call" | custom-call | flops 10000000000 | bytes 1000000 | tf_op jit(solution)/shard_map/pallas_call | solution.py:295
  85.6 0.1 collective-permute-start
  85.7 4.0 %collective-permute-done = f32[1,128,4096]{2,1,0:T(8,128)S(1)} collective-permute-done((f32[1,128,4096]{2,1,0:T(8,128)}, f32[1,128,4096]{2,1,0:T(8,128)S(1)}, u32[]{:S(2)}, u32[]{:S(2)}) %collective-permute-start) | collective-permute-done | bytes 2097184 | tf_op jit(solution)/shard_map/ppermute | solution.py:318
  89.8 3.2 %add_bitcast_fusion = f32[128,4096]{1,0:T(8,128)} fusion(f32[1,128,4096]{2,1,0:T(8,128)} %get-tuple-element.36, f32[1,128,4096]{2,1,0:T(8,128)S(1)} %collective-permute-done), kind=kLoop, calls=%fused_computation.10 | loop fusion | flops 524288 | bytes 6291456 | tf_op jit(solution)/shard_map/add | solution.py:338
  92.9 1.1 collective-permute-start.2
  94.1 31.8 %shard_map.105 = bf16[2048,4096]{1,0:T(8,128)(2,1)} custom-call(s32[8,128]{1,0:T(8,128)} %get-tuple-element.38.asked_ref, bf16[3,2,128,192]{3,2,1,0:T(8,128)(2,1)} %get-tuple-element.39.near_ref, bf16[1,2,128,192]{3,2,1,0:T(8,128)(2,1)} %get-tuple-element.40.far_ref, bf16[512,4096]{1,0:T(8,128)(2,1)} %bitcast.39), custom_call_target="tpu_custom_call" | custom-call | flops 25769803776 | bytes 16777216 | tf_op jit(solution)/shard_map/pallas_call | solution.py:322
  125.8 0.0 collective-permute-done.2
  125.8 0.0 collective-permute-done.1
  125.8 3.8 %fusion = f32[128,4096]{1,0:T(8,128)} fusion(f32[3,128,4096]{2,1,0:T(8,128)} %collective-permute-done.1, f32[3,128,4096]{2,1,0:T(8,128)} %get-tuple-element.34), kind=kLoop, calls=%fused_computation.1 | loop fusion | flops 524288 | bytes 6291456 | tf_op jit(solution)/shard_map/add | solution.py:340
  129.6 0.9 collective-permute-start.4
  130.5 4.6 %fusion.2 = f32[128,4096]{1,0:T(8,128)} fusion(f32[128,4096]{1,0:T(8,128)} %collective-permute-done.2, f32[3,128,4096]{2,1,0:T(8,128)} %collective-permute-done.1, f32[3,128,4096]{2,1,0:T(8,128)} %get-tuple-element.34), kind=kLoop, calls=%fused_computation.4 | loop fusion | flops 1048576 | bytes 8388608 | tf_op jit(solution)/shard_map/add | solution.py:343
  135.1 1.1 collective-permute-start.3
  136.2 31.7 %shard_map.106 = bf16[2048,4096]{1,0:T(8,128)(2,1)} custom-call(s32[8,128]{1,0:T(8,128)} %get-tuple-element.38.asked_ref, bf16[3,2,128,192]{3,2,1,0:T(8,128)(2,1)} %get-tuple-element.42.near_ref, bf16[1,2,128,192]{3,2,1,0:T(8,128)(2,1)} %get-tuple-element.43.far_ref, bf16[512,4096]{1,0:T(8,128)(2,1)} %bitcast.38), custom_call_target="tpu_custom_call" | custom-call | flops 25769803776 | bytes 16777216 | tf_op jit(solution)/shard_map/pallas_call | solution.py:322
  168.0 6.1 %collective-permute-done.4 = f32[128,4096]{1,0:T(8,128)} collective-permute-done((f32[128,4096]{1,0:T(8,128)}, f32[128,4096]{1,0:T(8,128)}, u32[]{:S(2)}, u32[]{:S(2)}) %collective-permute-start.4) | collective-permute-done | bytes 2097184 | tf_op jit(solution)/shard_map/ppermute | solution.py:318
  174.1 3.0 %collective-permute-done.3 = f32[128,4096]{1,0:T(8,128)} collective-permute-done((f32[128,4096]{1,0:T(8,128)}, f32[128,4096]{1,0:T(8,128)}, u32[]{:S(2)}, u32[]{:S(2)}) %collective-permute-start.3) | collective-permute-done | bytes 2097184 | tf_op jit(solution)/shard_map/ppermute | solution.py:318
  177.0 4.0 %fusion.6 = bf16[128,4096]{1,0:T(8,128)(2,1)S(1)} fusion(f32[128,4096]{1,0:T(8,128)} %collective-permute-done.3, f32[128,4096]{1,0:T(8,128)} %collective-permute-done.4, f32[3,128,4096]{2,1,0:T(8,128)} %collective-permute-done.1, f32[3,128,4096]{2,1,0:T(8,128)} %get-tuple-element.34), kind=kLoop, calls=%fused_computation.9 | loop fusion | flops 2097152 | bytes 9437184 | tf_op jit(solution)/shard_map/convert_element_type | solution.py:346
  181.0 0.1 fusion.10
  181.1 1.0 collective-permute-start.5
  182.1 1.5 collective-permute-done.5
  183.6 0.1 bitcast_select_fusion
  183.7 1.0 fusion.9
  (1 shorter events, 0.0 us)
Async XLA Ops:
  74.6 51.2 %collective-permute-start.1 = (f32[3,128,4096]{2,1,0:T(8,128)}, f32[3,128,4096]{2,1,0:T(8,128)}, u32[]{:S(2)}, u32[]{:S(2)}) collective-permute-start(f32[3,128,4096]{2,1,0:T(8,128)} %get-tuple-element.35), channel_id=1, source_target_pairs={{0,1},{1,0},{2,3},{3,2},{4,5},{5,4},{6,7},{7,6}} | collective-permute-start | bytes 18874376 | tf_op jit(solution)/shard_map/ppermute | solution.py:318
  85.6 4.2 %collective-permute-start = (f32[1,128,4096]{2,1,0:T(8,128)}, f32[1,128,4096]{2,1,0:T(8,128)S(1)}, u32[]{:S(2)}, u32[]{:S(2)}) collective-permute-start(f32[1,128,4096]{2,1,0:T(8,128)} %get-tuple-element.32), channel_id=1, source_target_pairs={{0,1},{1,0},{2,3},{3,2},{4,5},{5,4},{6,7},{7,6}} | collective-permute-start | bytes 6291464 | tf_op jit(solution)/shard_map/ppermute | solution.py:318
  92.9 32.9 %collective-permute-start.2 = (f32[128,4096]{1,0:T(8,128)}, f32[128,4096]{1,0:T(8,128)}, u32[]{:S(2)}, u32[]{:S(2)}) collective-permute-start(f32[128,4096]{1,0:T(8,128)} %add_bitcast_fusion), channel_id=1, source_target_pairs={{0,2},{1,5},{2,0},{3,7},{4,6},{5,1},{6,4},{7,3}} | collective-permute-start | bytes 6291464 | tf_op jit(solution)/shard_map/ppermute | solution.py:318
  129.6 44.4 %collective-permute-start.4 = (f32[128,4096]{1,0:T(8,128)}, f32[128,4096]{1,0:T(8,128)}, u32[]{:S(2)}, u32[]{:S(2)}) collective-permute-start(f32[128,4096]{1,0:T(8,128)} %fusion), channel_id=1, source_target_pairs={{0,2},{1,5},{2,0},{3,7},{4,6},{5,1},{6,4},{7,3}} | collective-permute-start | bytes 6291464 | tf_op jit(solution)/shard_map/ppermute | solution.py:318
  135.1 41.9 %collective-permute-start.3 = (f32[128,4096]{1,0:T(8,128)}, f32[128,4096]{1,0:T(8,128)}, u32[]{:S(2)}, u32[]{:S(2)}) collective-permute-start(f32[128,4096]{1,0:T(8,128)} %fusion.2), channel_id=1, source_target_pairs={{0,4},{1,3},{2,6},{3,1},{4,0},{5,7},{6,2},{7,5}} | collective-permute-start | bytes 6291464 | tf_op jit(solution)/shard_map/ppermute | solution.py:318
  181.1 2.5 %collective-permute-start.5 = (bf16[64,2,2048]{2,0,1:T(8,128)(2,1)S(1)}, bf16[64,2,2048]{2,0,1:T(8,128)(2,1)S(1)}, u32[]{:S(2)}, u32[]{:S(2)}) collective-permute-start(bf16[64,2,2048]{2,0,1:T(8,128)(2,1)S(1)} %bitcast.35), channel_id=1, source_target_pairs={{0,1},{1,0},{2,3},{3,2},{4,5},{5,4},{6,7},{7,6}} | collective-permute-start | bytes 1572872 | tf_op jit(solution)/shard_map/ppermute | solution.py:318

commit v5 on v0

v5 whole, which is shorter than its diff:
```python
import functools
import math
import jax
import jax.numpy as jnp
from jax import lax
from jax.experimental import pallas as pl
from jax.experimental.pallas import tpu as pltpu
from jax.sharding import PartitionSpec as P

F32, BF16, I32 = jnp.float32, jnp.bfloat16, jnp.int32
N_DEV, TOK, SLOTS, SEL = 8, 64, 128, 128
PAIR = 2 * TOK
TERMS = 3
CHUNK = 1024
ROW_CHUNK = 2048
LANES = 128
PAD = 4
VMEM_BYTES = 62 * 1024 * 1024
MESH = pl.DeviceIdType.MESH


def gelu_pair(pre_act):
    normal_cdf = 0.5 * (1.0 + lax.erf(pre_act * (2.0 ** -0.5)))
    normal_pdf = jnp.exp(-0.5 * pre_act * pre_act) * ((2.0 * math.pi) ** -0.5)
    return pre_act * normal_cdf, normal_cdf + pre_act * normal_pdf


def split3(wide):
    high = wide.astype(BF16)
    rest = wide - high.astype(F32)
    mid = rest.astype(BF16)
    low = (rest - mid.astype(F32)).astype(BF16)
    return high, mid, low


N_COPIES = 64


def layer_kernel(x_ref, dy_ref, slot_ref, gate_ref, req_ref, up_ref, down_ref,
                 x_out, dy_out, c_out, w_out, asked_out, first_sum, second_sum, own_mine, own_got,
                 x_all, dy_all, slot_all, gate_all, up_rows, down_rows, pair_recv, hop_recv, asked, asked_s, slot_t, w_t, c_t,
                 send_sem, recv_sem, own_sem, smem_sem, in_sem, out_sem):
    me = lax.axis_index("ep")
    core = lax.rem(me, 2)
    n_rows, width = up_ref.shape
    half = width // 2
    steps = [(ref, out, col) for ref, out in ((up_ref, up_rows), (down_ref, down_rows)) for col in range(0, width, CHUNK)]
    tiles = CHUNK // LANES
    wide_step, pick_step = n_rows + PAD, N_DEV * SLOTS + PAD
    sent = []

    def descriptor(k, src, dst, mask):
        view = lambda ref, index: ref if index is None else ref.at[index]
        return pltpu.make_async_remote_copy(src_ref=view(*src), dst_ref=view(*dst), send_sem=send_sem.at[k], recv_sem=recv_sem.at[k],
                                            device_id={"ep": me ^ mask}, device_id_type=MESH)

    def push(src, src_index, dst, dst_index, mask):
        spec = (len(sent), (src, src_index), (dst, dst_index), mask)
        descriptor(*spec).start()
        sent.append(spec)
        return spec

    def arrive(specs):
        for spec in specs:
            descriptor(*spec).wait_recv()

    def leave(specs):
        for spec in specs:
            descriptor(*spec).wait_send()

    own = [pltpu.make_async_copy(src, dst.at[0], own_sem.at[k]) for k, (src, dst) in enumerate(((x_ref, x_all), (dy_ref, dy_all), (slot_ref, slot_all), (gate_ref, gate_all)))]
    barrier = pltpu.get_barrier_semaphore()
    for b in range(1, N_DEV):
        pl.semaphore_signal(barrier, inc=1, device_id={"ep": me ^ b}, device_id_type=MESH)
    for copy in own:
        copy.start()
    pl.semaphore_wait(barrier, N_DEV - 1)

    asks = [push(req_ref, (0, pl.ds(me ^ b, 1)), asked, pl.ds(b, 1), b) for b in range(1, N_DEV)]
    first = [
        push(gate_ref, None, gate_all, 4, 4), push(slot_ref, None, slot_all, 2, 2),
        push(x_ref, None, x_all, 4, 4), push(dy_ref, None, dy_all, 2, 2),
    ]
    near_own = [push(gate_ref, None, gate_all, 1, 1), push(slot_ref, None, slot_all, 1, 1), push(x_ref, None, x_all, 1, 1), push(dy_ref, None, dy_all, 1, 1)]
    low, top = pl.ds(0, TOK // 2), pl.ds(TOK // 2, TOK // 2)
    second = [
        push(gate_ref, None, gate_all, 2, 2), push(slot_ref, None, slot_all, 4, 4),
        push(x_ref, low, x_all, (2, low), 2), push(dy_ref, low, dy_all, (4, low), 4),
    ]
    asked[pl.ds(0, 1), :] = req_ref[0, pl.ds(me, 1), :]
    arrive(asks)
    asked_out[...] = asked[...]
    to_smem = pltpu.make_async_copy(asked, asked_s, smem_sem)
    to_smem.start()
    to_smem.wait()

    def gather_all(table, wide, picked):
        def fetch(k):
            ref, _, col = steps[k]
            return pltpu.make_async_copy(ref.at[:, pl.ds(col, CHUNK)], table.at[k % 2], in_sem.at[k % 2])

        fetch(0).start()
        fetch(1).start()
        for k in range(len(steps)):
            if k == len(steps) // 2:
                arrive(first)
                far = [
                    push(gate_all, 4, gate_all, 6, 2), push(slot_all, 2, slot_all, 6, 4),
                    push(x_all, 4, x_all, 6, 2), push(dy_all, 2, dy_all, 6, 4),
                ]
                second.extend([push(x_ref, top, x_all, (2, top), 2), push(dy_ref, top, dy_all, (4, top), 4)])
                near_first = [push(gate_all, 4, gate_all, 5, 1), push(slot_all, 2, slot_all, 3, 1), push(x_all, 4, x_all, 5, 1), push(dy_all, 2, dy_all, 3, 1)]
            fetch(k).wait()

            def fill(t, _):
                r = pl.multiple_of(t * 32, 32)
                for j in range(tiles):
                    wide[pl.ds(j * wide_step + r, 32), :] = table[k % 2, pl.ds(r, 32), j * LANES:(j + 1) * LANES].astype(F32)
                return 0

            lax.fori_loop(0, n_rows // 32, fill, 0)
            if k + 2 < len(steps):
                fetch(k + 2).start()

            def pick_device(b, _):
                def pick(t, _):
                    for u in range(16):
                        row = asked_s[b, t * 16 + u]
                        picked[pl.ds(b * SLOTS + t * 16 + u, tiles, stride=pick_step), :] = wide[pl.ds(row, tiles, stride=wide_step), :]
                    return 0

                return lax.fori_loop(0, SLOTS // 16, pick, 0)

            lax.fori_loop(0, N_DEV, pick_device, 0)
            _, rows_ref, col = steps[k]

            def drain(t, _):
                r = pl.multiple_of(t * 32, 32)
                for j in range(tiles):
                    rows_ref[pl.ds(r, 32), col + j * LANES:col + (j + 1) * LANES] = picked[pl.ds(j * pick_step + r, 32), :].astype(BF16)
                return 0

            lax.fori_loop(0, N_DEV * SLOTS // 32, drain, 0)
        return far, near_first

    kept = []
    pl.run_scoped(
        lambda *bufs: kept.append(gather_all(*bufs)),
        pltpu.VMEM((2, n_rows, CHUNK), BF16), pltpu.VMEM((tiles * wide_step, LANES), F32), pltpu.VMEM((tiles * pick_step, LANES), F32),
    )
    far, near_first = kept[0]
    for copy in own:
        copy.wait()
    dims = (((1,), (1,)), ((), ()))
    row_iota = lax.broadcasted_iota(I32, (SLOTS, PAIR), 0)
    block_diag = (lax.broadcasted_iota(I32, (PAIR, 2 * SLOTS), 0) < TOK) == (lax.broadcasted_iota(I32, (PAIR, 2 * SLOTS), 1) < SLOTS)

    def block(r, mine, other):
        toks, rows = pl.ds(2 * r, 2), pl.ds(2 * r * SLOTS, 2 * SLOTS)

        def dots(tok, table):
            full = lax.dot_general(tok[toks].reshape(PAIR, width), table[rows, :], dims, preferred_element_type=F32)
            return jnp.concatenate([full[:TOK, :SLOTS], full[TOK:, SLOTS:]], axis=0)

        act, slope = gelu_pair(dots(x_all, up_rows))
        slope = slope * dots(dy_all, down_rows)
        local = slot_all[toks].reshape(PAIR, SEL) - me * SLOTS
        valid = (local >= 0) & (local < SLOTS)
        index = jnp.where(valid, local, 0)
        act = jnp.take_along_axis(act, index, axis=1)
        slope = jnp.take_along_axis(slope, index, axis=1)
        gate = gate_all[toks].reshape(PAIR, SEL)
        w_t[...] = jnp.where(valid, (gate * act).astype(BF16).astype(F32), 0.0).T
        c_t[...] = jnp.where(valid, (gate * slope).astype(BF16).astype(F32), 0.0).T
        slot_t[...] = jnp.where(valid, local, -1).T

        def step(s, acc):
            acc_w, acc_c = acc
            hit = row_iota == slot_t[pl.ds(s, 1), :]
            acc_w += jnp.where(hit, w_t[pl.ds(s, 1), :], 0.0)
            acc_c += jnp.where(hit, c_t[pl.ds(s, 1), :], 0.0)
            return acc_w, acc_c

        zero = jnp.zeros((SLOTS, PAIR), F32)
        acc_w, acc_c = lax.fori_loop(0, SEL, step, (zero, zero), unroll=4)
        for ref, acc in ((w_out, acc_w), (c_out, acc_c)):
            terms = split3(acc)
            for j in range(2):
                ref[2 * r + j] = jnp.concatenate([term[:, j * TOK:(j + 1) * TOK] for term in terms], axis=1)

        def spread(acc):
            both = jnp.concatenate([acc.T, acc.T], axis=1)
            return split3(jnp.where(block_diag, both, 0.0))

        w_terms, c_terms = spread(acc_w), spread(acc_c)
        for col in range(0, half, 512):
            for shift, terms, table in ((0, w_terms, down_rows), (half, c_terms, up_rows)):
                here = pl.ds(pl.multiple_of(core * half + col, 512), 512)
                there = pl.ds(pl.multiple_of((1 - core) * half + col, 512), 512)
                dst = slice(shift + col, shift + col + 512)
                mine[:, dst] = sum(jnp.dot(term, table[rows, here], preferred_element_type=F32) for term in terms)
                part = sum(jnp.dot(term, table[rows, there], preferred_element_type=F32) for term in terms)
                other[:TOK, dst] = part[TOK:]
                other[TOK:, dst] = part[:TOK]

    def add_into(dst, src):
        def add(t, _):
            r = pl.ds(pl.multiple_of(t * 16, 16), 16)
            dst[r, :] = dst[r, :] + src[r, :]
            return 0

        lax.fori_loop(0, PAIR // 16, add, 0)

    def blocks(mine, other):
        save = lambda src, dst, k: pltpu.make_async_copy(src, dst, out_sem.at[k])
        arrive(far)
        near_far = [push(ref, 6, ref, 7, 1) for ref in (gate_all, slot_all, x_all, dy_all)]
        arrive(near_own + near_first + near_far)
        block(3, mine.at[3], other.at[0])
        pair_far = push(other, 0, pair_recv, 0, 1)
        block(0, mine.at[0], other.at[1])
        pair_own = push(other, 1, own_got, None, 1)
        saves = [save(mine.at[0], own_mine, 0)]
        saves[0].start()
        arrive([pair_far])
        add_into(mine.at[3], pair_recv.at[0])
        hop = push(mine, 3, hop_recv, None, 2 + 2 * core)
        arrive(second)
        near_second = [push(gate_all, 2, gate_all, 3, 1), push(slot_all, 4, slot_all, 5, 1), push(x_all, 2, x_all, 3, 1), push(dy_all, 4, dy_all, 5, 1)]
        arrive(near_second)
        for k, (src, dst) in enumerate(((x_all, x_out), (dy_all, dy_out))):
            saves.append(save(src, dst, 1 + k))
            saves[-1].start()
        leave([pair_far])
        block(1, mine.at[1], other.at[0])
        pair_x = push(other, 0, pair_recv, 1, 1)
        leave([pair_own])
        block(2, mine.at[2], other.at[1])
        pair_y = push(other, 1, pair_recv, 2, 1)
        arrive([pair_x])
        add_into(mine.at[1], pair_recv.at[1])
        arrive([pair_y])
        add_into(mine.at[2], pair_recv.at[2])
        saves.append(save(mine.at[1 + core], first_sum, 3))
        saves[-1].start()
        arrive([hop])
        add_into(mine.at[2 - core], hop_recv)
        saves.append(save(mine.at[2 - core], second_sum, 4))
        saves[-1].start()
        arrive([pair_own])
        leave([spec for spec in sent if spec is not pair_far and spec is not pair_own])
        for copy in saves:
            copy.wait()

    pl.run_scoped(blocks, pltpu.VMEM((4, PAIR, width), F32), pltpu.VMEM((2, PAIR, width), F32))


def row_kernel(asked_ref, coef_ref, x_ref, out_ref, wide, part):
    n_rows, cols = out_ref.shape
    tiles = cols // LANES
    wide_step, part_step = n_rows + PAD, SLOTS + PAD

    def clear(t, _):
        r = pl.multiple_of(t * 32, 32)
        for j in range(tiles):
            wide[pl.ds(j * wide_step + r, 32), :] = jnp.zeros((32, LANES), F32)
        return 0

    lax.fori_loop(0, n_rows // 32, clear, 0)
    for q in range(N_DEV):
        tok = x_ref[q * TOK:(q + 1) * TOK, :]
        full = jnp.dot(coef_ref[q], jnp.concatenate([tok] * TERMS, axis=0), preferred_element_type=F32)
        for j in range(tiles):
            part[pl.ds(j * part_step, SLOTS), :] = full[:, j * LANES:(j + 1) * LANES]

        def add(t, _):
            rows = [asked_ref[q, t * 16 + u] for u in range(16)]
            sums = [wide[pl.ds(rows[u], tiles, stride=wide_step), :] + part[pl.ds(t * 16 + u, tiles, stride=part_step), :] for u in range(16)]
            for u in range(16):
                wide[pl.ds(rows[u], tiles, stride=wide_step), :] = sums[u]
            return 0

        lax.fori_loop(0, SLOTS // 16, add, 0)

    def drain(t, _):
        r = pl.multiple_of(t * 32, 32)
        for j in range(tiles):
            out_ref[pl.ds(r, 32), j * LANES:(j + 1) * LANES] = wide[pl.ds(j * wide_step + r, 32), :].astype(BF16)
        return 0

    lax.fori_loop(0, n_rows // 32, drain, 0)


def solution(mesh):
    tok_spec = P(('dp', 'ep'))
    table_spec = P('ep')

    def per_device(tokens, slot_ids, request_rows, gate_vals, grad_out, up_local, down_local):
        width = tokens.shape[1]
        rows_owner = up_local.shape[0]
        n_tok = N_DEV * TOK
        half = width // 2
        core = lax.axis_index('ep') % 2
        vmem, anyw = pl.BlockSpec(memory_space=pltpu.VMEM), pl.BlockSpec(memory_space=pl.ANY)
        shape = jax.ShapeDtypeStruct
        sums = shape((PAIR, width), F32)
        x_all, dy_all, c_terms, w_terms, asked, first_sum, second_sum, own_mine, own_got = pl.pallas_call(
            layer_kernel,
            in_specs=[anyw, anyw, vmem, vmem, vmem, anyw, anyw],
            out_specs=[anyw] * 2 + [vmem] * 3 + [anyw] * 4,
            out_shape=[shape((N_DEV, TOK, width), BF16)] * 2 + [shape((N_DEV, SLOTS, TERMS * TOK), BF16)] * 2 + [shape((N_DEV, SLOTS), I32)] + [sums] * 4,
            scratch_shapes=[
                pltpu.VMEM((N_DEV, TOK, width), BF16), pltpu.VMEM((N_DEV, TOK, width), BF16),
                pltpu.VMEM((N_DEV, TOK, SEL), I32), pltpu.VMEM((N_DEV, TOK, SEL), F32),
                pltpu.VMEM((N_DEV * SLOTS, width), BF16), pltpu.VMEM((N_DEV * SLOTS, width), BF16),
                pltpu.VMEM((3, PAIR, width), F32), pltpu.VMEM((PAIR, width), F32),
                pltpu.VMEM((N_DEV, SLOTS), I32), pltpu.SMEM((N_DEV, SLOTS), I32),
                pltpu.VMEM((SEL, PAIR), I32), pltpu.VMEM((SEL, PAIR), F32), pltpu.VMEM((SEL, PAIR), F32),
                pltpu.SemaphoreType.DMA((N_COPIES,)), pltpu.SemaphoreType.DMA((N_COPIES,)),
                pltpu.SemaphoreType.DMA((4,)), pltpu.SemaphoreType.DMA,
                pltpu.SemaphoreType.DMA((2,)), pltpu.SemaphoreType.DMA((5,)),
            ],
            compiler_params=pltpu.CompilerParams(collective_id=0, has_side_effects=True, vmem_limit_bytes=VMEM_BYTES),
        )(tokens, grad_out, slot_ids.reshape(TOK, SEL), gate_vals.reshape(TOK, SEL), request_rows, up_local, down_local)

        partner = [(i, i ^ 1) for i in range(N_DEV)]
        first_hop = [(i, i ^ (2 if i % 2 == 0 else 4)) for i in range(N_DEV)]
        second_hop = [(i, i ^ (4 if i % 2 == 0 else 2)) for i in range(N_DEV)]
        hop = lambda value, pairs: lax.ppermute(value, 'ep', pairs)

        def grad_rows(coef, tok):
            return pl.pallas_call(
                row_kernel,
                grid_spec=pltpu.PrefetchScalarGridSpec(
                    num_scalar_prefetch=1,
                    grid=(width // ROW_CHUNK,),
                    in_specs=[pl.BlockSpec(coef.shape, lambda i, a: (0, 0, 0)), pl.BlockSpec((n_tok, ROW_CHUNK), lambda i, a: (0, i))],
                    out_specs=pl.BlockSpec((rows_owner, ROW_CHUNK), lambda i, a: (0, i)),
                    scratch_shapes=[pltpu.VMEM((ROW_CHUNK // LANES * (rows_owner + PAD), LANES), F32), pltpu.VMEM((ROW_CHUNK // LANES * (SLOTS + PAD), LANES), F32)],
                ),
                out_shape=shape((rows_owner, width), BF16),
                compiler_params=pltpu.CompilerParams(vmem_limit_bytes=VMEM_BYTES),
                cost_estimate=pl.CostEstimate(flops=6 * rows_owner * width * n_tok, bytes_accessed=2 * rows_owner * width, transcendentals=0),
            )(asked, coef, tok.reshape(n_tok, width))

        got_own = hop(first_sum, first_hop)
        got_last = hop(second_sum, second_hop)
        grad_up = grad_rows(c_terms, x_all)
        grad_down = grad_rows(w_terms, dy_all)
        got_last, got_own, grad_up, grad_down = lax.optimization_barrier((got_last, got_own, grad_up, grad_down))
        final = (own_mine + own_got + got_own + got_last).astype(BF16).reshape(2, TOK, 2, half)
        keep, give = final[0], final[1]
        back = hop(give, partner)
        low = jnp.where(core == 0, keep, back)
        high = jnp.where(core == 0, back, keep)
        token_out = jnp.concatenate([low, high], axis=2)
        return token_out[:, 0], token_out[:, 1], grad_up, grad_down

    return jax.shard_map(per_device, mesh=mesh, in_specs=(tok_spec, tok_spec, tok_spec, tok_spec, tok_spec, table_spec, table_spec), out_specs=(tok_spec, tok_spec, tok_spec, tok_spec), check_vma=False)
```

time: 1500 us -> 143 us (0.10)
  other arithmetic: 719 us -> 5.08 us
  local copies, waits for them, and re-layouts: 333 us -> 3.2 us
  waiting for transfers between devices: 288 us -> 2.68 us
  Pallas kernels: 0 us -> 129 us
  matrix products: 120 us -> 0 us
    scatter-add x10 -> x0, other arithmetic: 571 us -> none  [the longest x4 248 us: scan_step(): acc_down = acc_down.at[flat_slots].add(down_part.reshape(-1, width))]
    gather x10 -> x0, local copies, waits for them, and re-layouts: 311 us -> none  [the longest x4 133 us: scan_step(): up_rows = up_table[slot_blk]]
    all_to_all x4 -> x0, waiting for transfers between devices: 288 us -> none  [the longest x1 93.5 us: per_device(): lax.all_to_all(up_local[asked_rows], 'ep', 0, 0, tiled=True)]
    pallas_call x0 -> x3, Pallas kernels: none -> 129 us  [the longest x1 83.3 us: per_device(): pl.pallas_call(layer_kernel, in_specs=[anyw, anyw, vmem, vmem, vmem, anyw...]
    dot_general x16 -> x0, matrix products: 120 us -> none  [the longest x4 46.1 us: scan_step(): jnp.einsum('bsd,bd->bs', up_rows, x_blk, preferred_element_type=jnp.float32)]
    mul x8 -> x0, other arithmetic: 88.1 us -> none  [scan_step(): down_part = w_out.astype(jnp.float32)[:, :, None] * dy_blk[:, None, :]]
    convert_element_type x8 -> x1, other arithmetic: 56.5 us -> 3.96 us  [per_device(): (own_mine + own_got + got_own + got_last).astype(BF16)]
    broadcast_in_dim x2 -> x0, local copies, waits for them, and re-layouts: 16.5 us -> none  [local_layer(): zero_acc = jnp.zeros((n_slots, width), jnp.float32)]
  transfers between devices with their start and end apart: 4 -> 3, of which waited for: 4 -> 2; matrix products, arithmetic and copies ran while one was open for 6% -> 0% of each run, Pallas kernels for 0% -> 32%
where the time goes in v5:
time: 143 us
  Pallas kernels  129 us (90%)
  other arithmetic  5.08 us (4%)
  local copies, waits for them, and re-layouts  3.2 us (2%)
  waiting for transfers between devices  2.68 us (2%)
  starting transfers between devices  2.07 us (1%)
    pallas_call x1, Pallas kernels, per_device(): pl.pallas_call(layer_kernel, in_specs=[anyw, anyw, vmem, vmem, vmem, anyw...  83.3 us
    pallas_call x2, Pallas kernels, grad_rows(): pl.pallas_call(row_kernel, grid_spec=pltpu.PrefetchScalarGridSpec(num_sca...  45.4 us
    convert_element_type x1, other arithmetic, per_device(): (own_mine + own_got + got_own + got_last).astype(BF16)  3.96 us
  transfers between devices with their start and end apart: 3, of which 2 were waited for; matrix products, arithmetic and copies ran while one was open for 0% of the time, Pallas kernels for 32%

profile of v5, /device:TPU:0, one launch (start us, length us, event | category | flops | bytes accessed | tf_op | source)
XLA Modules:
  0.0 142.5 jit_solution(955017108670514558)
XLA Ops:
  0.6 1.5 %copy.16.slot_ref = s32[64,128]{1,0:T(8,128)} copy(s32[64,128]{0,1:T(8,128)} %bitcast.19) | data formatting | bytes 65536 | tf_op jit(solution)/shard_map/reshape | solution.py:324
  2.2 1.5 %copy.17.gate_ref = f32[64,128]{1,0:T(8,128)} copy(f32[64,128]{0,1:T(8,128)} %bitcast.20) | data formatting | bytes 65536 | tf_op jit(solution)/shard_map/reshape | solution.py:324
  3.7 83.3 %shard_map.102 = (bf16[8,64,4096]{2,1,0:T(8,128)(2,1)}, bf16[8,64,4096]{2,1,0:T(8,128)(2,1)}, bf16[8,128,192]{2,1,0:T(8,128)(2,1)}, bf16[8,128,192]{2,1,0:T(8,12...) custom-call(bf16[64,4096]{1,0:T(8,128)(2,1)} %x_ref.1, ...), custom_call_target="tpu_custom_call" | custom-call | tf_op jit(solution)/shard_map/pallas_call | solution.py:307
  87.1 1.2 collective-permute-start
  88.3 0.8 collective-permute-start.1
  89.1 22.8 %shard_map.104 = bf16[2048,4096]{1,0:T(8,128)(2,1)} custom-call(s32[8,128]{1,0:T(8,128)} %get-tuple-element.21.asked_ref, bf16[8,128,192]{2,1,0:T(8,128)(2,1)} %get-tuple-element.24.coef_ref, bf16[512,4096]{1,0:T(8,128)(2,1)} %bitcast.22), custom_call_target="tpu_custom_call" | custom-call | flops 25769803776 | bytes 16777216 | tf_op jit(solution)/shard_map/pallas_call | solution.py:332
  111.9 22.6 %shard_map.103 = bf16[2048,4096]{1,0:T(8,128)(2,1)} custom-call(s32[8,128]{1,0:T(8,128)} %get-tuple-element.21.asked_ref, bf16[8,128,192]{2,1,0:T(8,128)(2,1)} %get-tuple-element.22.coef_ref, bf16[512,4096]{1,0:T(8,128)(2,1)} %bitcast.21), custom_call_target="tpu_custom_call" | custom-call | flops 25769803776 | bytes 16777216 | tf_op jit(solution)/shard_map/pallas_call | solution.py:332
  134.6 0.8 collective-permute-done
  135.3 0.0 collective-permute-done.1
  135.3 4.0 %add_convert_fusion = bf16[128,4096]{1,0:T(8,128)(2,1)S(1)} fusion(f32[128,4096]{1,0:T(8,128)} %collective-permute-done, f32[128,4096]{1,0:T(8,128)} %collective-permute-done.1, f32[128,4096]{1,0:T(8,128)} %get-tuple-element.17, f32[128,4096]{1,0:T(8,128)} %get-tuple-element.18), kind=kLoop, calls=%fused_computation | loop fusion | flops 2097152 | bytes 9437184 | tf_op jit(solution)/shard_map/convert_element_type | solution.py:351
  139.3 0.1 fusion.3
  139.5 0.0 collective-permute-start.2
  139.5 1.9 %collective-permute-done.2 = bf16[64,2,2048]{2,0,1:T(8,128)(2,1)S(1)} collective-permute-done((bf16[64,2,2048]{2,0,1:T(8,128)(2,1)S(1)}, bf16[64,2,2048]{2,0,1:T(8,128)(2,1)S(1)}, u32[]{:S(2)}, u32[]{:S(2)}) %collective-permute-start.2) | collective-permute-done | bytes 524320 | tf_op jit(solution)/shard_map/ppermute | solution.py:329
  141.4 0.1 bitcast_select_fusion
  141.5 1.0 fusion.2
  (1 shorter events, 0.0 us)
Async XLA Ops:
  87.1 48.3 %collective-permute-start = (f32[128,4096]{1,0:T(8,128)}, f32[128,4096]{1,0:T(8,128)}, u32[]{:S(2)}, u32[]{:S(2)}) collective-permute-start(f32[128,4096]{1,0:T(8,128)} %get-tuple-element.19), channel_id=1, source_target_pairs={{0,4},{1,3},{2,6},{3,1},{4,0},{5,7},{6,2},{7,5}} | collective-permute-start | bytes 6291464 | tf_op jit(solution)/shard_map/ppermute | solution.py:329
  88.3 47.1 %collective-permute-start.1 = (f32[128,4096]{1,0:T(8,128)}, f32[128,4096]{1,0:T(8,128)}, u32[]{:S(2)}, u32[]{:S(2)}) collective-permute-start(f32[128,4096]{1,0:T(8,128)} %get-tuple-element.20), channel_id=1, source_target_pairs={{0,2},{1,5},{2,0},{3,7},{4,6},{5,1},{6,4},{7,3}} | collective-permute-start | bytes 6291464 | tf_op jit(solution)/shard_map/ppermute | solution.py:329
  139.5 1.9 %collective-permute-start.2 = (bf16[64,2,2048]{2,0,1:T(8,128)(2,1)S(1)}, bf16[64,2,2048]{2,0,1:T(8,128)(2,1)S(1)}, u32[]{:S(2)}, u32[]{:S(2)}) collective-permute-start(bf16[64,2,2048]{2,0,1:T(8,128)(2,1)S(1)} %bitcast.18), channel_id=1, source_target_pairs={{0,1},{1,0},{2,3},{3,2},{4,5},{5,4},{6,7},{7,6}} | collective-permute-start | bytes 1572872 | tf_op jit(solution)/shard_map/ppermute | solution.py:329

commit v6 on v5

--- a/solution.py
+++ b/solution.py
@@ -34,10 +34,12 @@
 
 
 N_COPIES = 64
+SIDE_STEP, FAR_STEP, REST_STEP = 1, 4, 6
+COLS = 512
 
 
 def layer_kernel(x_ref, dy_ref, slot_ref, gate_ref, req_ref, up_ref, down_ref,
-                 x_out, dy_out, c_out, w_out, asked_out, first_sum, second_sum, own_mine, own_got,
+                 x_out, dy_out, c_out, w_out, asked_out, first_sum, second_sum, own_sum,
                  x_all, dy_all, slot_all, gate_all, up_rows, down_rows, pair_recv, hop_recv, asked, asked_s, slot_t, w_t, c_t,
                  send_sem, recv_sem, own_sem, smem_sem, in_sem, out_sem):
     me = lax.axis_index("ep")
@@ -68,7 +70,9 @@
         for spec in specs:
             descriptor(*spec).wait_send()
 
-    own = [pltpu.make_async_copy(src, dst.at[0], own_sem.at[k]) for k, (src, dst) in enumerate(((x_ref, x_all), (dy_ref, dy_all), (slot_ref, slot_all), (gate_ref, gate_all)))]
+    own = [pltpu.make_async_copy(src, dst.at[0], own_sem.at[k]) for k, (src, dst) in enumerate(((x_ref, x_all), (dy_ref, dy_all)))]
+    slot_all[0] = slot_ref[...].reshape(SEL, TOK).T
+    gate_all[0] = gate_ref[...].reshape(SEL, TOK).T
     barrier = pltpu.get_barrier_semaphore()
     for b in range(1, N_DEV):
         pl.semaphore_signal(barrier, inc=1, device_id={"ep": me ^ b}, device_id_type=MESH)
@@ -77,16 +81,10 @@
     pl.semaphore_wait(barrier, N_DEV - 1)
 
     asks = [push(req_ref, (0, pl.ds(me ^ b, 1)), asked, pl.ds(b, 1), b) for b in range(1, N_DEV)]
-    first = [
-        push(gate_ref, None, gate_all, 4, 4), push(slot_ref, None, slot_all, 2, 2),
-        push(x_ref, None, x_all, 4, 4), push(dy_ref, None, dy_all, 2, 2),
-    ]
-    near_own = [push(gate_ref, None, gate_all, 1, 1), push(slot_ref, None, slot_all, 1, 1), push(x_ref, None, x_all, 1, 1), push(dy_ref, None, dy_all, 1, 1)]
+    first = [push(x_ref, None, x_all, 4, 4), push(dy_ref, None, dy_all, 2, 2)]
+    near_own = [push(x_ref, None, x_all, 1, 1), push(dy_ref, None, dy_all, 1, 1)]
     low, top = pl.ds(0, TOK // 2), pl.ds(TOK // 2, TOK // 2)
-    second = [
-        push(gate_ref, None, gate_all, 2, 2), push(slot_ref, None, slot_all, 4, 4),
-        push(x_ref, low, x_all, (2, low), 2), push(dy_ref, low, dy_all, (4, low), 4),
-    ]
+    second = [push(x_ref, low, x_all, (2, low), 2), push(dy_ref, low, dy_all, (4, low), 4)]
     asked[pl.ds(0, 1), :] = req_ref[0, pl.ds(me, 1), :]
     arrive(asks)
     asked_out[...] = asked[...]
@@ -102,14 +100,19 @@
         fetch(0).start()
         fetch(1).start()
         for k in range(len(steps)):
-            if k == len(steps) // 2:
+            if k == SIDE_STEP:
+                side = [push(gate_all, 0, gate_all, 4, 4), push(slot_all, 0, slot_all, 2, 2)]
+                near_own.extend([push(gate_all, 0, gate_all, 1, 1), push(slot_all, 0, slot_all, 1, 1)])
+            if k == FAR_STEP:
                 arrive(first)
-                far = [
-                    push(gate_all, 4, gate_all, 6, 2), push(slot_all, 2, slot_all, 6, 4),
-                    push(x_all, 4, x_all, 6, 2), push(dy_all, 2, dy_all, 6, 4),
-                ]
+                far = [push(x_all, 4, x_all, 6, 2), push(dy_all, 2, dy_all, 6, 4)]
+                near_first = [push(x_all, 4, x_all, 5, 1), push(dy_all, 2, dy_all, 3, 1)]
+            if k == REST_STEP:
+                arrive(side)
+                far.extend([push(gate_all, 4, gate_all, 6, 2), push(slot_all, 2, slot_all, 6, 4)])
+                near_first.extend([push(gate_all, 4, gate_all, 5, 1), push(slot_all, 2, slot_all, 3, 1)])
+                second.extend([push(gate_all, 0, gate_all, 2, 2), push(slot_all, 0, slot_all, 4, 4)])
                 second.extend([push(x_ref, top, x_all, (2, top), 2), push(dy_ref, top, dy_all, (4, top), 4)])
-                near_first = [push(gate_all, 4, gate_all, 5, 1), push(slot_all, 2, slot_all, 3, 1), push(x_all, 4, x_all, 5, 1), push(dy_all, 2, dy_all, 3, 1)]
             fetch(k).wait()
 
             def fill(t, _):
@@ -155,7 +158,7 @@
     row_iota = lax.broadcasted_iota(I32, (SLOTS, PAIR), 0)
     block_diag = (lax.broadcasted_iota(I32, (PAIR, 2 * SLOTS), 0) < TOK) == (lax.broadcasted_iota(I32, (PAIR, 2 * SLOTS), 1) < SLOTS)
 
-    def block(r, mine, other):
+    def front(r):
         toks, rows = pl.ds(2 * r, 2), pl.ds(2 * r * SLOTS, 2 * SLOTS)
 
         def dots(tok, table):
@@ -192,46 +195,57 @@
             both = jnp.concatenate([acc.T, acc.T], axis=1)
             return split3(jnp.where(block_diag, both, 0.0))
 
-        w_terms, c_terms = spread(acc_w), spread(acc_c)
-        for col in range(0, half, 512):
-            for shift, terms, table in ((0, w_terms, down_rows), (half, c_terms, up_rows)):
-                here = pl.ds(pl.multiple_of(core * half + col, 512), 512)
-                there = pl.ds(pl.multiple_of((1 - core) * half + col, 512), 512)
-                dst = slice(shift + col, shift + col + 512)
-                mine[:, dst] = sum(jnp.dot(term, table[rows, here], preferred_element_type=F32) for term in terms)
-                part = sum(jnp.dot(term, table[rows, there], preferred_element_type=F32) for term in terms)
-                other[:TOK, dst] = part[TOK:]
-                other[TOK:, dst] = part[:TOK]
-
-    def add_into(dst, src):
+        return spread(acc_w), spread(acc_c)
+
+    def columns(r, terms, col, mine, other):
+        rows = pl.ds(2 * r * SLOTS, 2 * SLOTS)
+        table, terms = (down_rows, terms[0]) if col < half else (up_rows, terms[1])
+        here = pl.ds(pl.multiple_of(core * half + col % half, COLS), COLS)
+        there = pl.ds(pl.multiple_of((1 - core) * half + col % half, COLS), COLS)
+        mine[:, col:col + COLS] = sum(jnp.dot(term, table[rows, here], preferred_element_type=F32) for term in terms)
+        part = sum(jnp.dot(term, table[rows, there], preferred_element_type=F32) for term in terms)
+        other[:TOK, col:col + COLS] = part[TOK:]
+        other[TOK:, col:col + COLS] = part[:TOK]
+
+    def block(r, mine, other):
+        terms = front(r)
+        for col in range(0, width, COLS):
+            columns(r, terms, col, mine, other)
+
+    def add_into(dst, src, cols=slice(None), step=16):
         def add(t, _):
-            r = pl.ds(pl.multiple_of(t * 16, 16), 16)
-            dst[r, :] = dst[r, :] + src[r, :]
+            r = pl.ds(pl.multiple_of(t * step, step), step)
+            dst[r, cols] = dst[r, cols] + src[r, cols]
             return 0
 
-        lax.fori_loop(0, PAIR // 16, add, 0)
+        lax.fori_loop(0, PAIR // step, add, 0)
 
     def blocks(mine, other):
         save = lambda src, dst, k: pltpu.make_async_copy(src, dst, out_sem.at[k])
         arrive(far)
         near_far = [push(ref, 6, ref, 7, 1) for ref in (gate_all, slot_all, x_all, dy_all)]
         arrive(near_own + near_first + near_far)
-        block(3, mine.at[3], other.at[0])
-        pair_far = push(other, 0, pair_recv, 0, 1)
+        terms = front(3)
+        pair_far, hop = [], []
+        chunks = [pl.ds(col, COLS) for col in range(0, width, COLS)]
+        every = slice(None)
+        for cols in chunks:
+            columns(3, terms, cols.start, mine.at[3], other.at[0])
+            pair_far.append(push(other, (0, every, cols), pair_recv, (0, every, cols), 1))
+        for k, cols in enumerate(chunks):
+            arrive([pair_far[k]])
+            add_into(mine.at[3], pair_recv.at[0], cols, 64)
+            hop.append(push(mine, (3, every, cols), hop_recv, (every, cols), 2 + 2 * core))
         block(0, mine.at[0], other.at[1])
-        pair_own = push(other, 1, own_got, None, 1)
-        saves = [save(mine.at[0], own_mine, 0)]
-        saves[0].start()
-        arrive([pair_far])
-        add_into(mine.at[3], pair_recv.at[0])
-        hop = push(mine, 3, hop_recv, None, 2 + 2 * core)
+        pair_own = push(other, 1, pair_recv, 3, 1)
+        saves = []
         arrive(second)
         near_second = [push(gate_all, 2, gate_all, 3, 1), push(slot_all, 4, slot_all, 5, 1), push(x_all, 2, x_all, 3, 1), push(dy_all, 4, dy_all, 5, 1)]
         arrive(near_second)
         for k, (src, dst) in enumerate(((x_all, x_out), (dy_all, dy_out))):
             saves.append(save(src, dst, 1 + k))
             saves[-1].start()
-        leave([pair_far])
+        leave(pair_far)
         block(1, mine.at[1], other.at[0])
         pair_x = push(other, 0, pair_recv, 1, 1)
         leave([pair_own])
@@ -243,12 +257,16 @@
         add_into(mine.at[2], pair_recv.at[2])
         saves.append(save(mine.at[1 + core], first_sum, 3))
         saves[-1].start()
-        arrive([hop])
-        add_into(mine.at[2 - core], hop_recv)
+        arrive([pair_own])
+        add_into(mine.at[0], pair_recv.at[3])
+        saves.append(save(mine.at[0], own_sum, 0))
+        saves[-1].start()
+        for k, cols in enumerate(chunks):
+            arrive([hop[k]])
+            add_into(mine.at[2 - core], hop_recv, cols, 64)
         saves.append(save(mine.at[2 - core], second_sum, 4))
         saves[-1].start()
-        arrive([pair_own])
-        leave([spec for spec in sent if spec is not pair_far and spec is not pair_own])
+        leave([spec for spec in sent if spec not in pair_far and spec is not pair_own])
         for copy in saves:
             copy.wait()
 
@@ -304,24 +322,24 @@
         vmem, anyw = pl.BlockSpec(memory_space=pltpu.VMEM), pl.BlockSpec(memory_space=pl.ANY)
         shape = jax.ShapeDtypeStruct
         sums = shape((PAIR, width), F32)
-        x_all, dy_all, c_terms, w_terms, asked, first_sum, second_sum, own_mine, own_got = pl.pallas_call(
+        x_all, dy_all, c_terms, w_terms, asked, first_sum, second_sum, own_sum = pl.pallas_call(
             layer_kernel,
             in_specs=[anyw, anyw, vmem, vmem, vmem, anyw, anyw],
-            out_specs=[anyw] * 2 + [vmem] * 3 + [anyw] * 4,
-            out_shape=[shape((N_DEV, TOK, width), BF16)] * 2 + [shape((N_DEV, SLOTS, TERMS * TOK), BF16)] * 2 + [shape((N_DEV, SLOTS), I32)] + [sums] * 4,
+            out_specs=[anyw] * 2 + [vmem] * 3 + [anyw] * 3,
+            out_shape=[shape((N_DEV, TOK, width), BF16)] * 2 + [shape((N_DEV, SLOTS, TERMS * TOK), BF16)] * 2 + [shape((N_DEV, SLOTS), I32)] + [sums] * 3,
             scratch_shapes=[
                 pltpu.VMEM((N_DEV, TOK, width), BF16), pltpu.VMEM((N_DEV, TOK, width), BF16),
                 pltpu.VMEM((N_DEV, TOK, SEL), I32), pltpu.VMEM((N_DEV, TOK, SEL), F32),
                 pltpu.VMEM((N_DEV * SLOTS, width), BF16), pltpu.VMEM((N_DEV * SLOTS, width), BF16),
-                pltpu.VMEM((3, PAIR, width), F32), pltpu.VMEM((PAIR, width), F32),
+                pltpu.VMEM((4, PAIR, width), F32), pltpu.VMEM((PAIR, width), F32),
                 pltpu.VMEM((N_DEV, SLOTS), I32), pltpu.SMEM((N_DEV, SLOTS), I32),
                 pltpu.VMEM((SEL, PAIR), I32), pltpu.VMEM((SEL, PAIR), F32), pltpu.VMEM((SEL, PAIR), F32),
                 pltpu.SemaphoreType.DMA((N_COPIES,)), pltpu.SemaphoreType.DMA((N_COPIES,)),
-                pltpu.SemaphoreType.DMA((4,)), pltpu.SemaphoreType.DMA,
+                pltpu.SemaphoreType.DMA((2,)), pltpu.SemaphoreType.DMA,
                 pltpu.SemaphoreType.DMA((2,)), pltpu.SemaphoreType.DMA((5,)),
             ],
             compiler_params=pltpu.CompilerParams(collective_id=0, has_side_effects=True, vmem_limit_bytes=VMEM_BYTES),
-        )(tokens, grad_out, slot_ids.reshape(TOK, SEL), gate_vals.reshape(TOK, SEL), request_rows, up_local, down_local)
+        )(tokens, grad_out, slot_ids.transpose(1, 2, 0), gate_vals.transpose(1, 2, 0), request_rows, up_local, down_local)
 
         partner = [(i, i ^ 1) for i in range(N_DEV)]
         first_hop = [(i, i ^ (2 if i % 2 == 0 else 4)) for i in range(N_DEV)]
@@ -348,8 +366,7 @@
         grad_up = grad_rows(c_terms, x_all)
         grad_down = grad_rows(w_terms, dy_all)
         got_last, got_own, grad_up, grad_down = lax.optimization_barrier((got_last, got_own, grad_up, grad_down))
-        final = (own_mine + own_got + got_own + got_last).astype(BF16).reshape(2, TOK, 2, half)
-        keep, give = final[0], final[1]
+        keep, give = [(own_sum[rows] + got_own[rows] + got_last[rows]).astype(BF16).reshape(TOK, 2, half) for rows in (slice(0, TOK), slice(TOK, PAIR))]
         back = hop(give, partner)
         low = jnp.where(core == 0, keep, back)
         high = jnp.where(core == 0, back, keep)

time: 143 us -> 138 us (0.965)
  local copies, waits for them, and re-layouts: 3.2 us -> 0.04 us
    reshape x2 -> x1, local copies, waits for them, and re-layouts: 3.07 us -> 0.04 us  [per_device(): (own_sum[rows] + got_own[rows] + got_last[rows]).astype(BF16)]
  transfers between devices with their start and end apart: 3 -> 3, of which waited for: 2 -> 1; matrix products, arithmetic and copies ran while one was open for 0% -> 0% of each run, Pallas kernels for 32% -> 33%
where the time goes in v6:
time: 138 us
  Pallas kernels  128 us (93%)
  other arithmetic  4.26 us (3%)
  starting transfers between devices  3.16 us (2%)
  waiting for transfers between devices  1.76 us (1%)
    pallas_call x1, Pallas kernels, per_device(): pl.pallas_call(layer_kernel, in_specs=[anyw, anyw, vmem, vmem, vmem, anyw...  82.6 us
    pallas_call x2, Pallas kernels, grad_rows(): pl.pallas_call(row_kernel, grid_spec=pltpu.PrefetchScalarGridSpec(num_sca...  45.3 us
    ppermute x3, starting transfers between devices, per_device(): hop = lambda value, pairs: lax.ppermute(value, 'ep', pairs)  3.16 us
    convert_element_type x1, other arithmetic, per_device(): (own_sum[rows] + got_own[rows] + got_last[rows]).astype(BF16)  3.15 us
  transfers between devices with their start and end apart: 3, of which 1 were waited for; matrix products, arithmetic and copies ran while one was open for 0% of the time, Pallas kernels for 33%

profile of v6, /device:TPU:0, one launch (start us, length us, event | category | flops | bytes accessed | tf_op | source)
XLA Modules:
  0.0 137.7 jit_solution(15978873988524003226)
XLA Ops:
  0.6 82.6 %shard_map.102 = (bf16[8,64,4096]{2,1,0:T(8,128)(2,1)}, bf16[8,64,4096]{2,1,0:T(8,128)(2,1)}, bf16[8,128,192]{2,1,0:T(8,128)(2,1)}, bf16[8,128,192]{2,1,0:T(8,12...) custom-call(bf16[64,4096]{1,0:T(8,128)(2,1)} %x_ref.1, ...), custom_call_target="tpu_custom_call" | custom-call | tf_op jit(solution)/shard_map/pallas_call | solution.py:325
  83.2 1.5 %collective-permute-start = (f32[128,4096]{1,0:T(8,128)}, f32[128,4096]{1,0:T(8,128)}, u32[]{:S(2)}, u32[]{:S(2)}) collective-permute-start(f32[128,4096]{1,0:T(8,128)} %get-tuple-element.17), channel_id=1, source_target_pairs={{0,4},{1,3},{2,6},{3,1},{4,0},{5,7},{6,2},{7,5}} | collective-permute-start | bytes 6291464 | tf_op jit(solution)/shard_map/ppermute | solution.py:347
  84.7 1.5 %collective-permute-start.1 = (f32[128,4096]{1,0:T(8,128)}, f32[128,4096]{1,0:T(8,128)}, u32[]{:S(2)}, u32[]{:S(2)}) collective-permute-start(f32[128,4096]{1,0:T(8,128)} %get-tuple-element.18), channel_id=1, source_target_pairs={{0,2},{1,5},{2,0},{3,7},{4,6},{5,1},{6,4},{7,3}} | collective-permute-start | bytes 6291464 | tf_op jit(solution)/shard_map/ppermute | solution.py:347
  86.2 22.6 %shard_map.104 = bf16[2048,4096]{1,0:T(8,128)(2,1)} custom-call(s32[8,128]{1,0:T(8,128)} %get-tuple-element.19.asked_ref, bf16[8,128,192]{2,1,0:T(8,128)(2,1)} %get-tuple-element.22.coef_ref, bf16[512,4096]{1,0:T(8,128)(2,1)} %bitcast.22), custom_call_target="tpu_custom_call" | custom-call | flops 25769803776 | bytes 16777216 | tf_op jit(solution)/shard_map/pallas_call | solution.py:350
  108.8 22.6 %shard_map.103 = bf16[2048,4096]{1,0:T(8,128)(2,1)} custom-call(s32[8,128]{1,0:T(8,128)} %get-tuple-element.19.asked_ref, bf16[8,128,192]{2,1,0:T(8,128)(2,1)} %get-tuple-element.20.coef_ref, bf16[512,4096]{1,0:T(8,128)(2,1)} %bitcast.21), custom_call_target="tpu_custom_call" | custom-call | flops 25769803776 | bytes 16777216 | tf_op jit(solution)/shard_map/pallas_call | solution.py:350
  131.5 0.0 collective-permute-done
  131.5 0.0 collective-permute-done.1
  131.5 3.1 %add_convert_fusion.1 = (bf16[64,4096]{1,0:T(8,128)(2,1)S(1)}, bf16[64,4096]{1,0:T(8,128)(2,1)S(1)}) fusion(f32[128,4096]{1,0:T(8,128)} %collective-permute-done, f32[128,4096]{1,0:T(8,128)} %collective-permute-done.1, f32[128,4096]{1,0:T(8,128)} %get-tuple-element.16), kind=kLoop, calls=%fused_computation.3 | loop fusion | flops 1572864 | bytes 7340032 | tf_op jit(solution)/shard_map/convert_element_type | solution.py:369
  134.7 0.2 collective-permute-start.2
  134.9 1.8 %collective-permute-done.2 = bf16[64,2,2048]{2,0,1:T(8,128)(2,1)S(1)} collective-permute-done((bf16[64,2,2048]{2,0,1:T(8,128)(2,1)S(1)}, bf16[64,2,2048]{2,0,1:T(8,128)(2,1)S(1)}, u32[]{:S(2)}, u32[]{:S(2)}) %collective-permute-start.2) | collective-permute-done | bytes 524320 | tf_op jit(solution)/shard_map/ppermute | solution.py:347
  136.6 0.1 bitcast_select_fusion
  136.7 1.0 fusion.2
  (1 shorter events, 0.0 us)
Async XLA Ops:
  83.2 48.2 %collective-permute-start = (f32[128,4096]{1,0:T(8,128)}, f32[128,4096]{1,0:T(8,128)}, u32[]{:S(2)}, u32[]{:S(2)}) collective-permute-start(f32[128,4096]{1,0:T(8,128)} %get-tuple-element.17), channel_id=1, source_target_pairs={{0,4},{1,3},{2,6},{3,1},{4,0},{5,7},{6,2},{7,5}} | collective-permute-start | bytes 6291464 | tf_op jit(solution)/shard_map/ppermute | solution.py:347
  84.7 46.7 %collective-permute-start.1 = (f32[128,4096]{1,0:T(8,128)}, f32[128,4096]{1,0:T(8,128)}, u32[]{:S(2)}, u32[]{:S(2)}) collective-permute-start(f32[128,4096]{1,0:T(8,128)} %get-tuple-element.18), channel_id=1, source_target_pairs={{0,2},{1,5},{2,0},{3,7},{4,6},{5,1},{6,4},{7,3}} | collective-permute-start | bytes 6291464 | tf_op jit(solution)/shard_map/ppermute | solution.py:347
  134.7 1.9 %collective-permute-start.2 = (bf16[64,2,2048]{2,0,1:T(8,128)(2,1)S(1)}, bf16[64,2,2048]{2,0,1:T(8,128)(2,1)S(1)}, u32[]{:S(2)}, u32[]{:S(2)}) collective-permute-start(bf16[64,2,2048]{2,0,1:T(8,128)(2,1)S(1)} %bitcast.18), channel_id=1, source_target_pairs={{0,1},{1,0},{2,3},{3,2},{4,5},{5,4},{6,7},{7,6}} | collective-permute-start | bytes 1572872 | tf_op jit(solution)/shard_map/ppermute | solution.py:347

commit v7 on v6

--- a/solution.py
+++ b/solution.py
@@ -11,8 +11,9 @@
 N_DEV, TOK, SLOTS, SEL = 8, 64, 128, 128
 PAIR = 2 * TOK
 TERMS = 3
-CHUNK = 1024
+CHUNK = 2048
 ROW_CHUNK = 2048
+LOW = 16
 LANES = 128
 PAD = 4
 VMEM_BYTES = 62 * 1024 * 1024
@@ -48,7 +49,7 @@
     half = width // 2
     steps = [(ref, out, col) for ref, out in ((up_ref, up_rows), (down_ref, down_rows)) for col in range(0, width, CHUNK)]
     tiles = CHUNK // LANES
-    wide_step, pick_step = n_rows + PAD, N_DEV * SLOTS + PAD
+    wide_step, pick_step = n_rows + PAD, SLOTS + PAD
     sent = []
 
     def descriptor(k, src, dst, mask):
@@ -83,7 +84,7 @@
     asks = [push(req_ref, (0, pl.ds(me ^ b, 1)), asked, pl.ds(b, 1), b) for b in range(1, N_DEV)]
     first = [push(x_ref, None, x_all, 4, 4), push(dy_ref, None, dy_all, 2, 2)]
     near_own = [push(x_ref, None, x_all, 1, 1), push(dy_ref, None, dy_all, 1, 1)]
-    low, top = pl.ds(0, TOK // 2), pl.ds(TOK // 2, TOK // 2)
+    low, top = pl.ds(0, LOW), pl.ds(LOW, TOK - LOW)
     second = [push(x_ref, low, x_all, (2, low), 2), push(dy_ref, low, dy_all, (4, low), 4)]
     asked[pl.ds(0, 1), :] = req_ref[0, pl.ds(me, 1), :]
     arrive(asks)
@@ -95,61 +96,64 @@
     def gather_all(table, wide, picked):
         def fetch(k):
             ref, _, col = steps[k]
-            return pltpu.make_async_copy(ref.at[:, pl.ds(col, CHUNK)], table.at[k % 2], in_sem.at[k % 2])
+            return pltpu.make_async_copy(ref.at[:, pl.ds(col, CHUNK)], table, in_sem.at[0])
 
         fetch(0).start()
-        fetch(1).start()
-        for k in range(len(steps)):
-            if k == SIDE_STEP:
+        for sub in range(2 * len(steps)):
+            if sub == SIDE_STEP:
                 side = [push(gate_all, 0, gate_all, 4, 4), push(slot_all, 0, slot_all, 2, 2)]
                 near_own.extend([push(gate_all, 0, gate_all, 1, 1), push(slot_all, 0, slot_all, 1, 1)])
-            if k == FAR_STEP:
+            if sub == FAR_STEP:
                 arrive(first)
                 far = [push(x_all, 4, x_all, 6, 2), push(dy_all, 2, dy_all, 6, 4)]
                 near_first = [push(x_all, 4, x_all, 5, 1), push(dy_all, 2, dy_all, 3, 1)]
-            if k == REST_STEP:
+            if sub == REST_STEP:
                 arrive(side)
                 far.extend([push(gate_all, 4, gate_all, 6, 2), push(slot_all, 2, slot_all, 6, 4)])
                 near_first.extend([push(gate_all, 4, gate_all, 5, 1), push(slot_all, 2, slot_all, 3, 1)])
                 second.extend([push(gate_all, 0, gate_all, 2, 2), push(slot_all, 0, slot_all, 4, 4)])
                 second.extend([push(x_ref, top, x_all, (2, top), 2), push(dy_ref, top, dy_all, (4, top), 4)])
-            fetch(k).wait()
-
-            def fill(t, _):
-                r = pl.multiple_of(t * 32, 32)
-                for j in range(tiles):
-                    wide[pl.ds(j * wide_step + r, 32), :] = table[k % 2, pl.ds(r, 32), j * LANES:(j + 1) * LANES].astype(F32)
-                return 0
-
-            lax.fori_loop(0, n_rows // 32, fill, 0)
-            if k + 2 < len(steps):
-                fetch(k + 2).start()
-
-            def pick_device(b, _):
-                def pick(t, _):
-                    for u in range(16):
-                        row = asked_s[b, t * 16 + u]
-                        picked[pl.ds(b * SLOTS + t * 16 + u, tiles, stride=pick_step), :] = wide[pl.ds(row, tiles, stride=wide_step), :]
+            k = sub // 2
+            if sub % 2 == 0:
+                fetch(k).wait()
+
+                def fill(t, _):
+                    r = pl.multiple_of(t * 32, 32)
+                    for j in range(tiles):
+                        wide[pl.ds(j * wide_step + r, 32), :] = table[pl.ds(r, 32), j * LANES:(j + 1) * LANES].astype(F32)
                     return 0
 
-                return lax.fori_loop(0, SLOTS // 16, pick, 0)
-
-            lax.fori_loop(0, N_DEV, pick_device, 0)
-            _, rows_ref, col = steps[k]
-
-            def drain(t, _):
-                r = pl.multiple_of(t * 32, 32)
-                for j in range(tiles):
-                    rows_ref[pl.ds(r, 32), col + j * LANES:col + (j + 1) * LANES] = picked[pl.ds(j * pick_step + r, 32), :].astype(BF16)
-                return 0
-
-            lax.fori_loop(0, N_DEV * SLOTS // 32, drain, 0)
+                lax.fori_loop(0, n_rows // 32, fill, 0)
+                if k + 1 < len(steps):
+                    fetch(k + 1).start()
+            else:
+                _, rows_ref, col = steps[k]
+
+                def pick_device(b, _):
+                    def pick(t, _):
+                        for u in range(16):
+                            row = asked_s[b, t * 16 + u]
+                            picked[pl.ds(t * 16 + u, tiles, stride=pick_step), :] = wide[pl.ds(row, tiles, stride=wide_step), :]
+                        return 0
+
+                    lax.fori_loop(0, SLOTS // 16, pick, 0)
+
+                    def drain(t, _):
+                        r = pl.multiple_of(t * 32, 32)
+                        into = pl.multiple_of(b * SLOTS + t * 32, 32)
+                        for j in range(tiles):
+                            rows_ref[pl.ds(into, 32), col + j * LANES:col + (j + 1) * LANES] = picked[pl.ds(j * pick_step + r, 32), :].astype(BF16)
+                        return 0
+
+                    return lax.fori_loop(0, SLOTS // 32, drain, 0)
+
+                lax.fori_loop(0, N_DEV, pick_device, 0)
         return far, near_first
 
     kept = []
     pl.run_scoped(
         lambda *bufs: kept.append(gather_all(*bufs)),
-        pltpu.VMEM((2, n_rows, CHUNK), BF16), pltpu.VMEM((tiles * wide_step, LANES), F32), pltpu.VMEM((tiles * pick_step, LANES), F32),
+        pltpu.VMEM((n_rows, CHUNK), BF16), pltpu.VMEM((tiles * wide_step, LANES), F32), pltpu.VMEM((tiles * pick_step, LANES), F32),
     )
     far, near_first = kept[0]
     for copy in own:
@@ -222,9 +226,12 @@
 
     def blocks(mine, other):
         save = lambda src, dst, k: pltpu.make_async_copy(src, dst, out_sem.at[k])
+        arrive(near_own)
+        block(0, mine.at[0], other.at[1])
+        pair_own = push(other, 1, pair_recv, 3, 1)
         arrive(far)
         near_far = [push(ref, 6, ref, 7, 1) for ref in (gate_all, slot_all, x_all, dy_all)]
-        arrive(near_own + near_first + near_far)
+        arrive(near_first + near_far)
         terms = front(3)
         pair_far, hop = [], []
         chunks = [pl.ds(col, COLS) for col in range(0, width, COLS)]
@@ -236,9 +243,11 @@
             arrive([pair_far[k]])
             add_into(mine.at[3], pair_recv.at[0], cols, 64)
             hop.append(push(mine, (3, every, cols), hop_recv, (every, cols), 2 + 2 * core))
-        block(0, mine.at[0], other.at[1])
-        pair_own = push(other, 1, pair_recv, 3, 1)
         saves = []
+        arrive([pair_own])
+        add_into(mine.at[0], pair_recv.at[3])
+        saves.append(save(mine.at[0], own_sum, 0))
+        saves[-1].start()
         arrive(second)
         near_second = [push(gate_all, 2, gate_all, 3, 1), push(slot_all, 4, slot_all, 5, 1), push(x_all, 2, x_all, 3, 1), push(dy_all, 4, dy_all, 5, 1)]
         arrive(near_second)
@@ -256,10 +265,6 @@
         arrive([pair_y])
         add_into(mine.at[2], pair_recv.at[2])
         saves.append(save(mine.at[1 + core], first_sum, 3))
-        saves[-1].start()
-        arrive([pair_own])
-        add_into(mine.at[0], pair_recv.at[3])
-        saves.append(save(mine.at[0], own_sum, 0))
         saves[-1].start()
         for k, cols in enumerate(chunks):
             arrive([hop[k]])
@@ -336,7 +341,7 @@
                 pltpu.VMEM((SEL, PAIR), I32), pltpu.VMEM((SEL, PAIR), F32), pltpu.VMEM((SEL, PAIR), F32),
                 pltpu.SemaphoreType.DMA((N_COPIES,)), pltpu.SemaphoreType.DMA((N_COPIES,)),
                 pltpu.SemaphoreType.DMA((2,)), pltpu.SemaphoreType.DMA,
-                pltpu.SemaphoreType.DMA((2,)), pltpu.SemaphoreType.DMA((5,)),
+                pltpu.SemaphoreType.DMA((1,)), pltpu.SemaphoreType.DMA((5,)),
             ],
             compiler_params=pltpu.CompilerParams(collective_id=0, has_side_effects=True, vmem_limit_bytes=VMEM_BYTES),
         )(tokens, grad_out, slot_ids.transpose(1, 2, 0), gate_vals.transpose(1, 2, 0), request_rows, up_local, down_local)

time: 138 us -> 133 us (0.964)
  Pallas kernels: 128 us -> 123 us
    pallas_call x1, Pallas kernels: 82.6 us -> 77.6 us  [per_device(): pl.pallas_call(layer_kernel, in_specs=[anyw, anyw, vmem, vmem, vmem, anyw...]
  transfers between devices with their start and end apart: 3 -> 3, of which waited for: 1 -> 2; matrix products, arithmetic and copies ran while one was open for 0% -> 0% of each run, Pallas kernels for 33% -> 34%
where the time goes in v7:
time: 133 us
  Pallas kernels  123 us (92%)
  other arithmetic  4.25 us (3%)
  waiting for transfers between devices  2.82 us (2%)
  starting transfers between devices  2.08 us (2%)
    pallas_call x1, Pallas kernels, per_device(): pl.pallas_call(layer_kernel, in_specs=[anyw, anyw, vmem, vmem, vmem, anyw...  77.6 us
    pallas_call x2, Pallas kernels, grad_rows(): pl.pallas_call(row_kernel, grid_spec=pltpu.PrefetchScalarGridSpec(num_sca...  45.3 us
    convert_element_type x1, other arithmetic, per_device(): (own_sum[rows] + got_own[rows] + got_last[rows]).astype(BF16)  3.15 us
    ppermute x3, waiting for transfers between devices, per_device(): hop = lambda value, pairs: lax.ppermute(value, 'ep', pairs)  2.82 us
  transfers between devices with their start and end apart: 3, of which 2 were waited for; matrix products, arithmetic and copies ran while one was open for 0% of the time, Pallas kernels for 34%

profile of v7, /device:TPU:0, one launch (start us, length us, event | category | flops | bytes accessed | tf_op | source)
XLA Modules:
  0.0 132.8 jit_solution(7288292581540242161)
XLA Ops:
  0.6 77.6 %shard_map.102 = (bf16[8,64,4096]{2,1,0:T(8,128)(2,1)}, bf16[8,64,4096]{2,1,0:T(8,128)(2,1)}, bf16[8,128,192]{2,1,0:T(8,128)(2,1)}, bf16[8,128,192]{2,1,0:T(8,12...) custom-call(bf16[64,4096]{1,0:T(8,128)(2,1)} %x_ref.1, ...), custom_call_target="tpu_custom_call" | custom-call | tf_op jit(solution)/shard_map/pallas_call | solution.py:330
  78.2 1.2 collective-permute-start
  79.5 0.8 collective-permute-start.1
  80.3 22.6 %shard_map.104 = bf16[2048,4096]{1,0:T(8,128)(2,1)} custom-call(s32[8,128]{1,0:T(8,128)} %get-tuple-element.19.asked_ref, bf16[8,128,192]{2,1,0:T(8,128)(2,1)} %get-tuple-element.22.coef_ref, bf16[512,4096]{1,0:T(8,128)(2,1)} %bitcast.22), custom_call_target="tpu_custom_call" | custom-call | flops 25769803776 | bytes 16777216 | tf_op jit(solution)/shard_map/pallas_call | solution.py:355
  102.9 22.7 %shard_map.103 = bf16[2048,4096]{1,0:T(8,128)(2,1)} custom-call(s32[8,128]{1,0:T(8,128)} %get-tuple-element.19.asked_ref, bf16[8,128,192]{2,1,0:T(8,128)(2,1)} %get-tuple-element.20.coef_ref, bf16[512,4096]{1,0:T(8,128)(2,1)} %bitcast.21), custom_call_target="tpu_custom_call" | custom-call | flops 25769803776 | bytes 16777216 | tf_op jit(solution)/shard_map/pallas_call | solution.py:355
  125.6 0.9 collective-permute-done
  126.5 0.0 collective-permute-done.1
  126.5 3.1 %add_convert_fusion.1 = (bf16[64,4096]{1,0:T(8,128)(2,1)S(1)}, bf16[64,4096]{1,0:T(8,128)(2,1)S(1)}) fusion(f32[128,4096]{1,0:T(8,128)} %collective-permute-done, f32[128,4096]{1,0:T(8,128)} %collective-permute-done.1, f32[128,4096]{1,0:T(8,128)} %get-tuple-element.16), kind=kLoop, calls=%fused_computation.3 | loop fusion | flops 1572864 | bytes 7340032 | tf_op jit(solution)/shard_map/convert_element_type | solution.py:374
  129.7 0.0 collective-permute-start.2
  129.8 1.9 %collective-permute-done.2 = bf16[64,2,2048]{2,0,1:T(8,128)(2,1)S(1)} collective-permute-done((bf16[64,2,2048]{2,0,1:T(8,128)(2,1)S(1)}, bf16[64,2,2048]{2,0,1:T(8,128)(2,1)S(1)}, u32[]{:S(2)}, u32[]{:S(2)}) %collective-permute-start.2) | collective-permute-done | bytes 524320 | tf_op jit(solution)/shard_map/ppermute | solution.py:352
  131.7 0.1 bitcast_select_fusion
  131.7 1.0 fusion.2
  (1 shorter events, 0.0 us)
Async XLA Ops:
  78.2 48.3 %collective-permute-start = (f32[128,4096]{1,0:T(8,128)}, f32[128,4096]{1,0:T(8,128)}, u32[]{:S(2)}, u32[]{:S(2)}) collective-permute-start(f32[128,4096]{1,0:T(8,128)} %get-tuple-element.17), channel_id=1, source_target_pairs={{0,4},{1,3},{2,6},{3,1},{4,0},{5,7},{6,2},{7,5}} | collective-permute-start | bytes 6291464 | tf_op jit(solution)/shard_map/ppermute | solution.py:352
  79.5 47.0 %collective-permute-start.1 = (f32[128,4096]{1,0:T(8,128)}, f32[128,4096]{1,0:T(8,128)}, u32[]{:S(2)}, u32[]{:S(2)}) collective-permute-start(f32[128,4096]{1,0:T(8,128)} %get-tuple-element.18), channel_id=1, source_target_pairs={{0,2},{1,5},{2,0},{3,7},{4,6},{5,1},{6,4},{7,3}} | collective-permute-start | bytes 6291464 | tf_op jit(solution)/shard_map/ppermute | solution.py:352
  129.7 1.9 %collective-permute-start.2 = (bf16[64,2,2048]{2,0,1:T(8,128)(2,1)S(1)}, bf16[64,2,2048]{2,0,1:T(8,128)(2,1)S(1)}, u32[]{:S(2)}, u32[]{:S(2)}) collective-permute-start(bf16[64,2,2048]{2,0,1:T(8,128)(2,1)S(1)} %bitcast.18), channel_id=1, source_target_pairs={{0,1},{1,0},{2,3},{3,2},{4,5},{5,4},{6,7},{7,6}} | collective-permute-start | bytes 1572872 | tf_op jit(solution)/shard_map/ppermute | solution.py:352

commit v8 on v7

--- a/solution.py
+++ b/solution.py
@@ -12,7 +12,8 @@
 PAIR = 2 * TOK
 TERMS = 3
 CHUNK = 2048
-ROW_CHUNK = 2048
+ROW_CHUNK = 1024
+GROUP = 16
 LOW = 16
 LANES = 128
 PAD = 4
@@ -227,8 +228,6 @@
     def blocks(mine, other):
         save = lambda src, dst, k: pltpu.make_async_copy(src, dst, out_sem.at[k])
         arrive(near_own)
-        block(0, mine.at[0], other.at[1])
-        pair_own = push(other, 1, pair_recv, 3, 1)
         arrive(far)
         near_far = [push(ref, 6, ref, 7, 1) for ref in (gate_all, slot_all, x_all, dy_all)]
         arrive(near_first + near_far)
@@ -244,10 +243,6 @@
             add_into(mine.at[3], pair_recv.at[0], cols, 64)
             hop.append(push(mine, (3, every, cols), hop_recv, (every, cols), 2 + 2 * core))
         saves = []
-        arrive([pair_own])
-        add_into(mine.at[0], pair_recv.at[3])
-        saves.append(save(mine.at[0], own_sum, 0))
-        saves[-1].start()
         arrive(second)
         near_second = [push(gate_all, 2, gate_all, 3, 1), push(slot_all, 4, slot_all, 5, 1), push(x_all, 2, x_all, 3, 1), push(dy_all, 4, dy_all, 5, 1)]
         arrive(near_second)
@@ -257,58 +252,76 @@
         leave(pair_far)
         block(1, mine.at[1], other.at[0])
         pair_x = push(other, 0, pair_recv, 1, 1)
-        leave([pair_own])
         block(2, mine.at[2], other.at[1])
         pair_y = push(other, 1, pair_recv, 2, 1)
+        leave([pair_x])
+        block(0, mine.at[0], other.at[0])
+        pair_own = push(other, 0, pair_recv, 3, 1)
         arrive([pair_x])
         add_into(mine.at[1], pair_recv.at[1])
         arrive([pair_y])
         add_into(mine.at[2], pair_recv.at[2])
         saves.append(save(mine.at[1 + core], first_sum, 3))
         saves[-1].start()
+        arrive([pair_own])
+        add_into(mine.at[0], pair_recv.at[3])
+        saves.append(save(mine.at[0], own_sum, 0))
+        saves[-1].start()
         for k, cols in enumerate(chunks):
             arrive([hop[k]])
             add_into(mine.at[2 - core], hop_recv, cols, 64)
         saves.append(save(mine.at[2 - core], second_sum, 4))
         saves[-1].start()
-        leave([spec for spec in sent if spec not in pair_far and spec is not pair_own])
+        leave([spec for spec in sent if spec not in pair_far and spec is not pair_x])
         for copy in saves:
             copy.wait()
 
     pl.run_scoped(blocks, pltpu.VMEM((4, PAIR, width), F32), pltpu.VMEM((2, PAIR, width), F32))
 
 
-def row_kernel(asked_ref, coef_ref, x_ref, out_ref, wide, part):
-    n_rows, cols = out_ref.shape
+def row_kernel(asked_ref, c_ref, w_ref, x_ref, dy_ref, du_ref, dv_ref, wide_u, wide_v, part_u, part_v):
+    n_rows, cols = du_ref.shape
     tiles = cols // LANES
     wide_step, part_step = n_rows + PAD, SLOTS + PAD
+    part_size = tiles * part_step
 
     def clear(t, _):
         r = pl.multiple_of(t * 32, 32)
         for j in range(tiles):
-            wide[pl.ds(j * wide_step + r, 32), :] = jnp.zeros((32, LANES), F32)
+            for wide in (wide_u, wide_v):
+                wide[pl.ds(j * wide_step + r, 32), :] = jnp.zeros((32, LANES), F32)
         return 0
 
     lax.fori_loop(0, n_rows // 32, clear, 0)
-    for q in range(N_DEV):
-        tok = x_ref[q * TOK:(q + 1) * TOK, :]
-        full = jnp.dot(coef_ref[q], jnp.concatenate([tok] * TERMS, axis=0), preferred_element_type=F32)
-        for j in range(tiles):
-            part[pl.ds(j * part_step, SLOTS), :] = full[:, j * LANES:(j + 1) * LANES]
-
-        def add(t, _):
-            rows = [asked_ref[q, t * 16 + u] for u in range(16)]
-            sums = [wide[pl.ds(rows[u], tiles, stride=wide_step), :] + part[pl.ds(t * 16 + u, tiles, stride=part_step), :] for u in range(16)]
-            for u in range(16):
-                wide[pl.ds(rows[u], tiles, stride=wide_step), :] = sums[u]
-            return 0
-
-        lax.fori_loop(0, SLOTS // 16, add, 0)
+
+    def product(q, slot):
+        for coef, tok, part in ((c_ref, x_ref, part_u), (w_ref, dy_ref, part_v)):
+            rows = tok[pl.ds(pl.multiple_of(q * TOK, TOK), TOK), :]
+            full = jnp.dot(coef[q], jnp.concatenate([rows] * TERMS, axis=0), preferred_element_type=F32)
+            for j in range(tiles):
+                part[pl.ds(slot * part_size + j * part_step, SLOTS), :] = full[:, j * LANES:(j + 1) * LANES]
+
+    product(0, 0)
+
+    def device(q, _):
+        product(lax.rem(q + 1, N_DEV), lax.rem(q + 1, 2))
+        base = lax.rem(q, 2) * part_size
+        for t in range(0, SLOTS, GROUP):
+            rows = [asked_ref[q, t + u] for u in range(GROUP)]
+            sums = [[wide[pl.ds(row, tiles, stride=wide_step), :] + part[pl.ds(base + t + u, tiles, stride=part_step), :]
+                     for wide, part in ((wide_u, part_u), (wide_v, part_v))] for u, row in enumerate(rows)]
+            for row, pair in zip(rows, sums):
+                for wide, value in zip((wide_u, wide_v), pair):
+                    wide[pl.ds(row, tiles, stride=wide_step), :] = value
+        return 0
+
+    lax.fori_loop(0, N_DEV, device, 0)
 
     def drain(t, _):
         r = pl.multiple_of(t * 32, 32)
         for j in range(tiles):
-            out_ref[pl.ds(r, 32), j * LANES:(j + 1) * LANES] = wide[pl.ds(j * wide_step + r, 32), :].astype(BF16)
+            for wide, out in ((wide_u, du_ref), (wide_v, dv_ref)):
+                out[pl.ds(r, 32), j * LANES:(j + 1) * LANES] = wide[pl.ds(j * wide_step + r, 32), :].astype(BF16)
         return 0
 
     lax.fori_loop(0, n_rows // 32, drain, 0)
@@ -351,25 +364,28 @@
         second_hop = [(i, i ^ (4 if i % 2 == 0 else 2)) for i in range(N_DEV)]
         hop = lambda value, pairs: lax.ppermute(value, 'ep', pairs)
 
-        def grad_rows(coef, tok):
+        def grad_rows():
+            coef = pl.BlockSpec((N_DEV, SLOTS, TERMS * TOK), lambda i, a: (0, 0, 0))
+            tok = pl.BlockSpec((n_tok, ROW_CHUNK), lambda i, a: (0, i))
+            out = pl.BlockSpec((rows_owner, ROW_CHUNK), lambda i, a: (0, i))
+            tiles = ROW_CHUNK // LANES
             return pl.pallas_call(
                 row_kernel,
                 grid_spec=pltpu.PrefetchScalarGridSpec(
                     num_scalar_prefetch=1,
                     grid=(width // ROW_CHUNK,),
-                    in_specs=[pl.BlockSpec(coef.shape, lambda i, a: (0, 0, 0)), pl.BlockSpec((n_tok, ROW_CHUNK), lambda i, a: (0, i))],
-                    out_specs=pl.BlockSpec((rows_owner, ROW_CHUNK), lambda i, a: (0, i)),
-                    scratch_shapes=[pltpu.VMEM((ROW_CHUNK // LANES * (rows_owner + PAD), LANES), F32), pltpu.VMEM((ROW_CHUNK // LANES * (SLOTS + PAD), LANES), F32)],
+                    in_specs=[coef, coef, tok, tok],
+                    out_specs=[out, out],
+                    scratch_shapes=[pltpu.VMEM((tiles * (rows_owner + PAD), LANES), F32)] * 2 + [pltpu.VMEM((2 * tiles * (SLOTS + PAD), LANES), F32)] * 2,
                 ),
-                out_shape=shape((rows_owner, width), BF16),
+                out_shape=[shape((rows_owner, width), BF16)] * 2,
                 compiler_params=pltpu.CompilerParams(vmem_limit_bytes=VMEM_BYTES),
-                cost_estimate=pl.CostEstimate(flops=6 * rows_owner * width * n_tok, bytes_accessed=2 * rows_owner * width, transcendentals=0),
-            )(asked, coef, tok.reshape(n_tok, width))
+                cost_estimate=pl.CostEstimate(flops=12 * rows_owner * width * n_tok, bytes_accessed=4 * rows_owner * width, transcendentals=0),
+            )(asked, c_terms, w_terms, x_all.reshape(n_tok, width), dy_all.reshape(n_tok, width))
 
         got_own = hop(first_sum, first_hop)
         got_last = hop(second_sum, second_hop)
-        grad_up = grad_rows(c_terms, x_all)
-        grad_down = grad_rows(w_terms, dy_all)
+        grad_up, grad_down = grad_rows()
         got_last, got_own, grad_up, grad_down = lax.optimization_barrier((got_last, got_own, grad_up, grad_down))
         keep, give = [(own_sum[rows] + got_own[rows] + got_last[rows]).astype(BF16).reshape(TOK, 2, half) for rows in (slice(0, TOK), slice(TOK, PAIR))]
         back = hop(give, partner)

time: 133 us -> 130 us (0.977)
  Pallas kernels: 123 us -> 110 us
  waiting for transfers between devices: 2.82 us -> 12.4 us
    pallas_call x2 -> x1, Pallas kernels: 45.3 us -> 35.5 us  [grad_rows(): pl.pallas_call(row_kernel, grid_spec=pltpu.PrefetchScalarGridSpec(num_sca...]
    ppermute x3, waiting for transfers between devices: 2.82 us -> 12.4 us  [per_device(): hop = lambda value, pairs: lax.ppermute(value, 'ep', pairs)]
    pallas_call x1, Pallas kernels: 77.6 us -> 74.4 us  [per_device(): pl.pallas_call(layer_kernel, in_specs=[anyw, anyw, vmem, vmem, vmem, anyw...]
  transfers between devices with their start and end apart: 3 -> 3, of which waited for: 2 -> 2; matrix products, arithmetic and copies ran while one was open for 0% -> 0% of each run, Pallas kernels for 34% -> 27%
where the time goes in v8:
time: 130 us; the launch traced here: 129 us
  Pallas kernels  110 us (85%)
  waiting for transfers between devices  12.4 us (10%)
  other arithmetic  4.25 us (3%)
  starting transfers between devices  2.07 us (2%)
    pallas_call x1, Pallas kernels, per_device(): pl.pallas_call(layer_kernel, in_specs=[anyw, anyw, vmem, vmem, vmem, anyw...  74.4 us
    pallas_call x1, Pallas kernels, grad_rows(): pl.pallas_call(row_kernel, grid_spec=pltpu.PrefetchScalarGridSpec(num_sca...  35.5 us
    ppermute x3, waiting for transfers between devices, per_device(): hop = lambda value, pairs: lax.ppermute(value, 'ep', pairs)  12.4 us
    convert_element_type x1, other arithmetic, per_device(): (own_sum[rows] + got_own[rows] + got_last[rows]).astype(BF16)  3.15 us
  transfers between devices with their start and end apart: 3, of which 2 were waited for; matrix products, arithmetic and copies ran while one was open for 0% of the time, Pallas kernels for 27%

profile of v8, /device:TPU:0, one launch (start us, length us, event | category | flops | bytes accessed | tf_op | source)
XLA Modules:
  0.0 129.3 jit_solution(4787615410358243133)
XLA Ops:
  0.6 74.4 %shard_map.102 = (bf16[8,64,4096]{2,1,0:T(8,128)(2,1)}, bf16[8,64,4096]{2,1,0:T(8,128)(2,1)}, bf16[8,128,192]{2,1,0:T(8,128)(2,1)}, bf16[8,128,192]{2,1,0:T(8,12...) custom-call(bf16[64,4096]{1,0:T(8,128)(2,1)} %x_ref.1, ...), custom_call_target="tpu_custom_call" | custom-call | tf_op jit(solution)/shard_map/pallas_call | solution.py:343
  75.0 1.5 %collective-permute-start = (f32[128,4096]{1,0:T(8,128)}, f32[128,4096]{1,0:T(8,128)}, u32[]{:S(2)}, u32[]{:S(2)}) collective-permute-start(f32[128,4096]{1,0:T(8,128)} %get-tuple-element.19), channel_id=1, source_target_pairs={{0,4},{1,3},{2,6},{3,1},{4,0},{5,7},{6,2},{7,5}} | collective-permute-start | bytes 6291464 | tf_op jit(solution)/shard_map/ppermute | solution.py:365
  76.5 0.6 collective-permute-start.1
  77.1 35.5 %shard_map.103 = (bf16[2048,4096]{1,0:T(8,128)(2,1)}, bf16[2048,4096]{1,0:T(8,128)(2,1)}) custom-call(s32[8,128]{1,0:T(8,128)} %get-tuple-element.21.asked_ref, bf16[8,128,192]{2,1,0:T(8,128)(2,1)} %get-tuple-element.22.c_ref, bf16[8,128,192]{2,1,0:T(8,128)(2,1)} %get-tuple-element.23.w_ref, bf16[512,4096]{1,0:T(8,128)(2,1)} %bitcast.21, ...), custom_call_target="tpu_custom_call" | custom-call | flops 51539607552 | bytes 33554432 | tf_op jit(solution)/shard_map/pallas_call | solution.py:372
  112.6 10.5 %collective-permute-done = f32[128,4096]{1,0:T(8,128)} collective-permute-done((f32[128,4096]{1,0:T(8,128)}, f32[128,4096]{1,0:T(8,128)}, u32[]{:S(2)}, u32[]{:S(2)}) %collective-permute-start) | collective-permute-done | bytes 2097184 | tf_op jit(solution)/shard_map/ppermute | solution.py:365
  123.1 0.0 collective-permute-done.1
  123.1 3.1 %add_convert_fusion.1 = (bf16[64,4096]{1,0:T(8,128)(2,1)S(1)}, bf16[64,4096]{1,0:T(8,128)(2,1)S(1)}) fusion(f32[128,4096]{1,0:T(8,128)} %collective-permute-done, f32[128,4096]{1,0:T(8,128)} %collective-permute-done.1, f32[128,4096]{1,0:T(8,128)} %get-tuple-element.18), kind=kLoop, calls=%fused_computation.3 | loop fusion | flops 1572864 | bytes 7340032 | tf_op jit(solution)/shard_map/convert_element_type | solution.py:390
  126.3 0.0 collective-permute-start.2
  126.3 1.9 %collective-permute-done.2 = bf16[64,2,2048]{2,0,1:T(8,128)(2,1)S(1)} collective-permute-done((bf16[64,2,2048]{2,0,1:T(8,128)(2,1)S(1)}, bf16[64,2,2048]{2,0,1:T(8,128)(2,1)S(1)}, u32[]{:S(2)}, u32[]{:S(2)}) %collective-permute-start.2) | collective-permute-done | bytes 524320 | tf_op jit(solution)/shard_map/ppermute | solution.py:365
  128.2 0.1 bitcast_select_fusion
  128.3 1.0 fusion.2
  (1 shorter events, 0.0 us)
Async XLA Ops:
  75.0 48.1 %collective-permute-start = (f32[128,4096]{1,0:T(8,128)}, f32[128,4096]{1,0:T(8,128)}, u32[]{:S(2)}, u32[]{:S(2)}) collective-permute-start(f32[128,4096]{1,0:T(8,128)} %get-tuple-element.19), channel_id=1, source_target_pairs={{0,4},{1,3},{2,6},{3,1},{4,0},{5,7},{6,2},{7,5}} | collective-permute-start | bytes 6291464 | tf_op jit(solution)/shard_map/ppermute | solution.py:365
  76.5 46.6 %collective-permute-start.1 = (f32[128,4096]{1,0:T(8,128)}, f32[128,4096]{1,0:T(8,128)}, u32[]{:S(2)}, u32[]{:S(2)}) collective-permute-start(f32[128,4096]{1,0:T(8,128)} %get-tuple-element.20), channel_id=1, source_target_pairs={{0,2},{1,5},{2,0},{3,7},{4,6},{5,1},{6,4},{7,3}} | collective-permute-start | bytes 6291464 | tf_op jit(solution)/shard_map/ppermute | solution.py:365
  126.3 1.9 %collective-permute-start.2 = (bf16[64,2,2048]{2,0,1:T(8,128)(2,1)S(1)}, bf16[64,2,2048]{2,0,1:T(8,128)(2,1)S(1)}, u32[]{:S(2)}, u32[]{:S(2)}) collective-permute-start(bf16[64,2,2048]{2,0,1:T(8,128)(2,1)S(1)} %bitcast.18), channel_id=1, source_target_pairs={{0,1},{1,0},{2,3},{3,2},{4,5},{5,4},{6,7},{7,6}} | collective-permute-start | bytes 1572872 | tf_op jit(solution)/shard_map/ppermute | solution.py:365

commit v9 on v8

--- a/solution.py
+++ b/solution.py
@@ -38,11 +38,12 @@
 N_COPIES = 64
 SIDE_STEP, FAR_STEP, REST_STEP = 1, 4, 6
 COLS = 512
+PART = 32
 
 
 def layer_kernel(x_ref, dy_ref, slot_ref, gate_ref, req_ref, up_ref, down_ref,
-                 x_out, dy_out, c_out, w_out, asked_out, first_sum, second_sum, own_sum,
-                 x_all, dy_all, slot_all, gate_all, up_rows, down_rows, pair_recv, hop_recv, asked, asked_s, slot_t, w_t, c_t,
+                 x_out, dy_out, c_out, w_out, asked_out, first_keep, first_cross, second_keep, second_cross, own_keep, own_cross,
+                 x_all, dy_all, slot_all, gate_all, up_rows, down_rows, pair_recv, hop_recv, part_recv, asked, asked_s, slot_t, w_t, c_t,
                  send_sem, recv_sem, own_sem, smem_sem, in_sem, out_sem):
     me = lax.axis_index("ep")
     core = lax.rem(me, 2)
@@ -254,24 +255,39 @@
         pair_x = push(other, 0, pair_recv, 1, 1)
         block(2, mine.at[2], other.at[1])
         pair_y = push(other, 1, pair_recv, 2, 1)
-        leave([pair_x])
-        block(0, mine.at[0], other.at[0])
-        pair_own = push(other, 0, pair_recv, 3, 1)
         arrive([pair_x])
         add_into(mine.at[1], pair_recv.at[1])
         arrive([pair_y])
         add_into(mine.at[2], pair_recv.at[2])
-        saves.append(save(mine.at[1 + core], first_sum, 3))
-        saves[-1].start()
+        near, cross = pl.ds(0, TOK), pl.ds(TOK, TOK)
+        part = push(mine, (1 + core, pl.ds(0, PART)), part_recv, None, 2 + 2 * core)
+        saves.append(save(mine.at[1 + core, pl.ds(PART, TOK - PART)], first_keep, 0))
+        saves.append(save(mine.at[1 + core, cross], first_cross, 3))
+        for copy in saves[-2:]:
+            copy.start()
+        leave([pair_x])
+        block(0, mine.at[0], other.at[0])
+        pair_own = push(other, 0, pair_recv, 3, 1)
         arrive([pair_own])
         add_into(mine.at[0], pair_recv.at[3])
-        saves.append(save(mine.at[0], own_sum, 0))
-        saves[-1].start()
+        mine_cross = push(mine, (0, cross), own_cross, None, 1)
         for k, cols in enumerate(chunks):
             arrive([hop[k]])
             add_into(mine.at[2 - core], hop_recv, cols, 64)
-        saves.append(save(mine.at[2 - core], second_sum, 4))
+            for n, (rows, dst) in enumerate(((near, second_keep), (cross, second_cross))):
+                saves.append(save(mine.at[2 - core, rows, cols], dst.at[:, cols], 5 + 2 * k + n))
+                saves[-1].start()
+        arrive([part])
+
+        def add_part(t, _):
+            r = pl.ds(pl.multiple_of(t * 16, 16), 16)
+            mine[0, r, :] = mine[0, r, :] + part_recv[r, :]
+            return 0
+
+        lax.fori_loop(0, PART // 16, add_part, 0)
+        saves.append(save(mine.at[0, near], own_keep, 4))
         saves[-1].start()
+        arrive([mine_cross])
         leave([spec for spec in sent if spec not in pair_far and spec is not pair_x])
         for copy in saves:
             copy.wait()
@@ -327,6 +343,20 @@
     lax.fori_loop(0, n_rows // 32, drain, 0)
 
 
+def join_kernel(fk_ref, fc_ref, sk_ref, sc_ref, ok_ref, oc_ref, y_ref, dx_ref):
+    core = lax.rem(lax.axis_index("ep"), 2)
+    half = y_ref.shape[1] // 2
+    late = (pl.program_id(0) * y_ref.shape[0] >= PART).astype(F32)
+    keep = ok_ref[...] + sk_ref[...]
+    keep = jnp.where(late > 0, keep + fk_ref[...], keep).astype(BF16)
+    cross = (oc_ref[...] + fc_ref[...] + sc_ref[...]).astype(BF16)
+    here = pl.ds(pl.multiple_of(core * half, half), half)
+    there = pl.ds(pl.multiple_of((1 - core) * half, half), half)
+    for ref, cols in ((y_ref, slice(0, half)), (dx_ref, slice(half, 2 * half))):
+        ref[:, here] = keep[:, cols]
+        ref[:, there] = cross[:, cols]
+
+
 def solution(mesh):
     tok_spec = P(('dp', 'ep'))
     table_spec = P('ep')
@@ -339,29 +369,29 @@
         core = lax.axis_index('ep') % 2
         vmem, anyw = pl.BlockSpec(memory_space=pltpu.VMEM), pl.BlockSpec(memory_space=pl.ANY)
         shape = jax.ShapeDtypeStruct
-        sums = shape((PAIR, width), F32)
-        x_all, dy_all, c_terms, w_terms, asked, first_sum, second_sum, own_sum = pl.pallas_call(
+        sums = shape((TOK, width), F32)
+        x_all, dy_all, c_terms, w_terms, asked, first_keep, first_cross, second_keep, second_cross, own_keep, own_cross = pl.pallas_call(
             layer_kernel,
             in_specs=[anyw, anyw, vmem, vmem, vmem, anyw, anyw],
-            out_specs=[anyw] * 2 + [vmem] * 3 + [anyw] * 3,
-            out_shape=[shape((N_DEV, TOK, width), BF16)] * 2 + [shape((N_DEV, SLOTS, TERMS * TOK), BF16)] * 2 + [shape((N_DEV, SLOTS), I32)] + [sums] * 3,
+            out_specs=[anyw] * 2 + [vmem] * 3 + [anyw] * 6,
+            out_shape=[shape((N_DEV, TOK, width), BF16)] * 2 + [shape((N_DEV, SLOTS, TERMS * TOK), BF16)] * 2 + [shape((N_DEV, SLOTS), I32)] + [shape((TOK - PART, width), F32)] + [sums] * 5,
             scratch_shapes=[
                 pltpu.VMEM((N_DEV, TOK, width), BF16), pltpu.VMEM((N_DEV, TOK, width), BF16),
                 pltpu.VMEM((N_DEV, TOK, SEL), I32), pltpu.VMEM((N_DEV, TOK, SEL), F32),
                 pltpu.VMEM((N_DEV * SLOTS, width), BF16), pltpu.VMEM((N_DEV * SLOTS, width), BF16),
-                pltpu.VMEM((4, PAIR, width), F32), pltpu.VMEM((PAIR, width), F32),
+                pltpu.VMEM((4, PAIR, width), F32), pltpu.VMEM((PAIR, width), F32), pltpu.VMEM((PART, width), F32),
                 pltpu.VMEM((N_DEV, SLOTS), I32), pltpu.SMEM((N_DEV, SLOTS), I32),
                 pltpu.VMEM((SEL, PAIR), I32), pltpu.VMEM((SEL, PAIR), F32), pltpu.VMEM((SEL, PAIR), F32),
                 pltpu.SemaphoreType.DMA((N_COPIES,)), pltpu.SemaphoreType.DMA((N_COPIES,)),
                 pltpu.SemaphoreType.DMA((2,)), pltpu.SemaphoreType.DMA,
-                pltpu.SemaphoreType.DMA((1,)), pltpu.SemaphoreType.DMA((5,)),
+                pltpu.SemaphoreType.DMA((1,)), pltpu.SemaphoreType.DMA((5 + 2 * width // COLS,)),
             ],
             compiler_params=pltpu.CompilerParams(collective_id=0, has_side_effects=True, vmem_limit_bytes=VMEM_BYTES),
         )(tokens, grad_out, slot_ids.transpose(1, 2, 0), gate_vals.transpose(1, 2, 0), request_rows, up_local, down_local)
 
-        partner = [(i, i ^ 1) for i in range(N_DEV)]
         first_hop = [(i, i ^ (2 if i % 2 == 0 else 4)) for i in range(N_DEV)]
         second_hop = [(i, i ^ (4 if i % 2 == 0 else 2)) for i in range(N_DEV)]
+        over = lambda pairs: [(i, j ^ 1) for i, j in pairs]
         hop = lambda value, pairs: lax.ppermute(value, 'ep', pairs)
 
         def grad_rows():
@@ -383,15 +413,20 @@
                 cost_estimate=pl.CostEstimate(flops=12 * rows_owner * width * n_tok, bytes_accessed=4 * rows_owner * width, transcendentals=0),
             )(asked, c_terms, w_terms, x_all.reshape(n_tok, width), dy_all.reshape(n_tok, width))
 
-        got_own = hop(first_sum, first_hop)
-        got_last = hop(second_sum, second_hop)
+        got = (hop(first_keep, first_hop), hop(first_cross, over(first_hop)), hop(second_keep, second_hop), hop(second_cross, over(second_hop)))
         grad_up, grad_down = grad_rows()
-        got_last, got_own, grad_up, grad_down = lax.optimization_barrier((got_last, got_own, grad_up, grad_down))
-        keep, give = [(own_sum[rows] + got_own[rows] + got_last[rows]).astype(BF16).reshape(TOK, 2, half) for rows in (slice(0, TOK), slice(TOK, PAIR))]
-        back = hop(give, partner)
-        low = jnp.where(core == 0, keep, back)
-        high = jnp.where(core == 0, back, keep)
-        token_out = jnp.concatenate([low, high], axis=2)
-        return token_out[:, 0], token_out[:, 1], grad_up, grad_down
+        got, grad_up, grad_down = lax.optimization_barrier((got, grad_up, grad_down))
+        block = 16
+        rows = pl.BlockSpec((block, width), lambda i: (i, 0))
+        late = pl.BlockSpec((block, width), lambda i: (jnp.maximum(i - PART // block, 0), 0))
+        out_tokens, grad_tokens = pl.pallas_call(
+            join_kernel,
+            grid=(TOK // block,),
+            in_specs=[late] + [rows] * 5,
+            out_specs=[rows, rows],
+            out_shape=[shape((TOK, width), BF16)] * 2,
+            compiler_params=pltpu.CompilerParams(vmem_limit_bytes=VMEM_BYTES),
+        )(*got, own_keep, own_cross)
+        return out_tokens, grad_tokens, grad_up, grad_down
 
     return jax.shard_map(per_device, mesh=mesh, in_specs=(tok_spec, tok_spec, tok_spec, tok_spec, tok_spec, table_spec, table_spec), out_specs=(tok_spec, tok_spec, tok_spec, tok_spec), check_vma=False)

time: 130 us -> 127 us (0.977)
  Pallas kernels: 110 us -> 119 us
  waiting for transfers between devices: 12.4 us -> 3.91 us
  other arithmetic: 4.25 us -> 0 us
  starting transfers between devices: 2.07 us -> 3.51 us
    ppermute x3 -> x4, waiting for transfers between devices: 12.4 us -> 3.91 us  [per_device(): hop = lambda value, pairs: lax.ppermute(value, 'ep', pairs)]
    pallas_call x1, Pallas kernels: 74.4 us -> 79.1 us  [per_device(): pl.pallas_call(layer_kernel, in_specs=[anyw, anyw, vmem, vmem, vmem, anyw...]
    pallas_call x0 -> x1, Pallas kernels: none -> 4.33 us  [per_device(): pl.pallas_call(join_kernel, grid=(TOK // block,), in_specs=[late] + [rows...]
    convert_element_type x1 -> x0, other arithmetic: 3.15 us -> none  [per_device(): (own_sum[rows] + got_own[rows] + got_last[rows]).astype(BF16)]
    ppermute x3 -> x4, starting transfers between devices: 2.07 us -> 3.51 us  [per_device(): hop = lambda value, pairs: lax.ppermute(value, 'ep', pairs)]
  transfers between devices with their start and end apart: 3 -> 4, of which waited for: 2 -> 1; matrix products, arithmetic and copies ran while one was open for 0% -> 0% of each run, Pallas kernels for 27% -> 28%
where the time goes in v9:
time: 127 us
  Pallas kernels  119 us (94%)
  waiting for transfers between devices  3.91 us (3%)
  starting transfers between devices  3.51 us (3%)
    pallas_call x1, Pallas kernels, per_device(): pl.pallas_call(layer_kernel, in_specs=[anyw, anyw, vmem, vmem, vmem, anyw...  79.1 us
    pallas_call x1, Pallas kernels, grad_rows(): pl.pallas_call(row_kernel, grid_spec=pltpu.PrefetchScalarGridSpec(num_sca...  35.5 us
    pallas_call x1, Pallas kernels, per_device(): pl.pallas_call(join_kernel, grid=(TOK // block,), in_specs=[late] + [rows...  4.33 us
    ppermute x4, waiting for transfers between devices, per_device(): hop = lambda value, pairs: lax.ppermute(value, 'ep', pairs)  3.91 us
    ppermute x4, starting transfers between devices, per_device(): hop = lambda value, pairs: lax.ppermute(value, 'ep', pairs)  3.51 us
  transfers between devices with their start and end apart: 4, of which 1 were waited for; matrix products, arithmetic and copies ran while one was open for 0% of the time, Pallas kernels for 28%

profile of v9, /device:TPU:0, one launch (start us, length us, event | category | flops | bytes accessed | tf_op | source)
XLA Modules:
  0.0 127.0 jit_solution(17772912948173368769)
XLA Ops:
  0.6 79.1 %shard_map.102 = (bf16[8,64,4096]{2,1,0:T(8,128)(2,1)}, bf16[8,64,4096]{2,1,0:T(8,128)(2,1)}, bf16[8,128,192]{2,1,0:T(8,128)(2,1)}, bf16[8,128,192]{2,1,0:T(8,12...) custom-call(bf16[64,4096]{1,0:T(8,128)(2,1)} %x_ref.1, ...), custom_call_target="tpu_custom_call" | custom-call | tf_op jit(solution)/shard_map/pallas_call | solution.py:373
  79.8 1.5 %collective-permute-start = (f32[32,4096]{1,0:T(8,128)}, f32[32,4096]{1,0:T(8,128)S(1)}, u32[]{:S(2)}, u32[]{:S(2)}) collective-permute-start(f32[32,4096]{1,0:T(8,128)} %get-tuple-element.25), channel_id=1, source_target_pairs={{0,2},{1,5},{2,0},{3,7},{4,6},{5,1},{6,4},{7,3}} | collective-permute-start | bytes 1572872 | tf_op jit(solution)/shard_map/ppermute | solution.py:395
  81.3 0.0 collective-permute-start.1
  81.3 1.5 %collective-permute-start.2 = (f32[64,4096]{1,0:T(8,128)}, f32[64,4096]{1,0:T(8,128)}, u32[]{:S(2)}, u32[]{:S(2)}) collective-permute-start(f32[64,4096]{1,0:T(8,128)} %get-tuple-element.27), channel_id=1, source_target_pairs={{0,4},{1,3},{2,6},{3,1},{4,0},{5,7},{6,2},{7,5}} | collective-permute-start | bytes 3145736 | tf_op jit(solution)/shard_map/ppermute | solution.py:395
  82.7 0.6 collective-permute-start.3
  83.3 35.5 %shard_map.103 = (bf16[2048,4096]{1,0:T(8,128)(2,1)}, bf16[2048,4096]{1,0:T(8,128)(2,1)}) custom-call(s32[8,128]{1,0:T(8,128)} %get-tuple-element.29.asked_ref, bf16[8,128,192]{2,1,0:T(8,128)(2,1)} %get-tuple-element.30.c_ref, bf16[8,128,192]{2,1,0:T(8,128)(2,1)} %get-tuple-element.31.w_ref, bf16[512,4096]{1,0:T(8,128)(2,1)} %bitcast.6, ...), custom_call_target="tpu_custom_call" | custom-call | flops 51539607552 | bytes 33554432 | tf_op jit(solution)/shard_map/pallas_call | solution.py:402
  118.7 0.0 collective-permute-done.fk_ref
  118.8 0.0 copy-start.1
  118.8 0.0 collective-permute-done.1.fc_ref
  118.8 0.0 copy-start
  118.8 0.0 collective-permute-done.2.sk_ref
  118.8 3.9 %collective-permute-done.3.sc_ref = f32[64,4096]{1,0:T(8,128)} collective-permute-done((f32[64,4096]{1,0:T(8,128)}, f32[64,4096]{1,0:T(8,128)}, u32[]{:S(2)}, u32[]{:S(2)}) %collective-permute-start.3) | collective-permute-done | bytes 1048608 | tf_op jit(solution)/shard_map/ppermute | solution.py:395
  122.7 0.0 copy-done.1
  122.7 0.0 copy-done
  122.7 4.3 %shard_map.104 = (bf16[64,4096]{1,0:T(8,128)(2,1)}, bf16[64,4096]{1,0:T(8,128)(2,1)}) custom-call(f32[32,4096]{1,0:T(8,128)} %copy-done.1, f32[64,4096]{1,0:T(8,128)} %copy-done, f32[64,4096]{1,0:T(8,128)} %collective-permute-done.2.sk_ref, f32[64,4096]{1,0:T(8,128)} %collective-permute-done.3.sc_ref, f32[64,4096]{1,0:T(8,128)} %get-tuple-element.40.ok_ref, ...), custom_call_target="tpu_custom_call" | custom-call | tf_op jit(solution)/shard_map/pallas_call | solution.py:422
Async XLA Ops:
  79.8 39.0 %collective-permute-start = (f32[32,4096]{1,0:T(8,128)}, f32[32,4096]{1,0:T(8,128)S(1)}, u32[]{:S(2)}, u32[]{:S(2)}) collective-permute-start(f32[32,4096]{1,0:T(8,128)} %get-tuple-element.25), channel_id=1, source_target_pairs={{0,2},{1,5},{2,0},{3,7},{4,6},{5,1},{6,4},{7,3}} | collective-permute-start | bytes 1572872 | tf_op jit(solution)/shard_map/ppermute | solution.py:395
  81.3 37.5 %collective-permute-start.1 = (f32[64,4096]{1,0:T(8,128)}, f32[64,4096]{1,0:T(8,128)S(1)}, u32[]{:S(2)}, u32[]{:S(2)}) collective-permute-start(f32[64,4096]{1,0:T(8,128)} %get-tuple-element.26), channel_id=1, source_target_pairs={{0,3},{1,4},{2,1},{3,6},{4,7},{5,0},{6,5},{7,2}} | collective-permute-start | bytes 3145736 | tf_op jit(solution)/shard_map/ppermute | solution.py:395
  81.3 37.5 %collective-permute-start.2 = (f32[64,4096]{1,0:T(8,128)}, f32[64,4096]{1,0:T(8,128)}, u32[]{:S(2)}, u32[]{:S(2)}) collective-permute-start(f32[64,4096]{1,0:T(8,128)} %get-tuple-element.27), channel_id=1, source_target_pairs={{0,4},{1,3},{2,6},{3,1},{4,0},{5,7},{6,2},{7,5}} | collective-permute-start | bytes 3145736 | tf_op jit(solution)/shard_map/ppermute | solution.py:395
  82.7 40.0 %collective-permute-start.3 = (f32[64,4096]{1,0:T(8,128)}, f32[64,4096]{1,0:T(8,128)}, u32[]{:S(2)}, u32[]{:S(2)}) collective-permute-start(f32[64,4096]{1,0:T(8,128)} %get-tuple-element.28), channel_id=1, source_target_pairs={{0,5},{1,2},{2,7},{3,0},{4,1},{5,6},{6,3},{7,4}} | collective-permute-start | bytes 3145736 | tf_op jit(solution)/shard_map/ppermute | solution.py:395
  118.8 3.9 %copy-start.1 = (f32[32,4096]{1,0:T(8,128)}, f32[32,4096]{1,0:T(8,128)S(1)}, u32[]{:S(2)}) copy-start(f32[32,4096]{1,0:T(8,128)S(1)} %collective-permute-done.fk_ref) | copy-start | bytes 1572868
  118.8 3.9 %copy-start = (f32[64,4096]{1,0:T(8,128)}, f32[64,4096]{1,0:T(8,128)S(1)}, u32[]{:S(2)}) copy-start(f32[64,4096]{1,0:T(8,128)S(1)} %collective-permute-done.1.fc_ref) | copy-start | bytes 3145732

commit v10 on v9

--- a/solution.py
+++ b/solution.py
@@ -39,11 +39,12 @@
 SIDE_STEP, FAR_STEP, REST_STEP = 1, 4, 6
 COLS = 512
 PART = 32
-
-
-def layer_kernel(x_ref, dy_ref, slot_ref, gate_ref, req_ref, up_ref, down_ref,
-                 x_out, dy_out, c_out, w_out, asked_out, first_keep, first_cross, second_keep, second_cross, own_keep, own_cross,
-                 x_all, dy_all, slot_all, gate_all, up_rows, down_rows, pair_recv, hop_recv, part_recv, asked, asked_s, slot_t, w_t, c_t,
+TERM_SEM = 5 + 16
+
+
+def layer_kernel(x_ref, dy_ref, slot_in, gate_in, req_in, up_ref, down_ref,
+                 x_out, dy_out, c_out, w_out, asked_out, first_part, first_keep, first_cross, second_keep, second_cross, own_keep, own_cross,
+                 x_all, dy_all, slot_all, gate_all, up_rows, down_rows, pair_recv, hop_recv, slot_ref, gate_ref, req_ref, c_buf, w_buf, asked, asked_s, slot_t, w_t, c_t,
                  send_sem, recv_sem, own_sem, smem_sem, in_sem, out_sem):
     me = lax.axis_index("ep")
     core = lax.rem(me, 2)
@@ -74,13 +75,16 @@
             descriptor(*spec).wait_send()
 
     own = [pltpu.make_async_copy(src, dst.at[0], own_sem.at[k]) for k, (src, dst) in enumerate(((x_ref, x_all), (dy_ref, dy_all)))]
-    slot_all[0] = slot_ref[...].reshape(SEL, TOK).T
-    gate_all[0] = gate_ref[...].reshape(SEL, TOK).T
+    small = [pltpu.make_async_copy(src, dst, own_sem.at[2 + k]) for k, (src, dst) in enumerate(((slot_in, slot_ref), (gate_in, gate_ref), (req_in, req_ref)))]
     barrier = pltpu.get_barrier_semaphore()
     for b in range(1, N_DEV):
         pl.semaphore_signal(barrier, inc=1, device_id={"ep": me ^ b}, device_id_type=MESH)
-    for copy in own:
+    for copy in small + own:
         copy.start()
+    for copy in small:
+        copy.wait()
+    slot_all[0] = slot_ref[...].reshape(SEL, TOK).T
+    gate_all[0] = gate_ref[...].reshape(SEL, TOK).T
     pl.semaphore_wait(barrier, N_DEV - 1)
 
     asks = [push(req_ref, (0, pl.ds(me ^ b, 1)), asked, pl.ds(b, 1), b) for b in range(1, N_DEV)]
@@ -90,10 +94,11 @@
     second = [push(x_ref, low, x_all, (2, low), 2), push(dy_ref, low, dy_all, (4, low), 4)]
     asked[pl.ds(0, 1), :] = req_ref[0, pl.ds(me, 1), :]
     arrive(asks)
-    asked_out[...] = asked[...]
     to_smem = pltpu.make_async_copy(asked, asked_s, smem_sem)
     to_smem.start()
     to_smem.wait()
+    keep_asked = pltpu.make_async_copy(asked, asked_out, own_sem.at[5])
+    keep_asked.start()
 
     def gather_all(table, wide, picked):
         def fetch(k):
@@ -160,6 +165,7 @@
     far, near_first = kept[0]
     for copy in own:
         copy.wait()
+    keep_asked.wait()
     dims = (((1,), (1,)), ((), ()))
     row_iota = lax.broadcasted_iota(I32, (SLOTS, PAIR), 0)
     block_diag = (lax.broadcasted_iota(I32, (PAIR, 2 * SLOTS), 0) < TOK) == (lax.broadcasted_iota(I32, (PAIR, 2 * SLOTS), 1) < SLOTS)
@@ -192,7 +198,7 @@
 
         zero = jnp.zeros((SLOTS, PAIR), F32)
         acc_w, acc_c = lax.fori_loop(0, SEL, step, (zero, zero), unroll=4)
-        for ref, acc in ((w_out, acc_w), (c_out, acc_c)):
+        for ref, acc in ((w_buf, acc_w), (c_buf, acc_c)):
             terms = split3(acc)
             for j in range(2):
                 ref[2 * r + j] = jnp.concatenate([term[:, j * TOK:(j + 1) * TOK] for term in terms], axis=1)
@@ -228,6 +234,13 @@
 
     def blocks(mine, other):
         save = lambda src, dst, k: pltpu.make_async_copy(src, dst, out_sem.at[k])
+        saves = []
+
+        def keep_terms(r):
+            for n, (src, dst) in enumerate(((c_buf, c_out), (w_buf, w_out))):
+                saves.append(save(src.at[pl.ds(2 * r, 2)], dst.at[pl.ds(2 * r, 2)], TERM_SEM + 2 * r + n))
+                saves[-1].start()
+
         arrive(near_own)
         arrive(far)
         near_far = [push(ref, 6, ref, 7, 1) for ref in (gate_all, slot_all, x_all, dy_all)]
@@ -243,7 +256,7 @@
             arrive([pair_far[k]])
             add_into(mine.at[3], pair_recv.at[0], cols, 64)
             hop.append(push(mine, (3, every, cols), hop_recv, (every, cols), 2 + 2 * core))
-        saves = []
+        keep_terms(3)
         arrive(second)
         near_second = [push(gate_all, 2, gate_all, 3, 1), push(slot_all, 4, slot_all, 5, 1), push(x_all, 2, x_all, 3, 1), push(dy_all, 4, dy_all, 5, 1)]
         arrive(near_second)
@@ -253,14 +266,16 @@
         leave(pair_far)
         block(1, mine.at[1], other.at[0])
         pair_x = push(other, 0, pair_recv, 1, 1)
+        keep_terms(1)
         block(2, mine.at[2], other.at[1])
         pair_y = push(other, 1, pair_recv, 2, 1)
+        keep_terms(2)
         arrive([pair_x])
         add_into(mine.at[1], pair_recv.at[1])
         arrive([pair_y])
         add_into(mine.at[2], pair_recv.at[2])
         near, cross = pl.ds(0, TOK), pl.ds(TOK, TOK)
-        part = push(mine, (1 + core, pl.ds(0, PART)), part_recv, None, 2 + 2 * core)
+        part = push(mine, (1 + core, pl.ds(0, PART)), first_part, None, 2 + 2 * core)
         saves.append(save(mine.at[1 + core, pl.ds(PART, TOK - PART)], first_keep, 0))
         saves.append(save(mine.at[1 + core, cross], first_cross, 3))
         for copy in saves[-2:]:
@@ -268,26 +283,19 @@
         leave([pair_x])
         block(0, mine.at[0], other.at[0])
         pair_own = push(other, 0, pair_recv, 3, 1)
+        keep_terms(0)
         arrive([pair_own])
         add_into(mine.at[0], pair_recv.at[3])
         mine_cross = push(mine, (0, cross), own_cross, None, 1)
+        saves.append(save(mine.at[0, near], own_keep, 4))
+        saves[-1].start()
         for k, cols in enumerate(chunks):
             arrive([hop[k]])
             add_into(mine.at[2 - core], hop_recv, cols, 64)
             for n, (rows, dst) in enumerate(((near, second_keep), (cross, second_cross))):
                 saves.append(save(mine.at[2 - core, rows, cols], dst.at[:, cols], 5 + 2 * k + n))
                 saves[-1].start()
-        arrive([part])
-
-        def add_part(t, _):
-            r = pl.ds(pl.multiple_of(t * 16, 16), 16)
-            mine[0, r, :] = mine[0, r, :] + part_recv[r, :]
-            return 0
-
-        lax.fori_loop(0, PART // 16, add_part, 0)
-        saves.append(save(mine.at[0, near], own_keep, 4))
-        saves[-1].start()
-        arrive([mine_cross])
+        arrive([part, mine_cross])
         leave([spec for spec in sent if spec not in pair_far and spec is not pair_x])
         for copy in saves:
             copy.wait()
@@ -343,12 +351,11 @@
     lax.fori_loop(0, n_rows // 32, drain, 0)
 
 
-def join_kernel(fk_ref, fc_ref, sk_ref, sc_ref, ok_ref, oc_ref, y_ref, dx_ref):
+def join_kernel(fp_ref, fk_ref, fc_ref, sk_ref, sc_ref, ok_ref, oc_ref, y_ref, dx_ref):
     core = lax.rem(lax.axis_index("ep"), 2)
     half = y_ref.shape[1] // 2
-    late = (pl.program_id(0) * y_ref.shape[0] >= PART).astype(F32)
-    keep = ok_ref[...] + sk_ref[...]
-    keep = jnp.where(late > 0, keep + fk_ref[...], keep).astype(BF16)
+    late = pl.program_id(0) * y_ref.shape[0] >= PART
+    keep = (ok_ref[...] + jnp.where(late, fk_ref[...], fp_ref[...]) + sk_ref[...]).astype(BF16)
     cross = (oc_ref[...] + fc_ref[...] + sc_ref[...]).astype(BF16)
     here = pl.ds(pl.multiple_of(core * half, half), half)
     there = pl.ds(pl.multiple_of((1 - core) * half, half), half)
@@ -364,27 +371,30 @@
     def per_device(tokens, slot_ids, request_rows, gate_vals, grad_out, up_local, down_local):
         width = tokens.shape[1]
         rows_owner = up_local.shape[0]
+        heads, top_k = slot_ids.shape[1:]
         n_tok = N_DEV * TOK
         half = width // 2
         core = lax.axis_index('ep') % 2
-        vmem, anyw = pl.BlockSpec(memory_space=pltpu.VMEM), pl.BlockSpec(memory_space=pl.ANY)
+        anyw = pl.BlockSpec(memory_space=pl.ANY)
         shape = jax.ShapeDtypeStruct
         sums = shape((TOK, width), F32)
-        x_all, dy_all, c_terms, w_terms, asked, first_keep, first_cross, second_keep, second_cross, own_keep, own_cross = pl.pallas_call(
+        x_all, dy_all, c_terms, w_terms, asked, first_part, first_keep, first_cross, second_keep, second_cross, own_keep, own_cross = pl.pallas_call(
             layer_kernel,
-            in_specs=[anyw, anyw, vmem, vmem, vmem, anyw, anyw],
-            out_specs=[anyw] * 2 + [vmem] * 3 + [anyw] * 6,
-            out_shape=[shape((N_DEV, TOK, width), BF16)] * 2 + [shape((N_DEV, SLOTS, TERMS * TOK), BF16)] * 2 + [shape((N_DEV, SLOTS), I32)] + [shape((TOK - PART, width), F32)] + [sums] * 5,
+            in_specs=[anyw] * 7,
+            out_specs=[anyw] * 12,
+            out_shape=[shape((N_DEV, TOK, width), BF16)] * 2 + [shape((N_DEV, SLOTS, TERMS * TOK), BF16)] * 2 + [shape((N_DEV, SLOTS), I32)] + [shape((PART, width), F32), shape((TOK - PART, width), F32)] + [sums] * 5,
             scratch_shapes=[
                 pltpu.VMEM((N_DEV, TOK, width), BF16), pltpu.VMEM((N_DEV, TOK, width), BF16),
                 pltpu.VMEM((N_DEV, TOK, SEL), I32), pltpu.VMEM((N_DEV, TOK, SEL), F32),
                 pltpu.VMEM((N_DEV * SLOTS, width), BF16), pltpu.VMEM((N_DEV * SLOTS, width), BF16),
-                pltpu.VMEM((4, PAIR, width), F32), pltpu.VMEM((PAIR, width), F32), pltpu.VMEM((PART, width), F32),
+                pltpu.VMEM((4, PAIR, width), F32), pltpu.VMEM((PAIR, width), F32),
+                pltpu.VMEM((heads, top_k, TOK), I32), pltpu.VMEM((heads, top_k, TOK), F32), pltpu.VMEM((1, N_DEV, SLOTS), I32),
+                pltpu.VMEM((N_DEV, SLOTS, TERMS * TOK), BF16), pltpu.VMEM((N_DEV, SLOTS, TERMS * TOK), BF16),
                 pltpu.VMEM((N_DEV, SLOTS), I32), pltpu.SMEM((N_DEV, SLOTS), I32),
                 pltpu.VMEM((SEL, PAIR), I32), pltpu.VMEM((SEL, PAIR), F32), pltpu.VMEM((SEL, PAIR), F32),
                 pltpu.SemaphoreType.DMA((N_COPIES,)), pltpu.SemaphoreType.DMA((N_COPIES,)),
-                pltpu.SemaphoreType.DMA((2,)), pltpu.SemaphoreType.DMA,
-                pltpu.SemaphoreType.DMA((1,)), pltpu.SemaphoreType.DMA((5 + 2 * width // COLS,)),
+                pltpu.SemaphoreType.DMA((6,)), pltpu.SemaphoreType.DMA,
+                pltpu.SemaphoreType.DMA((1,)), pltpu.SemaphoreType.DMA((TERM_SEM + N_DEV,)),
             ],
             compiler_params=pltpu.CompilerParams(collective_id=0, has_side_effects=True, vmem_limit_bytes=VMEM_BYTES),
         )(tokens, grad_out, slot_ids.transpose(1, 2, 0), gate_vals.transpose(1, 2, 0), request_rows, up_local, down_local)
@@ -416,17 +426,17 @@
         got = (hop(first_keep, first_hop), hop(first_cross, over(first_hop)), hop(second_keep, second_hop), hop(second_cross, over(second_hop)))
         grad_up, grad_down = grad_rows()
         got, grad_up, grad_down = lax.optimization_barrier((got, grad_up, grad_down))
-        block = 16
+        block = 32
         rows = pl.BlockSpec((block, width), lambda i: (i, 0))
-        late = pl.BlockSpec((block, width), lambda i: (jnp.maximum(i - PART // block, 0), 0))
+        early = pl.BlockSpec((block, width), lambda i: (0, 0))
         out_tokens, grad_tokens = pl.pallas_call(
             join_kernel,
             grid=(TOK // block,),
-            in_specs=[late] + [rows] * 5,
+            in_specs=[early] * 2 + [rows] * 5,
             out_specs=[rows, rows],
             out_shape=[shape((TOK, width), BF16)] * 2,
-            compiler_params=pltpu.CompilerParams(vmem_limit_bytes=VMEM_BYTES),
-        )(*got, own_keep, own_cross)
+            compiler_params=pltpu.CompilerParams(vmem_limit_bytes=16 * 1024 * 1024),
+        )(first_part, *got, own_keep, own_cross)
         return out_tokens, grad_tokens, grad_up, grad_down
 
     return jax.shard_map(per_device, mesh=mesh, in_specs=(tok_spec, tok_spec, tok_spec, tok_spec, tok_spec, table_spec, table_spec), out_specs=(tok_spec, tok_spec, tok_spec, tok_spec), check_vma=False)

time: 127 us -> 126 us (level)
  Pallas kernels: 119 us -> 116 us
    pallas_call x2, Pallas kernels: 83.5 us -> 80.5 us  [the longest x1 77.5 us: per_device(): pl.pallas_call(layer_kernel, in_specs=[anyw] * 7, out_specs=[anyw] * 12,...]
where the time goes in v10:
time: 126 us; the launch traced here: 125 us
  Pallas kernels  116 us (92%)
  waiting for transfers between devices  3.91 us (3%)
  starting transfers between devices  3.51 us (3%)
    pallas_call x1, Pallas kernels, per_device(): pl.pallas_call(layer_kernel, in_specs=[anyw] * 7, out_specs=[anyw] * 12,...  77.5 us
    pallas_call x1, Pallas kernels, grad_rows(): pl.pallas_call(row_kernel, grid_spec=pltpu.PrefetchScalarGridSpec(num_sca...  35.5 us
    ppermute x4, waiting for transfers between devices, per_device(): hop = lambda value, pairs: lax.ppermute(value, 'ep', pairs)  3.91 us
    ppermute x4, starting transfers between devices, per_device(): hop = lambda value, pairs: lax.ppermute(value, 'ep', pairs)  3.51 us
    pallas_call x1, Pallas kernels, per_device(): pl.pallas_call(join_kernel, grid=(TOK // block,), in_specs=[early] * 2 +...  2.98 us
  transfers between devices with their start and end apart: 4, of which 1 were waited for; matrix products, arithmetic and copies ran while one was open for 0% of the time, Pallas kernels for 28%

profile of v10, /device:TPU:0, one launch (start us, length us, event | category | flops | bytes accessed | tf_op | source)
XLA Modules:
  0.0 125.3 jit_solution(1599103318484501732)
XLA Ops:
  0.6 77.5 %shard_map.102 = (bf16[8,64,4096]{2,1,0:T(8,128)(2,1)}, bf16[8,64,4096]{2,1,0:T(8,128)(2,1)}, bf16[8,128,192]{2,1,0:T(8,128)(2,1)}, bf16[8,128,192]{2,1,0:T(8,12...) custom-call(bf16[64,4096]{1,0:T(8,128)(2,1)} %x_ref.1, ...), custom_call_target="tpu_custom_call" | custom-call | tf_op jit(solution)/shard_map/pallas_call | solution.py:381
  78.1 1.5 %collective-permute-start = (f32[32,4096]{1,0:T(8,128)}, f32[32,4096]{1,0:T(8,128)}, u32[]{:S(2)}, u32[]{:S(2)}) collective-permute-start(f32[32,4096]{1,0:T(8,128)} %get-tuple-element.27), channel_id=1, source_target_pairs={{0,2},{1,5},{2,0},{3,7},{4,6},{5,1},{6,4},{7,3}} | collective-permute-start | bytes 1572872 | tf_op jit(solution)/shard_map/ppermute | solution.py:405
  79.6 0.0 collective-permute-start.1
  79.6 1.5 %collective-permute-start.2 = (f32[64,4096]{1,0:T(8,128)}, f32[64,4096]{1,0:T(8,128)}, u32[]{:S(2)}, u32[]{:S(2)}) collective-permute-start(f32[64,4096]{1,0:T(8,128)} %get-tuple-element.29), channel_id=1, source_target_pairs={{0,4},{1,3},{2,6},{3,1},{4,0},{5,7},{6,2},{7,5}} | collective-permute-start | bytes 3145736 | tf_op jit(solution)/shard_map/ppermute | solution.py:405
  81.1 0.6 collective-permute-start.3
  81.7 0.0 copy-start
  81.7 0.0 copy-start.2
  81.7 35.5 %shard_map.103 = (bf16[2048,4096]{1,0:T(8,128)(2,1)}, bf16[2048,4096]{1,0:T(8,128)(2,1)}) custom-call(s32[8,128]{1,0:T(8,128)} %get-tuple-element.31.asked_ref, bf16[8,128,192]{2,1,0:T(8,128)(2,1)} %get-tuple-element.32.c_ref, bf16[8,128,192]{2,1,0:T(8,128)(2,1)} %get-tuple-element.33.w_ref, bf16[512,4096]{1,0:T(8,128)(2,1)} %bitcast.6, ...), custom_call_target="tpu_custom_call" | custom-call | flops 51539607552 | bytes 33554432 | tf_op jit(solution)/shard_map/pallas_call | solution.py:412
  117.1 0.0 collective-permute-done.fk_ref
  117.1 0.0 collective-permute-done.1.fc_ref
  117.1 0.0 collective-permute-done.2.sk_ref
  117.2 3.9 %collective-permute-done.3.sc_ref = f32[64,4096]{1,0:T(8,128)} collective-permute-done((f32[64,4096]{1,0:T(8,128)}, f32[64,4096]{1,0:T(8,128)}, u32[]{:S(2)}, u32[]{:S(2)}) %collective-permute-start.3) | collective-permute-done | bytes 1048608 | tf_op jit(solution)/shard_map/ppermute | solution.py:405
  121.1 0.0 copy-done
  121.1 0.0 copy-done.2
  121.1 0.0 copy-start.1
  121.1 1.2 copy-done.1
  122.3 3.0 %shard_map.104 = (bf16[64,4096]{1,0:T(8,128)(2,1)}, bf16[64,4096]{1,0:T(8,128)(2,1)}) custom-call(f32[32,4096]{1,0:T(8,128)S(1)} %copy-done.2, f32[32,4096]{1,0:T(8,128)} %collective-permute-done.fk_ref, f32[64,4096]{1,0:T(8,128)} %collective-permute-done.1.fc_ref, f32[64,4096]{1,0:T(8,128)} %collective-permute-done.2.sk_ref, ...), custom_call_target="tpu_custom_call" | custom-call | tf_op jit(solution)/shard_map/pallas_call | solution.py:432
Async XLA Ops:
  78.1 39.0 %collective-permute-start = (f32[32,4096]{1,0:T(8,128)}, f32[32,4096]{1,0:T(8,128)}, u32[]{:S(2)}, u32[]{:S(2)}) collective-permute-start(f32[32,4096]{1,0:T(8,128)} %get-tuple-element.27), channel_id=1, source_target_pairs={{0,2},{1,5},{2,0},{3,7},{4,6},{5,1},{6,4},{7,3}} | collective-permute-start | bytes 1572872 | tf_op jit(solution)/shard_map/ppermute | solution.py:405
  79.6 37.5 %collective-permute-start.1 = (f32[64,4096]{1,0:T(8,128)}, f32[64,4096]{1,0:T(8,128)}, u32[]{:S(2)}, u32[]{:S(2)}) collective-permute-start(f32[64,4096]{1,0:T(8,128)} %get-tuple-element.28), channel_id=1, source_target_pairs={{0,3},{1,4},{2,1},{3,6},{4,7},{5,0},{6,5},{7,2}} | collective-permute-start | bytes 3145736 | tf_op jit(solution)/shard_map/ppermute | solution.py:405
  79.6 37.5 %collective-permute-start.2 = (f32[64,4096]{1,0:T(8,128)}, f32[64,4096]{1,0:T(8,128)}, u32[]{:S(2)}, u32[]{:S(2)}) collective-permute-start(f32[64,4096]{1,0:T(8,128)} %get-tuple-element.29), channel_id=1, source_target_pairs={{0,4},{1,3},{2,6},{3,1},{4,0},{5,7},{6,2},{7,5}} | collective-permute-start | bytes 3145736 | tf_op jit(solution)/shard_map/ppermute | solution.py:405
  81.1 40.0 %collective-permute-start.3 = (f32[64,4096]{1,0:T(8,128)}, f32[64,4096]{1,0:T(8,128)}, u32[]{:S(2)}, u32[]{:S(2)}) collective-permute-start(f32[64,4096]{1,0:T(8,128)} %get-tuple-element.30), channel_id=1, source_target_pairs={{0,5},{1,2},{2,7},{3,0},{4,1},{5,6},{6,3},{7,4}} | collective-permute-start | bytes 3145736 | tf_op jit(solution)/shard_map/ppermute | solution.py:405
  81.7 39.4 %copy-start = (f32[64,4096]{1,0:T(8,128)S(1)}, f32[64,4096]{1,0:T(8,128)}, u32[]{:S(2)}) copy-start(f32[64,4096]{1,0:T(8,128)} %get-tuple-element.42.ok_ref) | copy-start | bytes 3145732
  81.7 39.4 %copy-start.2 = (f32[32,4096]{1,0:T(8,128)S(1)}, f32[32,4096]{1,0:T(8,128)}, u32[]{:S(2)}) copy-start(f32[32,4096]{1,0:T(8,128)} %get-tuple-element.26.fp_ref) | copy-start | bytes 1572868
  121.1 1.2 copy-start.1

commit v11 on v10

--- a/solution.py
+++ b/solution.py
@@ -174,7 +174,7 @@
         toks, rows = pl.ds(2 * r, 2), pl.ds(2 * r * SLOTS, 2 * SLOTS)
 
         def dots(tok, table):
-            full = lax.dot_general(tok[toks].reshape(PAIR, width), table[rows, :], dims, preferred_element_type=F32)
+            full = lax.dot_general(table[rows, :], tok[toks].reshape(PAIR, width), dims, preferred_element_type=F32).T
             return jnp.concatenate([full[:TOK, :SLOTS], full[TOK:, SLOTS:]], axis=0)
 
         act, slope = gelu_pair(dots(x_all, up_rows))
@@ -197,7 +197,7 @@
             return acc_w, acc_c
 
         zero = jnp.zeros((SLOTS, PAIR), F32)
-        acc_w, acc_c = lax.fori_loop(0, SEL, step, (zero, zero), unroll=4)
+        acc_w, acc_c = lax.fori_loop(0, SEL, step, (zero, zero), unroll=8)
         for ref, acc in ((w_buf, acc_w), (c_buf, acc_c)):
             terms = split3(acc)
             for j in range(2):
@@ -435,7 +435,7 @@
             in_specs=[early] * 2 + [rows] * 5,
             out_specs=[rows, rows],
             out_shape=[shape((TOK, width), BF16)] * 2,
-            compiler_params=pltpu.CompilerParams(vmem_limit_bytes=16 * 1024 * 1024),
+            compiler_params=pltpu.CompilerParams(vmem_limit_bytes=VMEM_BYTES),
         )(first_part, *got, own_keep, own_cross)
         return out_tokens, grad_tokens, grad_up, grad_down
 

time: 126 us -> 124 us (0.984)
    pallas_call x1, Pallas kernels: 77.5 us -> 76.2 us  [per_device(): pl.pallas_call(layer_kernel, in_specs=[anyw] * 7, out_specs=[anyw] * 12,...]
  transfers between devices with their start and end apart: 4 -> 4, of which waited for: 1 -> 1; matrix products, arithmetic and copies ran while one was open for 0% -> 0% of each run, Pallas kernels for 28% -> 29%
where the time goes in v11:
time: 124 us
  Pallas kernels  115 us (93%)
  waiting for transfers between devices  3.89 us (3%)
  starting transfers between devices  3.51 us (3%)
    pallas_call x1, Pallas kernels, per_device(): pl.pallas_call(layer_kernel, in_specs=[anyw] * 7, out_specs=[anyw] * 12,...  76.2 us
    pallas_call x1, Pallas kernels, grad_rows(): pl.pallas_call(row_kernel, grid_spec=pltpu.PrefetchScalarGridSpec(num_sca...  35.5 us
    ppermute x4, waiting for transfers between devices, per_device(): hop = lambda value, pairs: lax.ppermute(value, 'ep', pairs)  3.89 us
    pallas_call x1, Pallas kernels, per_device(): pl.pallas_call(join_kernel, grid=(TOK // block,), in_specs=[early] * 2 +...  3.74 us
    ppermute x4, starting transfers between devices, per_device(): hop = lambda value, pairs: lax.ppermute(value, 'ep', pairs)  3.51 us
  transfers between devices with their start and end apart: 4, of which 1 were waited for; matrix products, arithmetic and copies ran while one was open for 0% of the time, Pallas kernels for 29%

profile of v11, /device:TPU:0, one launch (start us, length us, event | category | flops | bytes accessed | tf_op | source)
XLA Modules:
  0.0 123.5 jit_solution(4150267651523365044)
XLA Ops:
  0.6 76.2 %shard_map.102 = (bf16[8,64,4096]{2,1,0:T(8,128)(2,1)}, bf16[8,64,4096]{2,1,0:T(8,128)(2,1)}, bf16[8,128,192]{2,1,0:T(8,128)(2,1)}, bf16[8,128,192]{2,1,0:T(8,12...) custom-call(bf16[64,4096]{1,0:T(8,128)(2,1)} %x_ref.1, ...), custom_call_target="tpu_custom_call" | custom-call | tf_op jit(solution)/shard_map/pallas_call | solution.py:381
  76.9 1.5 %collective-permute-start = (f32[32,4096]{1,0:T(8,128)}, f32[32,4096]{1,0:T(8,128)S(1)}, u32[]{:S(2)}, u32[]{:S(2)}) collective-permute-start(f32[32,4096]{1,0:T(8,128)} %get-tuple-element.27), channel_id=1, source_target_pairs={{0,2},{1,5},{2,0},{3,7},{4,6},{5,1},{6,4},{7,3}} | collective-permute-start | bytes 1572872 | tf_op jit(solution)/shard_map/ppermute | solution.py:405
  78.4 0.0 collective-permute-start.1
  78.4 1.5 %collective-permute-start.2 = (f32[64,4096]{1,0:T(8,128)}, f32[64,4096]{1,0:T(8,128)}, u32[]{:S(2)}, u32[]{:S(2)}) collective-permute-start(f32[64,4096]{1,0:T(8,128)} %get-tuple-element.29), channel_id=1, source_target_pairs={{0,4},{1,3},{2,6},{3,1},{4,0},{5,7},{6,2},{7,5}} | collective-permute-start | bytes 3145736 | tf_op jit(solution)/shard_map/ppermute | solution.py:405
  79.8 0.6 collective-permute-start.3
  80.4 35.5 %shard_map.103 = (bf16[2048,4096]{1,0:T(8,128)(2,1)}, bf16[2048,4096]{1,0:T(8,128)(2,1)}) custom-call(s32[8,128]{1,0:T(8,128)} %get-tuple-element.31.asked_ref, bf16[8,128,192]{2,1,0:T(8,128)(2,1)} %get-tuple-element.32.c_ref, bf16[8,128,192]{2,1,0:T(8,128)(2,1)} %get-tuple-element.33.w_ref, bf16[512,4096]{1,0:T(8,128)(2,1)} %bitcast.6, ...), custom_call_target="tpu_custom_call" | custom-call | flops 51539607552 | bytes 33554432 | tf_op jit(solution)/shard_map/pallas_call | solution.py:412
  115.9 0.0 collective-permute-done.fk_ref
  115.9 0.0 copy-start.1
  115.9 0.0 collective-permute-done.1.fc_ref
  115.9 0.0 copy-start
  115.9 0.0 collective-permute-done.2.sk_ref
  115.9 3.9 %collective-permute-done.3.sc_ref = f32[64,4096]{1,0:T(8,128)} collective-permute-done((f32[64,4096]{1,0:T(8,128)}, f32[64,4096]{1,0:T(8,128)}, u32[]{:S(2)}, u32[]{:S(2)}) %collective-permute-start.3) | collective-permute-done | bytes 1048608 | tf_op jit(solution)/shard_map/ppermute | solution.py:405
  119.8 0.0 copy-done.1
  119.8 0.0 copy-done
  119.8 3.7 %shard_map.104 = (bf16[64,4096]{1,0:T(8,128)(2,1)}, bf16[64,4096]{1,0:T(8,128)(2,1)}) custom-call(f32[32,4096]{1,0:T(8,128)} %get-tuple-element.26.fp_ref, f32[32,4096]{1,0:T(8,128)} %copy-done.1, f32[64,4096]{1,0:T(8,128)} %copy-done, f32[64,4096]{1,0:T(8,128)} %collective-permute-done.2.sk_ref, f32[64,4096]{1,0:T(8,128)} %collective-permute-done.3.sc_ref, ...), custom_call_target="tpu_custom_call" | custom-call | tf_op jit(solution)/shard_map/pallas_call | solution.py:432
Async XLA Ops:
  76.9 39.0 %collective-permute-start = (f32[32,4096]{1,0:T(8,128)}, f32[32,4096]{1,0:T(8,128)S(1)}, u32[]{:S(2)}, u32[]{:S(2)}) collective-permute-start(f32[32,4096]{1,0:T(8,128)} %get-tuple-element.27), channel_id=1, source_target_pairs={{0,2},{1,5},{2,0},{3,7},{4,6},{5,1},{6,4},{7,3}} | collective-permute-start | bytes 1572872 | tf_op jit(solution)/shard_map/ppermute | solution.py:405
  78.4 37.5 %collective-permute-start.1 = (f32[64,4096]{1,0:T(8,128)}, f32[64,4096]{1,0:T(8,128)S(1)}, u32[]{:S(2)}, u32[]{:S(2)}) collective-permute-start(f32[64,4096]{1,0:T(8,128)} %get-tuple-element.28), channel_id=1, source_target_pairs={{0,3},{1,4},{2,1},{3,6},{4,7},{5,0},{6,5},{7,2}} | collective-permute-start | bytes 3145736 | tf_op jit(solution)/shard_map/ppermute | solution.py:405
  78.4 37.5 %collective-permute-start.2 = (f32[64,4096]{1,0:T(8,128)}, f32[64,4096]{1,0:T(8,128)}, u32[]{:S(2)}, u32[]{:S(2)}) collective-permute-start(f32[64,4096]{1,0:T(8,128)} %get-tuple-element.29), channel_id=1, source_target_pairs={{0,4},{1,3},{2,6},{3,1},{4,0},{5,7},{6,2},{7,5}} | collective-permute-start | bytes 3145736 | tf_op jit(solution)/shard_map/ppermute | solution.py:405
  79.8 40.0 %collective-permute-start.3 = (f32[64,4096]{1,0:T(8,128)}, f32[64,4096]{1,0:T(8,128)}, u32[]{:S(2)}, u32[]{:S(2)}) collective-permute-start(f32[64,4096]{1,0:T(8,128)} %get-tuple-element.30), channel_id=1, source_target_pairs={{0,5},{1,2},{2,7},{3,0},{4,1},{5,6},{6,3},{7,4}} | collective-permute-start | bytes 3145736 | tf_op jit(solution)/shard_map/ppermute | solution.py:405
  115.9 3.9 %copy-start.1 = (f32[32,4096]{1,0:T(8,128)}, f32[32,4096]{1,0:T(8,128)S(1)}, u32[]{:S(2)}) copy-start(f32[32,4096]{1,0:T(8,128)S(1)} %collective-permute-done.fk_ref) | copy-start | bytes 1572868
  115.9 3.9 %copy-start = (f32[64,4096]{1,0:T(8,128)}, f32[64,4096]{1,0:T(8,128)S(1)}, u32[]{:S(2)}) copy-start(f32[64,4096]{1,0:T(8,128)S(1)} %collective-permute-done.1.fc_ref) | copy-start | bytes 3145732

commit v12 on v11

--- a/solution.py
+++ b/solution.py
@@ -14,7 +14,6 @@
 CHUNK = 2048
 ROW_CHUNK = 1024
 GROUP = 16
-LOW = 16
 LANES = 128
 PAD = 4
 VMEM_BYTES = 62 * 1024 * 1024
@@ -36,7 +35,7 @@
 
 
 N_COPIES = 64
-SIDE_STEP, FAR_STEP, REST_STEP = 1, 4, 6
+SIDE_STEP, FAR_STEP, REST_STEP = 1, 3, 5
 COLS = 512
 PART = 32
 TERM_SEM = 5 + 16
@@ -90,8 +89,7 @@
     asks = [push(req_ref, (0, pl.ds(me ^ b, 1)), asked, pl.ds(b, 1), b) for b in range(1, N_DEV)]
     first = [push(x_ref, None, x_all, 4, 4), push(dy_ref, None, dy_all, 2, 2)]
     near_own = [push(x_ref, None, x_all, 1, 1), push(dy_ref, None, dy_all, 1, 1)]
-    low, top = pl.ds(0, LOW), pl.ds(LOW, TOK - LOW)
-    second = [push(x_ref, low, x_all, (2, low), 2), push(dy_ref, low, dy_all, (4, low), 4)]
+    second = []
     asked[pl.ds(0, 1), :] = req_ref[0, pl.ds(me, 1), :]
     arrive(asks)
     to_smem = pltpu.make_async_copy(asked, asked_s, smem_sem)
@@ -119,7 +117,7 @@
                 far.extend([push(gate_all, 4, gate_all, 6, 2), push(slot_all, 2, slot_all, 6, 4)])
                 near_first.extend([push(gate_all, 4, gate_all, 5, 1), push(slot_all, 2, slot_all, 3, 1)])
                 second.extend([push(gate_all, 0, gate_all, 2, 2), push(slot_all, 0, slot_all, 4, 4)])
-                second.extend([push(x_ref, top, x_all, (2, top), 2), push(dy_ref, top, dy_all, (4, top), 4)])
+                second.extend([push(x_ref, None, x_all, 2, 2), push(dy_ref, None, dy_all, 4, 4)])
             k = sub // 2
             if sub % 2 == 0:
                 fetch(k).wait()

time: 124 us -> 121 us (0.976)
  Pallas kernels: 115 us -> 113 us
    pallas_call x1, Pallas kernels: 76.2 us -> 73.9 us  [per_device(): pl.pallas_call(layer_kernel, in_specs=[anyw] * 7, out_specs=[anyw] * 12,...]
where the time goes in v12:
time: 121 us
  Pallas kernels  113 us (93%)
  waiting for transfers between devices  3.92 us (3%)
  starting transfers between devices  3.51 us (3%)
    pallas_call x1, Pallas kernels, per_device(): pl.pallas_call(layer_kernel, in_specs=[anyw] * 7, out_specs=[anyw] * 12,...  73.9 us
    pallas_call x1, Pallas kernels, grad_rows(): pl.pallas_call(row_kernel, grid_spec=pltpu.PrefetchScalarGridSpec(num_sca...  35.4 us
    ppermute x4, waiting for transfers between devices, per_device(): hop = lambda value, pairs: lax.ppermute(value, 'ep', pairs)  3.92 us
    pallas_call x1, Pallas kernels, per_device(): pl.pallas_call(join_kernel, grid=(TOK // block,), in_specs=[early] * 2 +...  3.74 us
    ppermute x4, starting transfers between devices, per_device(): hop = lambda value, pairs: lax.ppermute(value, 'ep', pairs)  3.51 us
  transfers between devices with their start and end apart: 4, of which 1 were waited for; matrix products, arithmetic and copies ran while one was open for 0% of the time, Pallas kernels for 29%

profile of v12, /device:TPU:0, one launch (start us, length us, event | category | flops | bytes accessed | tf_op | source)
XLA Modules:
  0.0 121.2 jit_solution(1519243448778459524)
XLA Ops:
  0.6 73.9 %shard_map.102 = (bf16[8,64,4096]{2,1,0:T(8,128)(2,1)}, bf16[8,64,4096]{2,1,0:T(8,128)(2,1)}, bf16[8,128,192]{2,1,0:T(8,128)(2,1)}, bf16[8,128,192]{2,1,0:T(8,12...) custom-call(bf16[64,4096]{1,0:T(8,128)(2,1)} %x_ref.1, ...), custom_call_target="tpu_custom_call" | custom-call | tf_op jit(solution)/shard_map/pallas_call | solution.py:379
  74.5 1.2 collective-permute-start
  75.7 0.3 collective-permute-start.1
  76.0 1.2 collective-permute-start.2
  77.2 0.9 collective-permute-start.3
  78.0 35.4 %shard_map.103 = (bf16[2048,4096]{1,0:T(8,128)(2,1)}, bf16[2048,4096]{1,0:T(8,128)(2,1)}) custom-call(s32[8,128]{1,0:T(8,128)} %get-tuple-element.31.asked_ref, bf16[8,128,192]{2,1,0:T(8,128)(2,1)} %get-tuple-element.32.c_ref, bf16[8,128,192]{2,1,0:T(8,128)(2,1)} %get-tuple-element.33.w_ref, bf16[512,4096]{1,0:T(8,128)(2,1)} %bitcast.6, ...), custom_call_target="tpu_custom_call" | custom-call | flops 51539607552 | bytes 33554432 | tf_op jit(solution)/shard_map/pallas_call | solution.py:410
  113.5 0.0 collective-permute-done.fk_ref
  113.5 0.0 copy-start.1
  113.5 0.0 collective-permute-done.1.fc_ref
  113.5 0.0 copy-start
  113.5 0.0 collective-permute-done.2.sk_ref
  113.5 3.9 %collective-permute-done.3.sc_ref = f32[64,4096]{1,0:T(8,128)} collective-permute-done((f32[64,4096]{1,0:T(8,128)}, f32[64,4096]{1,0:T(8,128)}, u32[]{:S(2)}, u32[]{:S(2)}) %collective-permute-start.3) | collective-permute-done | bytes 1048608 | tf_op jit(solution)/shard_map/ppermute | solution.py:403
  117.4 0.0 copy-done.1
  117.4 0.0 copy-done
  117.4 3.7 %shard_map.104 = (bf16[64,4096]{1,0:T(8,128)(2,1)}, bf16[64,4096]{1,0:T(8,128)(2,1)}) custom-call(f32[32,4096]{1,0:T(8,128)} %get-tuple-element.26.fp_ref, f32[32,4096]{1,0:T(8,128)} %copy-done.1, f32[64,4096]{1,0:T(8,128)} %copy-done, f32[64,4096]{1,0:T(8,128)} %collective-permute-done.2.sk_ref, f32[64,4096]{1,0:T(8,128)} %collective-permute-done.3.sc_ref, ...), custom_call_target="tpu_custom_call" | custom-call | tf_op jit(solution)/shard_map/pallas_call | solution.py:430
Async XLA Ops:
  74.5 39.0 %collective-permute-start = (f32[32,4096]{1,0:T(8,128)}, f32[32,4096]{1,0:T(8,128)S(1)}, u32[]{:S(2)}, u32[]{:S(2)}) collective-permute-start(f32[32,4096]{1,0:T(8,128)} %get-tuple-element.27), channel_id=1, source_target_pairs={{0,2},{1,5},{2,0},{3,7},{4,6},{5,1},{6,4},{7,3}} | collective-permute-start | bytes 1572872 | tf_op jit(solution)/shard_map/ppermute | solution.py:403
  75.7 37.8 %collective-permute-start.1 = (f32[64,4096]{1,0:T(8,128)}, f32[64,4096]{1,0:T(8,128)S(1)}, u32[]{:S(2)}, u32[]{:S(2)}) collective-permute-start(f32[64,4096]{1,0:T(8,128)} %get-tuple-element.28), channel_id=1, source_target_pairs={{0,3},{1,4},{2,1},{3,6},{4,7},{5,0},{6,5},{7,2}} | collective-permute-start | bytes 3145736 | tf_op jit(solution)/shard_map/ppermute | solution.py:403
  76.0 37.5 %collective-permute-start.2 = (f32[64,4096]{1,0:T(8,128)}, f32[64,4096]{1,0:T(8,128)}, u32[]{:S(2)}, u32[]{:S(2)}) collective-permute-start(f32[64,4096]{1,0:T(8,128)} %get-tuple-element.29), channel_id=1, source_target_pairs={{0,4},{1,3},{2,6},{3,1},{4,0},{5,7},{6,2},{7,5}} | collective-permute-start | bytes 3145736 | tf_op jit(solution)/shard_map/ppermute | solution.py:403
  77.2 40.3 %collective-permute-start.3 = (f32[64,4096]{1,0:T(8,128)}, f32[64,4096]{1,0:T(8,128)}, u32[]{:S(2)}, u32[]{:S(2)}) collective-permute-start(f32[64,4096]{1,0:T(8,128)} %get-tuple-element.30), channel_id=1, source_target_pairs={{0,5},{1,2},{2,7},{3,0},{4,1},{5,6},{6,3},{7,4}} | collective-permute-start | bytes 3145736 | tf_op jit(solution)/shard_map/ppermute | solution.py:403
  113.5 4.0 %copy-start.1 = (f32[32,4096]{1,0:T(8,128)}, f32[32,4096]{1,0:T(8,128)S(1)}, u32[]{:S(2)}) copy-start(f32[32,4096]{1,0:T(8,128)S(1)} %collective-permute-done.fk_ref) | copy-start | bytes 1572868
  113.5 3.9 %copy-start = (f32[64,4096]{1,0:T(8,128)}, f32[64,4096]{1,0:T(8,128)S(1)}, u32[]{:S(2)}) copy-start(f32[64,4096]{1,0:T(8,128)S(1)} %collective-permute-done.1.fc_ref) | copy-start | bytes 3145732

commit v13 on v12

--- a/solution.py
+++ b/solution.py
@@ -82,7 +82,7 @@
         copy.start()
     for copy in small:
         copy.wait()
-    slot_all[0] = slot_ref[...].reshape(SEL, TOK).T
+    slot_all[0] = slot_ref[...].reshape(SEL, TOK).T.astype(jnp.int16)
     gate_all[0] = gate_ref[...].reshape(SEL, TOK).T
     pl.semaphore_wait(barrier, N_DEV - 1)
 
@@ -177,7 +177,7 @@
 
         act, slope = gelu_pair(dots(x_all, up_rows))
         slope = slope * dots(dy_all, down_rows)
-        local = slot_all[toks].reshape(PAIR, SEL) - me * SLOTS
+        local = slot_all[toks].reshape(PAIR, SEL).astype(I32) - me * SLOTS
         valid = (local >= 0) & (local < SLOTS)
         index = jnp.where(valid, local, 0)
         act = jnp.take_along_axis(act, index, axis=1)
@@ -282,17 +282,17 @@
         block(0, mine.at[0], other.at[0])
         pair_own = push(other, 0, pair_recv, 3, 1)
         keep_terms(0)
-        arrive([pair_own])
-        add_into(mine.at[0], pair_recv.at[3])
-        mine_cross = push(mine, (0, cross), own_cross, None, 1)
-        saves.append(save(mine.at[0, near], own_keep, 4))
-        saves[-1].start()
         for k, cols in enumerate(chunks):
             arrive([hop[k]])
             add_into(mine.at[2 - core], hop_recv, cols, 64)
             for n, (rows, dst) in enumerate(((near, second_keep), (cross, second_cross))):
                 saves.append(save(mine.at[2 - core, rows, cols], dst.at[:, cols], 5 + 2 * k + n))
                 saves[-1].start()
+        arrive([pair_own])
+        add_into(mine.at[0], pair_recv.at[3])
+        mine_cross = push(mine, (0, cross), own_cross, None, 1)
+        saves.append(save(mine.at[0, near], own_keep, 4))
+        saves[-1].start()
         arrive([part, mine_cross])
         leave([spec for spec in sent if spec not in pair_far and spec is not pair_x])
         for copy in saves:
@@ -383,7 +383,7 @@
             out_shape=[shape((N_DEV, TOK, width), BF16)] * 2 + [shape((N_DEV, SLOTS, TERMS * TOK), BF16)] * 2 + [shape((N_DEV, SLOTS), I32)] + [shape((PART, width), F32), shape((TOK - PART, width), F32)] + [sums] * 5,
             scratch_shapes=[
                 pltpu.VMEM((N_DEV, TOK, width), BF16), pltpu.VMEM((N_DEV, TOK, width), BF16),
-                pltpu.VMEM((N_DEV, TOK, SEL), I32), pltpu.VMEM((N_DEV, TOK, SEL), F32),
+                pltpu.VMEM((N_DEV, TOK, SEL), jnp.int16), pltpu.VMEM((N_DEV, TOK, SEL), F32),
                 pltpu.VMEM((N_DEV * SLOTS, width), BF16), pltpu.VMEM((N_DEV * SLOTS, width), BF16),
                 pltpu.VMEM((4, PAIR, width), F32), pltpu.VMEM((PAIR, width), F32),
                 pltpu.VMEM((heads, top_k, TOK), I32), pltpu.VMEM((heads, top_k, TOK), F32), pltpu.VMEM((1, N_DEV, SLOTS), I32),

time: 121 us -> 121 us (level)
  no operation moved by 1% of the time
where the time goes in v13:
time: 121 us
  Pallas kernels  113 us (93%)
  waiting for transfers between devices  3.91 us (3%)
  starting transfers between devices  3.51 us (3%)
    pallas_call x1, Pallas kernels, per_device(): pl.pallas_call(layer_kernel, in_specs=[anyw] * 7, out_specs=[anyw] * 12,...  73.8 us
    pallas_call x1, Pallas kernels, grad_rows(): pl.pallas_call(row_kernel, grid_spec=pltpu.PrefetchScalarGridSpec(num_sca...  35.5 us
    ppermute x4, waiting for transfers between devices, per_device(): hop = lambda value, pairs: lax.ppermute(value, 'ep', pairs)  3.91 us
    pallas_call x1, Pallas kernels, per_device(): pl.pallas_call(join_kernel, grid=(TOK // block,), in_specs=[early] * 2 +...  3.74 us
    ppermute x4, starting transfers between devices, per_device(): hop = lambda value, pairs: lax.ppermute(value, 'ep', pairs)  3.51 us
  transfers between devices with their start and end apart: 4, of which 1 were waited for; matrix products, arithmetic and copies ran while one was open for 0% of the time, Pallas kernels for 29%

profile of v13, /device:TPU:0, one launch (start us, length us, event | category | flops | bytes accessed | tf_op | source)
XLA Modules:
  0.0 121.1 jit_solution(16895902841478967081)
XLA Ops:
  0.6 73.8 %shard_map.102 = (bf16[8,64,4096]{2,1,0:T(8,128)(2,1)}, bf16[8,64,4096]{2,1,0:T(8,128)(2,1)}, bf16[8,128,192]{2,1,0:T(8,128)(2,1)}, bf16[8,128,192]{2,1,0:T(8,12...) custom-call(bf16[64,4096]{1,0:T(8,128)(2,1)} %x_ref.1, ...), custom_call_target="tpu_custom_call" | custom-call | tf_op jit(solution)/shard_map/pallas_call | solution.py:379
  74.5 0.7 collective-permute-start
  75.2 0.8 collective-permute-start.1
  76.0 0.7 collective-permute-start.2
  76.7 1.3 %collective-permute-start.3 = (f32[64,4096]{1,0:T(8,128)}, f32[64,4096]{1,0:T(8,128)}, u32[]{:S(2)}, u32[]{:S(2)}) collective-permute-start(f32[64,4096]{1,0:T(8,128)} %get-tuple-element.30), channel_id=1, source_target_pairs={{0,5},{1,2},{2,7},{3,0},{4,1},{5,6},{6,3},{7,4}} | collective-permute-start | bytes 3145736 | tf_op jit(solution)/shard_map/ppermute | solution.py:403
  78.0 35.5 %shard_map.103 = (bf16[2048,4096]{1,0:T(8,128)(2,1)}, bf16[2048,4096]{1,0:T(8,128)(2,1)}) custom-call(s32[8,128]{1,0:T(8,128)} %get-tuple-element.31.asked_ref, bf16[8,128,192]{2,1,0:T(8,128)(2,1)} %get-tuple-element.32.c_ref, bf16[8,128,192]{2,1,0:T(8,128)(2,1)} %get-tuple-element.33.w_ref, bf16[512,4096]{1,0:T(8,128)(2,1)} %bitcast.6, ...), custom_call_target="tpu_custom_call" | custom-call | flops 51539607552 | bytes 33554432 | tf_op jit(solution)/shard_map/pallas_call | solution.py:410
  113.4 0.0 collective-permute-done.fk_ref
  113.4 0.0 copy-start.1
  113.4 0.0 collective-permute-done.1.fc_ref
  113.4 0.0 copy-start
  113.5 0.0 collective-permute-done.2.sk_ref
  113.5 3.9 %collective-permute-done.3.sc_ref = f32[64,4096]{1,0:T(8,128)} collective-permute-done((f32[64,4096]{1,0:T(8,128)}, f32[64,4096]{1,0:T(8,128)}, u32[]{:S(2)}, u32[]{:S(2)}) %collective-permute-start.3) | collective-permute-done | bytes 1048608 | tf_op jit(solution)/shard_map/ppermute | solution.py:403
  117.4 0.0 copy-done.1
  117.4 0.0 copy-done
  117.4 3.7 %shard_map.104 = (bf16[64,4096]{1,0:T(8,128)(2,1)}, bf16[64,4096]{1,0:T(8,128)(2,1)}) custom-call(f32[32,4096]{1,0:T(8,128)} %get-tuple-element.26.fp_ref, f32[32,4096]{1,0:T(8,128)} %copy-done.1, f32[64,4096]{1,0:T(8,128)} %copy-done, f32[64,4096]{1,0:T(8,128)} %collective-permute-done.2.sk_ref, f32[64,4096]{1,0:T(8,128)} %collective-permute-done.3.sc_ref, ...), custom_call_target="tpu_custom_call" | custom-call | tf_op jit(solution)/shard_map/pallas_call | solution.py:430
Async XLA Ops:
  74.5 39.0 %collective-permute-start = (f32[32,4096]{1,0:T(8,128)}, f32[32,4096]{1,0:T(8,128)S(1)}, u32[]{:S(2)}, u32[]{:S(2)}) collective-permute-start(f32[32,4096]{1,0:T(8,128)} %get-tuple-element.27), channel_id=1, source_target_pairs={{0,2},{1,5},{2,0},{3,7},{4,6},{5,1},{6,4},{7,3}} | collective-permute-start | bytes 1572872 | tf_op jit(solution)/shard_map/ppermute | solution.py:403
  75.2 38.3 %collective-permute-start.1 = (f32[64,4096]{1,0:T(8,128)}, f32[64,4096]{1,0:T(8,128)S(1)}, u32[]{:S(2)}, u32[]{:S(2)}) collective-permute-start(f32[64,4096]{1,0:T(8,128)} %get-tuple-element.28), channel_id=1, source_target_pairs={{0,3},{1,4},{2,1},{3,6},{4,7},{5,0},{6,5},{7,2}} | collective-permute-start | bytes 3145736 | tf_op jit(solution)/shard_map/ppermute | solution.py:403
  76.0 37.5 %collective-permute-start.2 = (f32[64,4096]{1,0:T(8,128)}, f32[64,4096]{1,0:T(8,128)}, u32[]{:S(2)}, u32[]{:S(2)}) collective-permute-start(f32[64,4096]{1,0:T(8,128)} %get-tuple-element.29), channel_id=1, source_target_pairs={{0,4},{1,3},{2,6},{3,1},{4,0},{5,7},{6,2},{7,5}} | collective-permute-start | bytes 3145736 | tf_op jit(solution)/shard_map/ppermute | solution.py:403
  76.7 40.7 %collective-permute-start.3 = (f32[64,4096]{1,0:T(8,128)}, f32[64,4096]{1,0:T(8,128)}, u32[]{:S(2)}, u32[]{:S(2)}) collective-permute-start(f32[64,4096]{1,0:T(8,128)} %get-tuple-element.30), channel_id=1, source_target_pairs={{0,5},{1,2},{2,7},{3,0},{4,1},{5,6},{6,3},{7,4}} | collective-permute-start | bytes 3145736 | tf_op jit(solution)/shard_map/ppermute | solution.py:403
  113.4 3.9 %copy-start.1 = (f32[32,4096]{1,0:T(8,128)}, f32[32,4096]{1,0:T(8,128)S(1)}, u32[]{:S(2)}) copy-start(f32[32,4096]{1,0:T(8,128)S(1)} %collective-permute-done.fk_ref) | copy-start | bytes 1572868
  113.4 3.9 %copy-start = (f32[64,4096]{1,0:T(8,128)}, f32[64,4096]{1,0:T(8,128)S(1)}, u32[]{:S(2)}) copy-start(f32[64,4096]{1,0:T(8,128)S(1)} %collective-permute-done.1.fc_ref) | copy-start | bytes 3145732
